TPU v7x, 32 devices: a whole 2x2x4 slice. The times are simulated.
32 devices in a mesh: dp: 16 (over z, y, core), rep: 2 (over x).
Axes of the slice: x: 2, y: 2, z: 4, core: 2. Of those that a mesh axis runs over, the one named last changes fastest.
Arguments:
- gate_pre: bfloat16 [2, 2048, 5632], P(None, 'dp', 'rep'), may hold values from -8 to 8
- up_pre: bfloat16 [2, 2048, 5632], P(None, 'dp', 'rep'), may hold values from -6 to 6
- out_grad: bfloat16 [2, 2048, 1024], P(None, 'dp'), may hold values from -6 to 6
- master: float32 [1024, 5632], P('dp', 'rep'), may hold values from -0.078125 to 0.078125
- moment_one: float32 [1024, 5632], P('dp', 'rep'), may hold values from -0.02 to 0.02
- moment_two: float32 [1024, 5632], P('dp', 'rep'), may hold values from 1e-06 to 1e-05
Outputs:
- layer_out: bfloat16 [2, 2048, 1024], P(None, 'dp', 'rep')
- gate_grad: bfloat16 [2, 2048, 5632], P(None, 'dp', 'rep')
- up_grad: bfloat16 [2, 2048, 5632], P(None, 'dp', 'rep')
- master_new: float32 [1024, 5632], P('dp', 'rep')
- moment_one_new: float32 [1024, 5632], P('dp', 'rep')
- moment_two_new: float32 [1024, 5632], P('dp', 'rep')
All inputs are finite; a program needn't handle non-finite values.
Results may differ from a plain program's by a relative error of at most 0.0048.
The roundings to bfloat16 on the way count: a program that leaves them out, or rounds other values in their place, can miss the bound.
Values may be sent and summed in bfloat16 or wider, within the bound.
No kernel may reach another device: no remote copies, remote signals or barrier semaphores. Data moves between devices by JAX's collectives and lax.ppermute only.
A program may use at most 128 MiB of HBM per device.

v0:
```python
import jax
import jax.numpy as jnp
from jax import lax
from jax.sharding import PartitionSpec as P

first_power = 2.6561398887587544e-05
second_power = 0.005920529220333997


def grad_rows(cotangent, hidden):
    return lax.dot_general(
        cotangent, hidden, (((0,), (0,)), ((), ())), preferred_element_type=jnp.float32
    )


def on_device(gate_pre, up_pre, out_grad, master, moment_one, moment_two):
    shard_bf = master.astype(jnp.bfloat16)
    weights = lax.all_gather(shard_bf, "dp", axis=0, tiled=True)
    micro = gate_pre.shape[0]
    total = micro * gate_pre.shape[1] * lax.axis_size("dp")
    own_rows = master.shape[0]
    outs_list = []
    gate_list = []
    up_list = []
    hidden_list = []
    grad_sum = None
    for index in range(micro):
        gate = gate_pre[index].astype(jnp.float32)
        up_val = up_pre[index].astype(jnp.float32)
        sig = jax.nn.sigmoid(gate)
        hidden = (gate * sig * up_val).astype(jnp.bfloat16)
        hidden_list.append(hidden)
        partial_out = lax.dot_general(
            hidden, weights, (((1,), (1,)), ((), ())), preferred_element_type=jnp.float32
        )
        outs_list.append(
            lax.psum_scatter(partial_out, "rep", scatter_dimension=1, tiled=True).astype(
                jnp.bfloat16
            )
        )
        hid_grad = jnp.dot(out_grad[index], weights, preferred_element_type=jnp.float32)
        gate_list.append(
            (hid_grad * up_val * sig * (1.0 + gate * (1.0 - sig))).astype(jnp.bfloat16)
        )
        up_list.append((hid_grad * gate * sig).astype(jnp.bfloat16))

        def single_term(start, count, cotangent=out_grad[index], current=hidden):
            return grad_rows(cotangent, current)

        shard_grad = lax.psum_scatter(
            single_term(jnp.int32(0), lax.axis_size("dp") * own_rows),
            "dp",
            scatter_dimension=0,
            tiled=True,
        )
        grad_sum = shard_grad if grad_sum is None else grad_sum + shard_grad
    main_grad = grad_sum / jnp.float32(total)
    first = 0.9 * moment_one + 0.1 * main_grad
    second = 0.95 * moment_two + 0.05 * main_grad * main_grad
    update = first / (1.0 - first_power) / (jnp.sqrt(second / (1.0 - second_power)) + 1e-08)
    master_new = master - 0.003 * (update + 0.1 * master)
    return (
        jnp.stack(outs_list),
        jnp.stack(gate_list),
        jnp.stack(up_list),
        master_new,
        first,
        second,
    )


def solution(mesh):
    placed = (
        P(None, "dp", "rep"),
        P(None, "dp", "rep"),
        P(None, "dp", None),
        P("dp", "rep"),
        P("dp", "rep"),
        P("dp", "rep"),
    )
    return jax.shard_map(
        on_device,
        mesh=mesh,
        in_specs=placed,
        out_specs=(
            P(None, "dp", "rep"),
            P(None, "dp", "rep"),
            P(None, "dp", "rep"),
            P("dp", "rep"),
            P("dp", "rep"),
            P("dp", "rep"),
        ),
        check_vma=False,
    )
```

profile of v0, /device:TPU:0, one launch (start us, length us, event | category | flops | bytes accessed | tf_op | source)
XLA Modules:
  0.0 264.3 jit_solution(14178496637402104767)
XLA Ops:
  7.2 0.0 copy-start
  7.2 0.0 copy-start.1
  7.2 0.0 copy-start.3
  7.2 0.0 reduce-scatter.10.cloned.1.call-start
  7.2 3.2 %fusion.45 = f32[2816,1024]{1,0:T(8,128)S(1)} fusion(bf16[2,128,2816]{2,1,0:T(8,128)(2,1)} %param.7, bf16[2,128,2816]{2,1,0:T(8,128)(2,1)} %param.6, bf16[2,128,1024]{2,1,0:T(8,128)(2,1)} %param.8), kind=kOutput, calls=%fused_computation.56 | convolution fusion | flops 741081088 | bytes 13238272 | tf_op jit(solution)/shard_map/dot_general | solution.py:11
  10.5 0.0 copy-done
  10.5 0.0 copy-done.1
  10.5 0.0 copy-done.3
  10.5 6.0 %add_bitcast_fusion = f32[1024,2816]{0,1:T(8,128)} fusion(f32[2816,1024]{1,0:T(8,128)S(1)} %fusion.45, bf16[2,128,2816]{2,1,0:T(8,128)(2,1)S(1)} %copy-done, bf16[2,128,2816]{2,1,0:T(8,128)(2,1)S(1)} %copy-done.1, bf16[2,128,1024]{2,1,0:T(8,128)(2,1)S(1)} %copy-done.3), kind=kOutput, calls=%fused_computation | convolution fusion | flops 743964672 | bytes 24772608 | tf_op jit(solution)/shard_map/dot_general | solution.py:11
  16.5 12.0 %copy.29 = f32[1024,2816]{1,0:T(8,128)} copy(f32[1024,2816]{0,1:T(8,128)} %add_bitcast_fusion) | data formatting | bytes 23068672
  28.4 0.0 reduce-scatter.10.cloned.1.call-update
  28.5 0.0 all-gather.2.cloned.1.call-start
  28.5 129.9 %reduce-scatter.10.cloned.1.call-done = f32[64,2816]{1,0:T(8,128)} async-done(((f32[1024,2816]{1,0:T(8,128)}), f32[64,2816]{1,0:T(8,128)}) %reduce-scatter.10.cloned.1.call-update) | async-done | bytes 720912 | tf_op jit(solution)/shard_map/reduce_scatter | solution.py:50
  158.4 3.8 %multiply_subtract_fusion = (f32[64,2816]{1,0:T(8,128)}, f32[64,2816]{1,0:T(8,128)}, f32[64,2816]{1,0:T(8,128)}, bf16[64,2816]{1,0:T(8,128)(2,1)}) fusion(f32[64,2816]{1,0:T(8,128)} %param.9, f32[64,2816]{1,0:T(8,128)} %reduce-scatter.10.cloned.1.call-done, f32[64,2816]{1,0:T(8,128)} %param.10, f32[64,2816]{1,0:T(8,128)} %param.11), kind=kLoop, calls=%fused_computation.58 | loop fusion | flops 3063808 | bytes 5406720 | tf_op jit(solution)/shard_map/sub | solution.py:61
  162.2 0.0 all-gather.2.cloned.1.call-update
  162.2 0.0 reduce-scatter.8.cloned.1.call-start
  162.3 58.1 %all-gather.2.cloned.1.call-done = bf16[1024,2816]{1,0:T(8,128)(2,1)} async-done(((bf16[64,2816]{1,0:T(8,128)(2,1)}), bf16[1024,2816]{1,0:T(8,128)(2,1)}) %all-gather.2.cloned.1.call-update) | async-done | bytes 5767184 | tf_op jit(solution)/shard_map/all_gather | solution.py:18
  220.4 5.4 %fusion.40 = f32[128,1024]{1,0:T(8,128)} fusion(bf16[1024,2816]{1,0:T(8,128)(2,1)} %all-gather.2.cloned.1.call-done, bf16[2,128,2816]{2,1,0:T(8,128)(2,1)S(1)} %copy-done, bf16[2,128,2816]{2,1,0:T(8,128)(2,1)S(1)} %copy-done.1), kind=kOutput, calls=%fused_computation.53 | convolution fusion | flops 741081088 | bytes 7733248 | tf_op jit(solution)/shard_map/dot_general | solution.py:33
  225.8 0.0 reduce-scatter.8.cloned.1.call-update
  225.8 0.0 reduce-scatter.6.cloned.1.call-start
  225.9 5.4 %fusion.42 = f32[128,1024]{1,0:T(8,128)} fusion(bf16[1024,2816]{1,0:T(8,128)(2,1)} %all-gather.2.cloned.1.call-done, bf16[2,128,2816]{2,1,0:T(8,128)(2,1)S(1)} %copy-done, bf16[2,128,2816]{2,1,0:T(8,128)(2,1)S(1)} %copy-done.1), kind=kOutput, calls=%fused_computation.54 | convolution fusion | flops 741081088 | bytes 7733248 | tf_op jit(solution)/shard_map/dot_general | solution.py:33
  231.3 0.0 slice-start
  231.3 0.0 reduce-scatter.6.cloned.1.call-update
  231.3 0.0 slice-start.1
  231.3 0.0 copy-start.2
  231.4 3.7 %fusion.64 = f32[128,2816]{1,0:T(8,128)S(1)} fusion(bf16[1024,2816]{1,0:T(8,128)(2,1)} %all-gather.2.cloned.1.call-done, bf16[2,128,1024]{2,1,0:T(8,128)(2,1)S(1)} %copy-done.3), kind=kOutput, calls=%fused_computation.77 | convolution fusion | flops 738197504 | bytes 7471104 | tf_op jit(solution)/shard_map/dot_general | solution.py:41
  235.1 0.0 slice-done
  235.1 0.6 slice-done.1
  235.7 0.4 copy-done.2
  236.1 2.1 fusion.52
  238.2 1.8 pad_maximum_fusion
  240.0 0.0 reduce-scatter.8.cloned.1.call-done
  240.0 1.0 convert_bitcast_fusion.4
  241.0 15.1 %reduce-scatter.6.cloned.1.call-done = f32[128,512]{1,0:T(8,128)} async-done(((f32[128,1024]{1,0:T(8,128)}), f32[128,512]{1,0:T(8,128)}) %reduce-scatter.6.cloned.1.call-update) | async-done | bytes 262160 | tf_op jit(solution)/shard_map/reduce_scatter | solution.py:37
  256.0 1.0 convert_bitcast_fusion.5
  257.0 0.7 pad_maximum_fusion.2
  (1 shorter events, 0.0 us)
Async XLA Ops:
  7.2 3.3 %copy-start = (bf16[2,128,2816]{2,1,0:T(8,128)(2,1)S(1)}, bf16[2,128,2816]{2,1,0:T(8,128)(2,1)}, u32[]{:S(2)}) copy-start(bf16[2,128,2816]{2,1,0:T(8,128)(2,1)} %param.7) | copy-start | bytes 4325380
  7.2 3.3 %copy-start.1 = (bf16[2,128,2816]{2,1,0:T(8,128)(2,1)S(1)}, bf16[2,128,2816]{2,1,0:T(8,128)(2,1)}, u32[]{:S(2)}) copy-start(bf16[2,128,2816]{2,1,0:T(8,128)(2,1)} %param.6) | copy-start | bytes 4325380
  7.2 3.3 %copy-start.3 = (bf16[2,128,1024]{2,1,0:T(8,128)(2,1)S(1)}, bf16[2,128,1024]{2,1,0:T(8,128)(2,1)}, u32[]{:S(2)}) copy-start(bf16[2,128,1024]{2,1,0:T(8,128)(2,1)} %param.8) | copy-start | bytes 1572868
  7.2 151.2 %reduce-scatter.10.cloned.1.call-start = ((), (), s32[]{:S(2)}) async-start(), calls=%async_computation.6 | async-start | bytes 12255232 | tf_op jit(solution)/shard_map/reduce_scatter | solution.py:50
  28.5 191.9 %all-gather.2.cloned.1.call-start = ((), (), s32[]{:S(2)}) async-start(), calls=%async_computation.3 | async-start | bytes 6127616 | tf_op jit(solution)/shard_map/all_gather | solution.py:18
  162.2 77.8 %reduce-scatter.8.cloned.1.call-start = ((), (), s32[]{:S(2)}) async-start(), calls=%async_computation.5 | async-start | bytes 786432 | tf_op jit(solution)/shard_map/reduce_scatter | solution.py:37
  225.8 30.2 %reduce-scatter.6.cloned.1.call-start = ((), (), s32[]{:S(2)}) async-start(), calls=%async_computation.4 | async-start | bytes 786432 | tf_op jit(solution)/shard_map/reduce_scatter | solution.py:37
  231.3 3.8 %slice-start = ((s8[5767168]{0:T(1024)(128)(4,1)}), s8[1572864]{0:T(1024)(128)(4,1)S(1)}, s32[]{:S(2)}) async-start(s8[5767168]{0:T(1024)(128)(4,1)} %bitcast.145), calls=%async_computation.7 | async-start | bytes 3145728
  231.3 4.3 %slice-start.1 = ((s8[5767168]{0:T(1024)(128)(4,1)}), s8[4194304]{0:T(1024)(128)(4,1)S(1)}, s32[]{:S(2)}) async-start(s8[5767168]{0:T(1024)(128)(4,1)} %bitcast.145), calls=%async_computation.8 | async-start | bytes 8388608
  231.3 4.7 %copy-start.2 = (bf16[2,128,2816]{2,1,0:T(8,128)(2,1)S(1)}, bf16[2,128,2816]{2,1,0:T(8,128)(2,1)}, u32[]{:S(2)}) copy-start(bf16[2,128,2816]{2,1,0:T(8,128)(2,1)} %param.6) | copy-start | bytes 4325380
Sparse Core Ops, SparseCore 0:
  28.6 129.7 reduce-scatter.9
  162.3 57.9 all-gather.1
  225.9 13.2 reduce-scatter.7
  241.3 14.6 reduce-scatter.5
where the time goes:
time: 265 us; the launch traced here: 264 us
  waiting for transfers between devices  203 us (77%)
  matrix products  25.9 us (10%)
  between operations  13.9 us (5%)
  local copies, waits for them, and re-layouts  13 us (5%)
  other arithmetic  8.28 us (3%)
    reduce_scatter x1, waiting for transfers between devices, on_device(): lax.psum_scatter(single_term(jnp.int32(0), lax.axis_size('dp') * own_rows...  130 us
    all_gather x1, waiting for transfers between devices, on_device(): weights = lax.all_gather(shard_bf, 'dp', axis=0, tiled=True)  58.1 us
    reduce_scatter x2, waiting for transfers between devices, on_device(): lax.psum_scatter(partial_out, 'rep', scatter_dimension=1, tiled=True)  15.1 us
    unnamed x13, local copies, waits for them, and re-layouts  13 us
    dot_general x2, matrix products, on_device(): lax.dot_general(hidden, weights, (((1,), (1,)), ((), ())), preferred_elem...  10.9 us
    dot_general x2, matrix products, grad_rows(): lax.dot_general(cotangent, hidden, (((0,), (0,)), ((), ())), preferred_el...  9.21 us
    dot_general x2, matrix products, on_device(): jnp.dot(out_grad[index], weights, preferred_element_type=jnp.float32)  5.76 us
  transfers between devices with their start and end apart: 4, of which 3 were waited for; matrix products, arithmetic and copies ran while one was open for 5% of the time, Pallas kernels for 0%

commit v1 on v0

v1 whole, which is shorter than its diff:
```python
import functools
import jax
import jax.numpy as jnp
from jax import lax
from jax.experimental import pallas as pl
from jax.experimental.pallas import tpu as pltpu
from jax.sharding import PartitionSpec as P


first_power = 2.6561398887587544e-05
second_power = 0.005920529220333997


VMEM = pl.BlockSpec(memory_space=pltpu.VMEM)
SMEM = pl.BlockSpec(memory_space=pltpu.SMEM)
TILE = 256


def adamw(main_grad, master, moment_one, moment_two):
    first = 0.9 * moment_one + 0.1 * main_grad
    second = 0.95 * moment_two + 0.05 * main_grad * main_grad
    update = first / (1.0 - first_power) / (jnp.sqrt(second / (1.0 - second_power)) + 1e-08)
    return master - 0.003 * (update + 0.1 * master), first, second


def gated(gate, up_val):
    gate = gate.astype(jnp.float32)
    return (gate * jax.nn.sigmoid(gate) * up_val.astype(jnp.float32)).astype(jnp.bfloat16)


def plain(gate_pre, up_pre, out_grad, master, moment_one, moment_two):
    micro, rows, width = gate_pre.shape
    total = micro * rows * lax.axis_size("dp")
    weights = lax.all_gather(master.astype(jnp.bfloat16), "dp", axis=0, tiled=True)
    hidden = gated(gate_pre, up_pre).reshape(-1, width)
    cotangent = out_grad.reshape(-1, out_grad.shape[2])
    grads = lax.dot_general(
        cotangent, hidden, (((0,), (0,)), ((), ())), preferred_element_type=jnp.float32
    )
    part = lax.dot_general(
        hidden, weights, (((1,), (1,)), ((), ())), preferred_element_type=jnp.float32
    )
    hid_grad = jnp.dot(cotangent, weights, preferred_element_type=jnp.float32)
    grads = lax.psum_scatter(grads, "dp", scatter_dimension=0, tiled=True)
    out = lax.psum_scatter(part, "rep", scatter_dimension=1, tiled=True).astype(jnp.bfloat16)
    gate = gate_pre.reshape(-1, width).astype(jnp.float32)
    up_val = up_pre.reshape(-1, width).astype(jnp.float32)
    sig = jax.nn.sigmoid(gate)
    gate_grad = (hid_grad * up_val * sig * (1.0 + gate * (1.0 - sig))).astype(jnp.bfloat16)
    up_grad = (hid_grad * gate * sig).astype(jnp.bfloat16)
    master_new, first, second = adamw(
        grads / jnp.float32(total), master, moment_one, moment_two
    )
    return (
        out.reshape(micro, rows, -1),
        gate_grad.reshape(gate_pre.shape),
        up_grad.reshape(gate_pre.shape),
        master_new,
        first,
        second,
    )


def select_kernel(zs, rows, me_ref, og_ref, *refs):
    outs, turned = refs[:4], refs[4]
    turned[...] = og_ref[...].T
    me = me_ref[0]
    for m in range(4):
        for s in range(zs):
            start = pl.multiple_of(((me ^ (4 * s)) ^ m) * rows, rows)
            outs[m][s * rows : (s + 1) * rows, :] = turned[pl.ds(start, rows), :]


def turn_kernel(*refs):
    count = len(refs) // 2
    for source, target in zip(refs[:count], refs[count:]):
        target[...] = source[...].T


def each_tile(width, body):
    for start in range(0, width, TILE):
        body(slice(start, start + TILE))


def grads_kernel(zs, rows, *refs):
    lefts, rights, outs = refs[:4], refs[4:8], refs[8 : 8 + zs]

    def body(at):
        total = None
        for left, right in zip(lefts, rights):
            term = jnp.dot(left[...], right[:, at], preferred_element_type=jnp.float32)
            total = term if total is None else total + term
        for s in range(zs):
            outs[s][:, at] = total[s * rows : (s + 1) * rows, :].astype(outs[s].dtype)

    each_tile(rights[0].shape[1], body)


def stacked(chunks, at):
    return jnp.concatenate([chunk[:, at] for chunk in chunks], axis=0)


def out_rows(zs, me_ref, rep_ref, turned, chunks, keep, send, total):
    base, value = 0, None
    for piece in turned:
        at = slice(base, base + piece.shape[0])
        term = jnp.dot(stacked(chunks, at), piece[...], preferred_element_type=jnp.float32)
        value = term if value is None else value + term
        base = at.stop
    total[...] = value
    half = keep.shape[0]
    flip = ((me_ref[0] // (2 * zs)) ^ rep_ref[0]) & 1
    keep[...] = total[pl.ds(pl.multiple_of(flip * half, half), half), :]
    send[...] = total[pl.ds(pl.multiple_of((1 - flip) * half, half), half), :]


def near_kernel(zs, me_ref, rep_ref, *refs):
    turned, (one, two), chunks = refs[:2], refs[2:4], refs[4 : 4 + 2 * zs]
    keep, send, early, left, total = refs[4 + 2 * zs :]
    out_rows(zs, me_ref, rep_ref, turned, chunks, keep, send, total)
    width = one.shape[0]
    left[:, :width] = one[...].T
    left[:, width:] = two[...].T
    order = chunks[0::2] + chunks[1::2]

    def body(at):
        early[:, at] = jnp.dot(
            left[...], stacked(order, at), preferred_element_type=jnp.float32
        )

    each_tile(early.shape[1], body)


def far_kernel(zs, me_ref, rep_ref, *refs):
    turned, chunks = refs[:2], refs[2 : 2 + 2 * zs]
    keep, send, total = refs[2 + 2 * zs :]
    out_rows(zs, me_ref, rep_ref, turned, chunks, keep, send, total)


def back_kernel(zs, *refs):
    (one, two, gate_ref, up_ref, early), chunks = refs[:5], refs[5 : 5 + 2 * zs]
    gate_out, up_out, left = refs[5 + 2 * zs :]
    width = one.shape[0]
    left[:, :width] = one[...].T
    left[:, width:] = two[...].T
    order = chunks[0::2] + chunks[1::2]

    def body(at):
        hid_grad = early[:, at] + jnp.dot(
            left[...], stacked(order, at), preferred_element_type=jnp.float32
        )
        gate = gate_ref[:, at].astype(jnp.float32)
        up_val = up_ref[:, at].astype(jnp.float32)
        sig = jax.nn.sigmoid(gate)
        gate_out[:, at] = (
            hid_grad * up_val * sig * (1.0 + gate * (1.0 - sig))
        ).astype(jnp.bfloat16)
        up_out[:, at] = (hid_grad * gate * sig).astype(jnp.bfloat16)

    each_tile(gate_out.shape[1], body)


def merge_kernel(zs, rows, me_ref, *refs):
    parts, out, placed = refs[:4], refs[4], refs[5]
    me = me_ref[0]
    for far in range(2):
        value = parts[2 * far][...] + parts[2 * far + 1][...]
        for s in range(zs // 2):
            for core in range(2):
                block = me ^ (4 * s + 2 * far + core)
                start = pl.multiple_of((block % (2 * zs)) * rows, rows)
                first = (2 * s + core) * rows
                placed[pl.ds(start, rows), :] = value[first : first + rows, :]
    out[...] = placed[...].T.astype(out.dtype)


def adamw_kernel(zs, total, *refs):
    pieces, states, outs = refs[: 2 * zs], refs[2 * zs : 2 * zs + 3], refs[2 * zs + 3 :]
    base = 0
    for p in range(2):
        own, others = pieces[p * zs], pieces[p * zs + 1 : (p + 1) * zs]
        at = slice(base, base + own.shape[1])
        base = at.stop
        grad = own[...]
        for other in others:
            grad = grad + other[...].astype(jnp.float32)
        for out, value in zip(
            outs, adamw(grad / jnp.float32(total), *[state[:, at] for state in states])
        ):
            out[:, at] = value


def estimate(flops, moved):
    return pl.CostEstimate(flops=int(flops), bytes_accessed=int(moved), transcendentals=0)


def call(kernel, outs, ins, scratch=(), smem=0, flops=0):
    moved = sum(v.size * v.dtype.itemsize for v in list(ins) + list(outs))
    return pl.pallas_call(
        kernel,
        out_shape=list(outs),
        in_specs=[SMEM] * smem + [VMEM] * (len(ins) - smem),
        out_specs=[VMEM] * len(outs),
        scratch_shapes=list(scratch),
        compiler_params=pltpu.CompilerParams(vmem_limit_bytes=24 << 20),
        cost_estimate=estimate(flops, moved),
    )(*ins)


def direct(gate_pre, up_pre, out_grad, master, moment_one, moment_two):
    n = lax.axis_size("dp")
    zs = n // 4
    micro, span, width = gate_pre.shape
    tokens = micro * span
    depth = out_grad.shape[2]
    rows = master.shape[0]
    total = micro * span * n
    me_arr = jnp.full((1,), lax.axis_index("dp"), jnp.int32)
    rep_arr = jnp.full((1,), lax.axis_index("rep"), jnp.int32)
    tiles = width // TILE
    cuts = [0, (tiles + 1) // 2 * TILE, width]
    spread = range(1, zs)

    def swap(value, m):
        return lax.ppermute(value, "dp", [(i, i ^ m) for i in range(n)])

    def bf16(*shape):
        return jax.ShapeDtypeStruct(shape, jnp.bfloat16)

    def f32(*shape):
        return jax.ShapeDtypeStruct(shape, jnp.float32)

    gate = gate_pre.reshape(tokens, width)
    up_val = up_pre.reshape(tokens, width)
    cotangent = out_grad.reshape(tokens, depth)

    chunk = {0: lax.optimization_barrier(master.astype(jnp.bfloat16))}
    for s in spread:
        chunk[4 * s] = swap(chunk[0], 4 * s)
    for s in range(zs):
        chunk[4 * s + 2] = swap(chunk[4 * s], 2)
    for s in range(zs):
        chunk[4 * s + 1] = swap(chunk[4 * s], 1)
        chunk[4 * s + 3] = swap(chunk[4 * s + 2], 1)

    picked = call(
        functools.partial(select_kernel, zs, rows),
        [bf16(zs * rows, tokens)] * 4,
        [me_arr, cotangent],
        [pltpu.VMEM((depth, tokens), jnp.bfloat16)],
        smem=1,
    )
    lefts = [picked[0]] + [swap(picked[m], m) for m in range(1, 4)]
    hidden, sums = [], []
    for lo, hi in zip(cuts[:-1], cuts[1:]):
        own = gated(gate[:, lo:hi], up_val[:, lo:hi])
        hidden.append(own)
        across = swap(own, 2)
        rights = [own, swap(own, 1), across, swap(across, 1)]
        size = hi - lo
        parts = call(
            functools.partial(grads_kernel, zs, rows),
            [f32(rows, size)] + [bf16(rows, size)] * (zs - 1),
            lefts + rights,
            flops=8 * zs * rows * tokens * size,
        )
        sums.extend([parts[0]] + [swap(parts[s], 4 * s) for s in spread])
    turned = call(turn_kernel, [bf16(h.shape[1], tokens) for h in hidden], hidden)

    near = [chunk[4 * s + m] for s in range(zs) for m in (0, 1)]
    far = [chunk[4 * s + m] for s in range(zs) for m in (2, 3)]
    deep, half = depth // 2, depth // 4
    work = 2 * tokens * deep * width
    left = [pltpu.VMEM((tokens, deep), jnp.bfloat16)]
    product = [pltpu.VMEM((deep, tokens), jnp.float32)]
    keep_near, send_near, early = call(
        functools.partial(near_kernel, zs),
        [f32(half, tokens), f32(half, tokens), f32(tokens, width)],
        [me_arr, rep_arr, *turned, picked[0], picked[1], *near],
        left + product,
        smem=2,
        flops=2 * work,
    )

    def across_rep(value):
        return lax.ppermute(value, "rep", [(0, 1), (1, 0)])

    got_near = across_rep(send_near)
    keep_far, send_far = call(
        functools.partial(far_kernel, zs),
        [f32(half, tokens), f32(half, tokens)],
        [me_arr, rep_arr, *turned, *far],
        product,
        smem=2,
        flops=work,
    )
    got_far = across_rep(send_far)
    gate_grad, up_grad = call(
        functools.partial(back_kernel, zs),
        [bf16(tokens, width)] * 2,
        [picked[2], picked[3], gate, up_val, early, *far],
        left,
        flops=work,
    )
    (out,) = call(
        functools.partial(merge_kernel, zs, rows),
        [bf16(tokens, 2 * half)],
        [me_arr, keep_near, got_near, keep_far, got_far],
        [pltpu.VMEM((2 * half, tokens), jnp.float32)],
        smem=1,
    )
    master_new, first, second = call(
        functools.partial(adamw_kernel, zs, total),
        [f32(rows, width)] * 3,
        sums + [master, moment_one, moment_two],
    )
    return (
        out.reshape(micro, span, 2 * half),
        gate_grad.reshape(gate_pre.shape),
        up_grad.reshape(gate_pre.shape),
        master_new,
        first,
        second,
    )


def small(n, reps, width):
    return n == 16 and reps == 2 and width % TILE == 0


def on_device(gate_pre, *rest):
    if small(lax.axis_size("dp"), lax.axis_size("rep"), gate_pre.shape[2]):
        return direct(gate_pre, *rest)
    return plain(gate_pre, *rest)


def solution(mesh):
    placed = (
        P(None, "dp", "rep"),
        P(None, "dp", "rep"),
        P(None, "dp", None),
        P("dp", "rep"),
        P("dp", "rep"),
        P("dp", "rep"),
    )
    return jax.shard_map(
        on_device,
        mesh=mesh,
        in_specs=placed,
        out_specs=(
            P(None, "dp", "rep"),
            P(None, "dp", "rep"),
            P(None, "dp", "rep"),
            P("dp", "rep"),
            P("dp", "rep"),
            P("dp", "rep"),
        ),
        check_vma=False,
    )
```

time: 265 us -> 143 us (0.54)
  waiting for transfers between devices: 203 us -> 69.7 us
  starting transfers between devices: 0.16 us -> 29 us
  matrix products: 25.9 us -> 0 us
  Pallas kernels: 0 us -> 17.7 us
  between operations: 13.9 us -> 0.98 us
  local copies, waits for them, and re-layouts: 13 us -> 20.1 us
  other arithmetic: 8.28 us -> 5.1 us
    reduce_scatter x3 -> x0, waiting for transfers between devices: 145 us -> none  [the longest x1 130 us: on_device(): lax.psum_scatter(single_term(jnp.int32(0), lax.axis_size('dp') * own_rows...]
    ppermute x0 -> x32, waiting for transfers between devices: none -> 69.7 us  [the longest x30 69.7 us: swap(): return lax.ppermute(value, 'dp', [(i, i ^ m) for i in range(n)])]
    all_gather x1 -> x0, waiting for transfers between devices: 58.1 us -> none  [on_device(): weights = lax.all_gather(shard_bf, 'dp', axis=0, tiled=True)]
    ppermute x0 -> x32, starting transfers between devices: none -> 29 us  [the longest x30 26.8 us: swap(): return lax.ppermute(value, 'dp', [(i, i ^ m) for i in range(n)])]
    dot_general x6 -> x0, matrix products: 25.9 us -> none  [the longest x2 10.9 us: on_device(): lax.dot_general(hidden, weights, (((1,), (1,)), ((), ())), preferred_elem...]
    pallas_call x0 -> x9, Pallas kernels: none -> 17.7 us  [call(): pl.pallas_call(kernel, out_shape=list(outs), in_specs=[SMEM] * smem + [VM...]
    unnamed x13 -> x84, local copies, waits for them, and re-layouts: 13 us -> 20.1 us
    convert_element_type x0 -> x3, other arithmetic: none -> 5.1 us  [the longest x2 3.11 us: gated(): (gate * jax.nn.sigmoid(gate) * up_val.astype(jnp.float32)).astype(jnp.bfl...]
  transfers between devices with their start and end apart: 4 -> 32, of which waited for: 3 -> 6; matrix products, arithmetic and copies ran while one was open for 5% -> 2% of each run, Pallas kernels for 0% -> 11%
where the time goes in v1:
time: 143 us
  waiting for transfers between devices  69.7 us (49%)
  starting transfers between devices  29 us (20%)
  local copies, waits for them, and re-layouts  20.1 us (14%)
  Pallas kernels  17.7 us (12%)
  other arithmetic  5.1 us (4%)
    ppermute x30, waiting for transfers between devices, swap(): return lax.ppermute(value, 'dp', [(i, i ^ m) for i in range(n)])  69.7 us
    ppermute x30, starting transfers between devices, swap(): return lax.ppermute(value, 'dp', [(i, i ^ m) for i in range(n)])  26.8 us
    unnamed x84, local copies, waits for them, and re-layouts  20.1 us
    pallas_call x9, Pallas kernels, call(): pl.pallas_call(kernel, out_shape=list(outs), in_specs=[SMEM] * smem + [VM...  17.7 us
    convert_element_type x2, other arithmetic, gated(): (gate * jax.nn.sigmoid(gate) * up_val.astype(jnp.float32)).astype(jnp.bfl...  3.11 us
  transfers between devices with their start and end apart: 32, of which 6 were waited for; matrix products, arithmetic and copies ran while one was open for 2% of the time, Pallas kernels for 11%

profile of v1, /device:TPU:0, one launch (start us, length us, event | category | flops | bytes accessed | tf_op | source)
XLA Modules:
  0.0 142.6 jit_solution(2774871922188559242)
XLA Ops:
  0.6 2.0 %convert_element_type.27.refs_4_ = bf16[64,2816]{1,0:T(8,128)(2,1)} convert(f32[64,2816]{1,0:T(8,128)} %refs_8_.1) | non-fusion elementwise | flops 180224 | bytes 1081344 | tf_op jit(solution)/shard_map/convert_element_type | solution.py:237
  2.6 0.5 collective-permute-start
  3.1 2.6 %collective-permute-start.1 = (bf16[64,2816]{1,0:T(8,128)(2,1)}, bf16[64,2816]{1,0:T(8,128)(2,1)}, u32[]{:S(2)}, u32[]{:S(2)}) collective-permute-start(bf16[64,2816]{1,0:T(8,128)(2,1)} %convert_element_type.27.refs_4_), channel_id=1, source_target_pairs={{0,8},{2,10},{4,12},{6,14},{8,0},{10,2},{12,4},{14,6},{16,24},{18,... | collective-permute-start | bytes 1081352 | tf_op jit(solution)/shard_map/ppermute | solution.py:225
  5.7 1.0 copy-done.23
  7.0 0.3 collective-permute-start.17
  7.3 1.5 %collective-permute-start.18 = (bf16[256,256]{1,0:T(8,128)(2,1)S(1)}, bf16[256,256]{1,0:T(8,128)(2,1)S(1)}, u32[]{:S(2)}, u32[]{:S(2)}) collective-permute-start(bf16[256,256]{1,0:T(8,128)(2,1)S(1)} %get-tuple-element.38.refs_0_), channel_id=1, source_target_pairs={{0,4},{2,6},{4,0},{6,2},{8,12},{10,14},{12,8},{14,10},{16,20},{18,... | collective-permute-start | bytes 393224 | tf_op jit(solution)/shard_map/ppermute | solution.py:225
  8.9 1.5 %fusion.9.refs_1_.refs_4_ = bf16[256,1280]{1,0:T(8,128)(2,1)S(1)} fusion(bf16[256,2816]{1,0:T(8,128)(2,1)S(1)} %bitcast.8, bf16[256,2816]{1,0:T(8,128)(2,1)} %bitcast.11), kind=kLoop, calls=%fused_computation.13 | loop fusion | flops 2621440 | bytes 1966080 | tf_op jit(solution)/shard_map/convert_element_type | solution.py:28
  10.4 1.6 %collective-permute-start.27 = (bf16[256,1280]{1,0:T(8,128)(2,1)S(1)}, bf16[256,1280]{1,0:T(8,128)(2,1)}, u32[]{:S(2)}, u32[]{:S(2)}) collective-permute-start(bf16[256,1280]{1,0:T(8,128)(2,1)S(1)} %fusion.9.refs_1_.refs_4_), channel_id=1, source_target_pairs={{0,4},{2,6},{4,0},{6,2},{8,12},{10,14},{12,8},{14,10},{16,20},{18,... | collective-permute-start | bytes 1966088 | tf_op jit(solution)/shard_map/ppermute | solution.py:225
  12.0 1.6 %collective-permute-done.18.refs_2_ = bf16[256,256]{1,0:T(8,128)(2,1)S(1)} collective-permute-done((bf16[256,256]{1,0:T(8,128)(2,1)S(1)}, bf16[256,256]{1,0:T(8,128)(2,1)S(1)}, u32[]{:S(2)}, u32[]{:S(2)}) %collective-permute-start.18) | collective-permute-done | bytes 131104 | tf_op jit(solution)/shard_map/ppermute | solution.py:225
  13.7 2.6 %collective-permute-start.3 = (bf16[64,2816]{1,0:T(8,128)(2,1)}, bf16[64,2816]{1,0:T(8,128)(2,1)S(1)}, u32[]{:S(2)}, u32[]{:S(2)}) collective-permute-start(bf16[64,2816]{1,0:T(8,128)(2,1)} %convert_element_type.27.refs_4_), channel_id=1, source_target_pairs={{0,16},{2,18},{4,20},{6,22},{8,24},{10,26},{12,28},{14,30},{16,0},... | collective-permute-start | bytes 1081352 | tf_op jit(solution)/shard_map/ppermute | solution.py:225
  16.3 1.7 %collective-permute-start.5 = (bf16[64,2816]{1,0:T(8,128)(2,1)}, bf16[64,2816]{1,0:T(8,128)(2,1)S(1)}, u32[]{:S(2)}, u32[]{:S(2)}) collective-permute-start(bf16[64,2816]{1,0:T(8,128)(2,1)} %convert_element_type.27.refs_4_), channel_id=1, source_target_pairs={{0,24},{2,26},{4,28},{6,30},{8,16},{10,18},{12,20},{14,22},{16,8},... | collective-permute-start | bytes 1081352 | tf_op jit(solution)/shard_map/ppermute | solution.py:225
  18.0 0.7 copy-done.28
  18.7 1.1 collective-permute-start.8
  19.8 0.9 collective-permute-start.2
  20.7 1.6 %fusion.4.refs_0_.refs_4_ = bf16[256,1536]{1,0:T(8,128)(2,1)S(1)} fusion(bf16[256,2816]{1,0:T(8,128)(2,1)S(1)} %bitcast.9, bf16[256,2816]{1,0:T(8,128)(2,1)} %bitcast.12), kind=kLoop, calls=%fused_computation.8 | loop fusion | flops 3145728 | bytes 2359296 | tf_op jit(solution)/shard_map/convert_element_type | solution.py:28
  22.3 18.1 %collective-permute-done.3.refs_8_ = bf16[64,2816]{1,0:T(8,128)(2,1)S(1)} collective-permute-done((bf16[64,2816]{1,0:T(8,128)(2,1)}, bf16[64,2816]{1,0:T(8,128)(2,1)S(1)}, u32[]{:S(2)}, u32[]{:S(2)}) %collective-permute-start.3) | collective-permute-done | bytes 360480 | tf_op jit(solution)/shard_map/ppermute | solution.py:225
  40.4 1.5 %collective-permute-start.21 = (bf16[256,1536]{1,0:T(8,128)(2,1)S(1)}, bf16[256,1536]{1,0:T(8,128)(2,1)}, u32[]{:S(2)}, u32[]{:S(2)}) collective-permute-start(bf16[256,1536]{1,0:T(8,128)(2,1)S(1)} %fusion.4.refs_0_.refs_4_), channel_id=1, source_target_pairs={{0,4},{2,6},{4,0},{6,2},{8,12},{10,14},{12,8},{14,10},{16,20},{18,... | collective-permute-start | bytes 2359304 | tf_op jit(solution)/shard_map/ppermute | solution.py:225
  42.0 0.5 collective-permute-start.6
  42.5 0.5 collective-permute-start.10
  43.0 0.7 copy-done.34
  43.7 1.5 %collective-permute-start.12 = (bf16[64,2816]{1,0:T(8,128)(2,1)S(1)}, bf16[64,2816]{1,0:T(8,128)(2,1)S(1)}, u32[]{:S(2)}, u32[]{:S(2)}) collective-permute-start(bf16[64,2816]{1,0:T(8,128)(2,1)S(1)} %collective-permute-done.3.refs_8_), channel_id=1, source_target_pairs={{0,4},{2,6},{4,0},{6,2},{8,12},{10,14},{12,8},{14,10},{16,20},{18,... | collective-permute-start | bytes 1081352 | tf_op jit(solution)/shard_map/ppermute | solution.py:225
  45.3 0.7 copy-done.30
  46.0 0.8 copy-done.36
  46.8 0.7 copy-done.38
  47.5 0.5 collective-permute-start.14
  48.0 0.8 copy-done.32
  48.8 19.8 %collective-permute-done.10.refs_4_.refs_7_ = bf16[64,2816]{1,0:T(8,128)(2,1)S(1)} collective-permute-done((bf16[64,2816]{1,0:T(8,128)(2,1)}, bf16[64,2816]{1,0:T(8,128)(2,1)S(1)}, u32[]{:S(2)}, u32[]{:S(2)}) %collective-permute-start.10) | collective-permute-done | bytes 360480 | tf_op jit(solution)/shard_map/ppermute | solution.py:225
  68.6 0.8 copy-done.3
  69.4 6.9 %collective-permute-done.12.refs_6_.refs_9_ = bf16[64,2816]{1,0:T(8,128)(2,1)S(1)} collective-permute-done((bf16[64,2816]{1,0:T(8,128)(2,1)S(1)}, bf16[64,2816]{1,0:T(8,128)(2,1)S(1)}, u32[]{:S(2)}, u32[]{:S(2)}) %collective-permute-start.12) | collective-permute-done | bytes 360480 | tf_op jit(solution)/shard_map/ppermute | solution.py:225
  76.3 0.8 copy-done.5
  77.1 0.7 copy-done.7
  77.8 0.5 collective-permute-start.26
  78.3 2.8 %collective-permute-done.14.refs_8_.refs_11_ = bf16[64,2816]{1,0:T(8,128)(2,1)} collective-permute-done((bf16[64,2816]{1,0:T(8,128)(2,1)S(1)}, bf16[64,2816]{1,0:T(8,128)(2,1)}, u32[]{:S(2)}, u32[]{:S(2)}) %collective-permute-start.14) | collective-permute-done | bytes 360480 | tf_op jit(solution)/shard_map/ppermute | solution.py:225
  81.2 0.5 collective-permute-start.22
  81.7 0.8 copy-done.9
  82.5 0.7 copy-done.11
  83.2 0.5 collective-permute-start.15
  83.7 0.4 shard_map.109
  84.1 0.9 copy-done.13
  85.0 0.8 copy-done.17
  85.8 1.1 copy-done.14
  87.0 1.1 copy-done.18
  88.1 1.0 copy-done.29
  89.1 1.0 copy-done.31
  90.0 1.0 copy-done.33
  91.0 1.0 copy-done.35
  92.0 1.0 copy-done.37
  93.0 1.0 copy-done.39
  94.0 0.9 copy-done.41
  94.9 3.0 %shard_map.111 = (f32[256,256]{1,0:T(8,128)S(1)}, f32[256,256]{1,0:T(8,128)S(1)}, f32[256,2816]{1,0:T(8,128)S(1)}) custom-call(s32[1]{0:T(128)} %bitcast.me_ref, s32[1]{0:T(128)} %bitcast.1.rep_ref, bf16[1536,256]{1,0:T(8,128)(2,1)S(1)} %copy-done.14, bf16[1280,256]{1,0:T(8,128)(2,1)S(1)} %copy-done.18, ...), custom_call_target="tpu_custom_call" | custom-call | flops 1476395008 | bytes 7995400 | tf_op jit(solution)/shard_map/pallas_call | solution.py:199
  97.9 1.6 %collective-permute-start.7 = (f32[256,256]{1,0:T(8,128)S(1)}, f32[256,256]{1,0:T(8,128)S(1)}, u32[]{:S(2)}, u32[]{:S(2)}) collective-permute-start(f32[256,256]{1,0:T(8,128)S(1)} %get-tuple-element.35), channel_id=1, source_target_pairs={{0,1},{1,0},{2,3},{3,2},{4,5},{5,4},{6,7},{7,6},{8,9},{9,8},{10,11... | collective-permute-start | bytes 786440 | tf_op jit(solution)/shard_map/ppermute | solution.py:286
  99.5 2.1 %shard_map.112 = (f32[256,256]{1,0:T(8,128)S(1)}, f32[256,256]{1,0:T(8,128)S(1)}) custom-call(s32[1]{0:T(128)} %bitcast.me_ref, s32[1]{0:T(128)} %bitcast.1.rep_ref, bf16[1536,256]{1,0:T(8,128)(2,1)S(1)} %copy-done.14, bf16[1280,256]{1,0:T(8,128)(2,1)S(1)} %copy-done.18, bf16[64,2816]{1,0:T(8,128)(2,1)S(1)} %collective-permute-done.8.refs_2_.refs_5_, ...), custom_call_target="tpu_custom_call" | custom-call | flops 738197504 | bytes 4849672 | tf_op jit(solution)/shard_map/pallas_call | solution.py:199
  101.6 0.6 collective-permute-start.16
  102.2 2.3 %shard_map.116 = (f32[64,1280]{1,0:T(8,128)S(1)}, bf16[64,1280]{1,0:T(8,128)(2,1)S(1)}, bf16[64,1280]{1,0:T(8,128)(2,1)S(1)}, bf16[64,1280]{1,0:T(8,128)(2,1)S(1)}) custom-call(bf16[256,256]{1,0:T(8,128)(2,1)S(1)} %get-tuple-element.32.refs_2_.refs_0_, bf16[256,256]{1,0:T(8,128)(2,1)S(1)} %collective-permute-done.17.refs_1_, ...), custom_call_target="tpu_custom_call" | custom-call | flops 671088640 | bytes 3964928 | tf_op jit(solution)/shard_map/pallas_call | solution.py:199
  104.7 2.7 %shard_map.115 = (f32[64,1536]{1,0:T(8,128)S(1)}, bf16[64,1536]{1,0:T(8,128)(2,1)S(1)}, bf16[64,1536]{1,0:T(8,128)(2,1)S(1)}, bf16[64,1536]{1,0:T(8,128)(2,1)S(1)}) custom-call(bf16[256,256]{1,0:T(8,128)(2,1)S(1)} %get-tuple-element.32.refs_2_.refs_0_, bf16[256,256]{1,0:T(8,128)(2,1)S(1)} %collective-permute-done.17.refs_1_, ...), custom_call_target="tpu_custom_call" | custom-call | flops 805306368 | bytes 4653056 | tf_op jit(solution)/shard_map/pallas_call | solution.py:199
  107.3 2.0 %collective-permute-start.23 = (bf16[64,1536]{1,0:T(8,128)(2,1)S(1)}, bf16[64,1536]{1,0:T(8,128)(2,1)S(1)}, u32[]{:S(2)}, u32[]{:S(2)}) collective-permute-start(bf16[64,1536]{1,0:T(8,128)(2,1)S(1)} %get-tuple-element.44), channel_id=1, source_target_pairs={{0,8},{2,10},{4,12},{6,14},{8,0},{10,2},{12,4},{14,6},{16,24},{18,... | collective-permute-start | bytes 589832 | tf_op jit(solution)/shard_map/ppermute | solution.py:225
  109.3 1.1 collective-permute-start.24
  110.4 1.4 collective-permute-start.25
  111.8 2.0 %collective-permute-start.30 = (bf16[64,1280]{1,0:T(8,128)(2,1)S(1)}, bf16[64,1280]{1,0:T(8,128)(2,1)S(1)}, u32[]{:S(2)}, u32[]{:S(2)}) collective-permute-start(bf16[64,1280]{1,0:T(8,128)(2,1)S(1)} %get-tuple-element.49), channel_id=1, source_target_pairs={{0,16},{2,18},{4,20},{6,22},{8,24},{10,26},{12,28},{14,30},{16,0},... | collective-permute-start | bytes 491528 | tf_op jit(solution)/shard_map/ppermute | solution.py:225
  113.8 1.4 collective-permute-start.31
  115.2 4.4 %shard_map.114 = (bf16[256,2816]{1,0:T(8,128)(2,1)}, bf16[256,2816]{1,0:T(8,128)(2,1)}) custom-call(bf16[256,256]{1,0:T(8,128)(2,1)S(1)} %copy-done.25, bf16[256,256]{1,0:T(8,128)(2,1)S(1)} %copy-done.27, bf16[256,2816]{1,0:T(8,128)(2,1)S(1)} %bitcast.13, bf16[256,2816]{1,0:T(8,128)(2,1)S(1)} %bitcast.10, f32[256,2816]{1,0:T(8,128)S(1)} %get-tuple-element.40.refs_4_, ...), custom_call_target="tpu_custom_call" | custom-call | flops 738197504 | bytes 11796480 | tf_op jit(solution)/shard_map/pallas_call | solution.py:199
  119.6 0.9 shard_map.113
  120.5 20.3 %collective-permute-done.30.refs_6_ = bf16[64,1280]{1,0:T(8,128)(2,1)S(1)} collective-permute-done((bf16[64,1280]{1,0:T(8,128)(2,1)S(1)}, bf16[64,1280]{1,0:T(8,128)(2,1)S(1)}, u32[]{:S(2)}, u32[]{:S(2)}) %collective-permute-start.30) | collective-permute-done | bytes 163872 | tf_op jit(solution)/shard_map/ppermute | solution.py:225
  140.9 1.7 %shard_map.117 = (f32[64,2816]{1,0:T(8,128)}, f32[64,2816]{1,0:T(8,128)}, f32[64,2816]{1,0:T(8,128)}) custom-call(f32[64,1536]{1,0:T(8,128)S(1)} %get-tuple-element.43.refs_0_, bf16[64,1536]{1,0:T(8,128)(2,1)S(1)} %collective-permute-done.23.refs_1_, bf16[64,1536]{1,0:T(8,128)(2,1)S(1)} %collective-permute-done.24.refs_2_, ...), custom_call_target="tpu_custom_call" | custom-call | bytes 6127616 | tf_op jit(solution)/shard_map/pallas_call | solution.py:199
  (96 shorter events, 0.6 us)
Async XLA Ops:
  0.6 8.3 %copy-start = (bf16[2,128,2816]{2,1,0:T(8,128)(2,1)S(1)}, bf16[2,128,2816]{2,1,0:T(8,128)(2,1)}, u32[]{:S(2)}) copy-start(bf16[2,128,2816]{2,1,0:T(8,128)(2,1)} %param.7) | copy-start | bytes 4325380
  2.6 15.4 %collective-permute-start = (bf16[64,2816]{1,0:T(8,128)(2,1)}, bf16[64,2816]{1,0:T(8,128)(2,1)S(1)}, u32[]{:S(2)}, u32[]{:S(2)}) collective-permute-start(bf16[64,2816]{1,0:T(8,128)(2,1)} %convert_element_type.27.refs_4_), channel_id=1, source_target_pairs={{0,2},{2,0},{4,6},{6,4},{8,10},{10,8},{12,14},{14,12},{16,18},{18,... | collective-permute-start | bytes 1081352 | tf_op jit(solution)/shard_map/ppermute | solution.py:225
  3.1 16.7 %collective-permute-start.1 = (bf16[64,2816]{1,0:T(8,128)(2,1)}, bf16[64,2816]{1,0:T(8,128)(2,1)}, u32[]{:S(2)}, u32[]{:S(2)}) collective-permute-start(bf16[64,2816]{1,0:T(8,128)(2,1)} %convert_element_type.27.refs_4_), channel_id=1, source_target_pairs={{0,8},{2,10},{4,12},{6,14},{8,0},{10,2},{12,4},{14,6},{16,24},{18,... | collective-permute-start | bytes 1081352 | tf_op jit(solution)/shard_map/ppermute | solution.py:225
  5.7 1.0 copy-start.23
  7.0 15.3 %copy-start.24 = (bf16[256,256]{1,0:T(8,128)(2,1)}, bf16[256,256]{1,0:T(8,128)(2,1)S(1)}, u32[]{:S(2)}) copy-start(bf16[256,256]{1,0:T(8,128)(2,1)S(1)} %get-tuple-element.38.refs_0_) | copy-start | bytes 393220
  7.0 15.3 %copy-start.26 = (bf16[256,256]{1,0:T(8,128)(2,1)}, bf16[256,256]{1,0:T(8,128)(2,1)S(1)}, u32[]{:S(2)}) copy-start(bf16[256,256]{1,0:T(8,128)(2,1)S(1)} %get-tuple-element.39.refs_1_) | copy-start | bytes 393220
  7.0 15.3 %copy-start.40 = (bf16[256,256]{1,0:T(8,128)(2,1)}, bf16[256,256]{1,0:T(8,128)(2,1)S(1)}, u32[]{:S(2)}) copy-start(bf16[256,256]{1,0:T(8,128)(2,1)S(1)} %get-tuple-element.33.refs_3_) | copy-start | bytes 393220
  7.0 3.4 %collective-permute-start.17 = (bf16[256,256]{1,0:T(8,128)(2,1)S(1)}, bf16[256,256]{1,0:T(8,128)(2,1)S(1)}, u32[]{:S(2)}, u32[]{:S(2)}) collective-permute-start(bf16[256,256]{1,0:T(8,128)(2,1)S(1)} %get-tuple-element.33.refs_3_), channel_id=1, source_target_pairs={{0,2},{2,0},{4,6},{6,4},{8,10},{10,8},{12,14},{14,12},{16,18},{18,... | collective-permute-start | bytes 393224 | tf_op jit(solution)/shard_map/ppermute | solution.py:225
  7.3 6.4 %collective-permute-start.18 = (bf16[256,256]{1,0:T(8,128)(2,1)S(1)}, bf16[256,256]{1,0:T(8,128)(2,1)S(1)}, u32[]{:S(2)}, u32[]{:S(2)}) collective-permute-start(bf16[256,256]{1,0:T(8,128)(2,1)S(1)} %get-tuple-element.38.refs_0_), channel_id=1, source_target_pairs={{0,4},{2,6},{4,0},{6,2},{8,12},{10,14},{12,8},{14,10},{16,20},{18,... | collective-permute-start | bytes 393224 | tf_op jit(solution)/shard_map/ppermute | solution.py:225
  8.8 7.4 %collective-permute-start.19 = (bf16[256,256]{1,0:T(8,128)(2,1)S(1)}, bf16[256,256]{1,0:T(8,128)(2,1)S(1)}, u32[]{:S(2)}, u32[]{:S(2)}) collective-permute-start(bf16[256,256]{1,0:T(8,128)(2,1)S(1)} %get-tuple-element.39.refs_1_), channel_id=1, source_target_pairs={{0,6},{2,4},{4,2},{6,0},{8,14},{10,12},{12,10},{14,8},{16,22},{18,... | collective-permute-start | bytes 393224 | tf_op jit(solution)/shard_map/ppermute | solution.py:225
  10.4 32.1 %collective-permute-start.27 = (bf16[256,1280]{1,0:T(8,128)(2,1)S(1)}, bf16[256,1280]{1,0:T(8,128)(2,1)}, u32[]{:S(2)}, u32[]{:S(2)}) collective-permute-start(bf16[256,1280]{1,0:T(8,128)(2,1)S(1)} %fusion.9.refs_1_.refs_4_), channel_id=1, source_target_pairs={{0,4},{2,6},{4,0},{6,2},{8,12},{10,14},{12,8},{14,10},{16,20},{18,... | collective-permute-start | bytes 1966088 | tf_op jit(solution)/shard_map/ppermute | solution.py:225
  13.7 68.8 %copy-start.19 = (bf16[256,256]{1,0:T(8,128)(2,1)}, bf16[256,256]{1,0:T(8,128)(2,1)S(1)}, u32[]{:S(2)}) copy-start(bf16[256,256]{1,0:T(8,128)(2,1)S(1)} %collective-permute-done.18.refs_2_) | copy-start | bytes 393220
  13.7 26.8 %collective-permute-start.3 = (bf16[64,2816]{1,0:T(8,128)(2,1)}, bf16[64,2816]{1,0:T(8,128)(2,1)S(1)}, u32[]{:S(2)}, u32[]{:S(2)}) collective-permute-start(bf16[64,2816]{1,0:T(8,128)(2,1)} %convert_element_type.27.refs_4_), channel_id=1, source_target_pairs={{0,16},{2,18},{4,20},{6,22},{8,24},{10,26},{12,28},{14,30},{16,0},... | collective-permute-start | bytes 1081352 | tf_op jit(solution)/shard_map/ppermute | solution.py:225
  16.3 66.2 %copy-start.21 = (bf16[256,256]{1,0:T(8,128)(2,1)}, bf16[256,256]{1,0:T(8,128)(2,1)S(1)}, u32[]{:S(2)}) copy-start(bf16[256,256]{1,0:T(8,128)(2,1)S(1)} %collective-permute-done.19.refs_3_) | copy-start | bytes 393220
  16.3 25.7 %collective-permute-start.5 = (bf16[64,2816]{1,0:T(8,128)(2,1)}, bf16[64,2816]{1,0:T(8,128)(2,1)S(1)}, u32[]{:S(2)}, u32[]{:S(2)}) collective-permute-start(bf16[64,2816]{1,0:T(8,128)(2,1)} %convert_element_type.27.refs_4_), channel_id=1, source_target_pairs={{0,24},{2,26},{4,28},{6,30},{8,16},{10,18},{12,20},{14,22},{16,8},... | collective-permute-start | bytes 1081352 | tf_op jit(solution)/shard_map/ppermute | solution.py:225
  18.7 23.3 %collective-permute-start.8 = (bf16[64,2816]{1,0:T(8,128)(2,1)}, bf16[64,2816]{1,0:T(8,128)(2,1)S(1)}, u32[]{:S(2)}, u32[]{:S(2)}) collective-permute-start(bf16[64,2816]{1,0:T(8,128)(2,1)} %convert_element_type.27.refs_4_), channel_id=1, source_target_pairs={{0,4},{2,6},{4,0},{6,2},{8,12},{10,14},{12,8},{14,10},{16,20},{18,... | collective-permute-start | bytes 1081352 | tf_op jit(solution)/shard_map/ppermute | solution.py:225
  19.8 23.2 %collective-permute-start.2 = (bf16[64,2816]{1,0:T(8,128)(2,1)}, bf16[64,2816]{1,0:T(8,128)(2,1)S(1)}, u32[]{:S(2)}, u32[]{:S(2)}) collective-permute-start(bf16[64,2816]{1,0:T(8,128)(2,1)} %collective-permute-done.1.refs_6_), channel_id=1, source_target_pairs={{0,2},{2,0},{4,6},{6,4},{8,10},{10,8},{12,14},{14,12},{16,18},{18,... | collective-permute-start | bytes 1081352 | tf_op jit(solution)/shard_map/ppermute | solution.py:225
  40.4 40.7 %collective-permute-start.21 = (bf16[256,1536]{1,0:T(8,128)(2,1)S(1)}, bf16[256,1536]{1,0:T(8,128)(2,1)}, u32[]{:S(2)}, u32[]{:S(2)}) collective-permute-start(bf16[256,1536]{1,0:T(8,128)(2,1)S(1)} %fusion.4.refs_0_.refs_4_), channel_id=1, source_target_pairs={{0,4},{2,6},{4,0},{6,2},{8,12},{10,14},{12,8},{14,10},{16,20},{18,... | collective-permute-start | bytes 2359304 | tf_op jit(solution)/shard_map/ppermute | solution.py:225
  42.0 4.0 %collective-permute-start.4 = (bf16[64,2816]{1,0:T(8,128)(2,1)S(1)}, bf16[64,2816]{1,0:T(8,128)(2,1)S(1)}, u32[]{:S(2)}, u32[]{:S(2)}) collective-permute-start(bf16[64,2816]{1,0:T(8,128)(2,1)S(1)} %collective-permute-done.3.refs_8_), channel_id=1, source_target_pairs={{0,2},{2,0},{4,6},{6,4},{8,10},{10,8},{12,14},{14,12},{16,18},{18,... | collective-permute-start | bytes 1081352 | tf_op jit(solution)/shard_map/ppermute | solution.py:225
  42.0 4.8 %collective-permute-start.6 = (bf16[64,2816]{1,0:T(8,128)(2,1)S(1)}, bf16[64,2816]{1,0:T(8,128)(2,1)S(1)}, u32[]{:S(2)}, u32[]{:S(2)}) collective-permute-start(bf16[64,2816]{1,0:T(8,128)(2,1)S(1)} %collective-permute-done.5.refs_10_), channel_id=1, source_target_pairs={{0,2},{2,0},{4,6},{6,4},{8,10},{10,8},{12,14},{14,12},{16,18},{18,... | collective-permute-start | bytes 1081352 | tf_op jit(solution)/shard_map/ppermute | solution.py:225
  42.5 26.1 %collective-permute-start.10 = (bf16[64,2816]{1,0:T(8,128)(2,1)}, bf16[64,2816]{1,0:T(8,128)(2,1)S(1)}, u32[]{:S(2)}, u32[]{:S(2)}) collective-permute-start(bf16[64,2816]{1,0:T(8,128)(2,1)} %collective-permute-done.1.refs_6_), channel_id=1, source_target_pairs={{0,4},{2,6},{4,0},{6,2},{8,12},{10,14},{12,8},{14,10},{16,20},{18,... | collective-permute-start | bytes 1081352 | tf_op jit(solution)/shard_map/ppermute | solution.py:225
  43.7 32.6 %collective-permute-start.12 = (bf16[64,2816]{1,0:T(8,128)(2,1)S(1)}, bf16[64,2816]{1,0:T(8,128)(2,1)S(1)}, u32[]{:S(2)}, u32[]{:S(2)}) collective-permute-start(bf16[64,2816]{1,0:T(8,128)(2,1)S(1)} %collective-permute-done.3.refs_8_), channel_id=1, source_target_pairs={{0,4},{2,6},{4,0},{6,2},{8,12},{10,14},{12,8},{14,10},{16,20},{18,... | collective-permute-start | bytes 1081352 | tf_op jit(solution)/shard_map/ppermute | solution.py:225
  46.7 30.3 %collective-permute-start.9 = (bf16[64,2816]{1,0:T(8,128)(2,1)S(1)}, bf16[64,2816]{1,0:T(8,128)(2,1)S(1)}, u32[]{:S(2)}, u32[]{:S(2)}) collective-permute-start(bf16[64,2816]{1,0:T(8,128)(2,1)S(1)} %collective-permute-done.8.refs_2_.refs_5_), channel_id=1, source_target_pairs={{0,2},{2,0},{4,6},{6,4},{8,10},{10,8},{12,14},{14,12},{16,18},{18,... | collective-permute-start | bytes 1081352 | tf_op jit(solution)/shard_map/ppermute | solution.py:225
  47.5 33.7 %collective-permute-start.14 = (bf16[64,2816]{1,0:T(8,128)(2,1)S(1)}, bf16[64,2816]{1,0:T(8,128)(2,1)}, u32[]{:S(2)}, u32[]{:S(2)}) collective-permute-start(bf16[64,2816]{1,0:T(8,128)(2,1)S(1)} %collective-permute-done.5.refs_10_), channel_id=1, source_target_pairs={{0,4},{2,6},{4,0},{6,2},{8,12},{10,14},{12,8},{14,10},{16,20},{18,... | collective-permute-start | bytes 1081352 | tf_op jit(solution)/shard_map/ppermute | solution.py:225
  68.6 13.1 %collective-permute-start.11 = (bf16[64,2816]{1,0:T(8,128)(2,1)S(1)}, bf16[64,2816]{1,0:T(8,128)(2,1)S(1)}, u32[]{:S(2)}, u32[]{:S(2)}) collective-permute-start(bf16[64,2816]{1,0:T(8,128)(2,1)S(1)} %collective-permute-done.10.refs_4_.refs_7_), channel_id=1, source_target_pairs={{0,2},{2,0},{4,6},{6,4},{8,10},{10,8},{12,14},{14,12},{16,18},{18,... | collective-permute-start | bytes 1081352 | tf_op jit(solution)/shard_map/ppermute | solution.py:225
  68.6 0.8 copy-start.3
  76.3 6.1 %collective-permute-start.13 = (bf16[64,2816]{1,0:T(8,128)(2,1)S(1)}, bf16[64,2816]{1,0:T(8,128)(2,1)S(1)}, u32[]{:S(2)}, u32[]{:S(2)}) collective-permute-start(bf16[64,2816]{1,0:T(8,128)(2,1)S(1)} %collective-permute-done.12.refs_6_.refs_9_), channel_id=1, source_target_pairs={{0,2},{2,0},{4,6},{6,4},{8,10},{10,8},{12,14},{14,12},{16,18},{18,... | collective-permute-start | bytes 1081352 | tf_op jit(solution)/shard_map/ppermute | solution.py:225
  77.8 23.7 %collective-permute-start.26 = (bf16[256,1280]{1,0:T(8,128)(2,1)S(1)}, bf16[256,1280]{1,0:T(8,128)(2,1)}, u32[]{:S(2)}, u32[]{:S(2)}) collective-permute-start(bf16[256,1280]{1,0:T(8,128)(2,1)S(1)} %fusion.9.refs_1_.refs_4_), channel_id=1, source_target_pairs={{0,2},{2,0},{4,6},{6,4},{8,10},{10,8},{12,14},{14,12},{16,18},{18,... | collective-permute-start | bytes 1966088 | tf_op jit(solution)/shard_map/ppermute | solution.py:225
  81.2 23.5 %collective-permute-start.20 = (bf16[256,1536]{1,0:T(8,128)(2,1)S(1)}, bf16[256,1536]{1,0:T(8,128)(2,1)}, u32[]{:S(2)}, u32[]{:S(2)}) collective-permute-start(bf16[256,1536]{1,0:T(8,128)(2,1)S(1)} %fusion.4.refs_0_.refs_4_), channel_id=1, source_target_pairs={{0,2},{2,0},{4,6},{6,4},{8,10},{10,8},{12,14},{14,12},{16,18},{18,... | collective-permute-start | bytes 2359304 | tf_op jit(solution)/shard_map/ppermute | solution.py:225
  81.2 23.5 %collective-permute-start.22 = (bf16[256,1536]{1,0:T(8,128)(2,1)}, bf16[256,1536]{1,0:T(8,128)(2,1)}, u32[]{:S(2)}, u32[]{:S(2)}) collective-permute-start(bf16[256,1536]{1,0:T(8,128)(2,1)} %collective-permute-done.21.refs_6_), channel_id=1, source_target_pairs={{0,2},{2,0},{4,6},{6,4},{8,10},{10,8},{12,14},{14,12},{16,18},{18,... | collective-permute-start | bytes 2359304 | tf_op jit(solution)/shard_map/ppermute | solution.py:225
  82.4 19.7 %collective-permute-start.28 = (bf16[256,1280]{1,0:T(8,128)(2,1)}, bf16[256,1280]{1,0:T(8,128)(2,1)}, u32[]{:S(2)}, u32[]{:S(2)}) collective-permute-start(bf16[256,1280]{1,0:T(8,128)(2,1)} %collective-permute-done.27.refs_6_), channel_id=1, source_target_pairs={{0,2},{2,0},{4,6},{6,4},{8,10},{10,8},{12,14},{14,12},{16,18},{18,... | collective-permute-start | bytes 1966088 | tf_op jit(solution)/shard_map/ppermute | solution.py:225
  83.2 14.7 %collective-permute-start.15 = (bf16[64,2816]{1,0:T(8,128)(2,1)}, bf16[64,2816]{1,0:T(8,128)(2,1)}, u32[]{:S(2)}, u32[]{:S(2)}) collective-permute-start(bf16[64,2816]{1,0:T(8,128)(2,1)} %collective-permute-done.14.refs_8_.refs_11_), channel_id=1, source_target_pairs={{0,2},{2,0},{4,6},{6,4},{8,10},{10,8},{12,14},{14,12},{16,18},{18,... | collective-permute-start | bytes 1081352 | tf_op jit(solution)/shard_map/ppermute | solution.py:225
  84.1 0.9 copy-start.13
  85.0 0.8 copy-start.17
  85.8 1.1 copy-start.14
  87.0 1.1 copy-start.18
  88.1 1.0 copy-start.29
  89.0 1.0 copy-start.31
  90.0 1.0 copy-start.33
  91.0 1.0 copy-start.35
  92.0 1.0 copy-start.37
  93.0 1.0 copy-start.39
  94.0 0.9 copy-start.41
  94.9 4.6 %copy-start.4 = (bf16[64,2816]{1,0:T(8,128)(2,1)S(1)}, bf16[64,2816]{1,0:T(8,128)(2,1)}, u32[]{:S(2)}) copy-start(bf16[64,2816]{1,0:T(8,128)(2,1)} %copy-done.3) | copy-start | bytes 1081348
  94.9 4.6 %copy-start.6 = (bf16[64,2816]{1,0:T(8,128)(2,1)S(1)}, bf16[64,2816]{1,0:T(8,128)(2,1)}, u32[]{:S(2)}) copy-start(bf16[64,2816]{1,0:T(8,128)(2,1)} %copy-done.5) | copy-start | bytes 1081348
  94.9 4.6 %copy-start.8 = (bf16[64,2816]{1,0:T(8,128)(2,1)S(1)}, bf16[64,2816]{1,0:T(8,128)(2,1)}, u32[]{:S(2)}) copy-start(bf16[64,2816]{1,0:T(8,128)(2,1)} %copy-done.7) | copy-start | bytes 1081348
  94.9 4.6 %copy-start.10 = (bf16[64,2816]{1,0:T(8,128)(2,1)S(1)}, bf16[64,2816]{1,0:T(8,128)(2,1)}, u32[]{:S(2)}) copy-start(bf16[64,2816]{1,0:T(8,128)(2,1)} %copy-done.9) | copy-start | bytes 1081348
  94.9 4.6 %copy-start.12 = (bf16[64,2816]{1,0:T(8,128)(2,1)S(1)}, bf16[64,2816]{1,0:T(8,128)(2,1)}, u32[]{:S(2)}) copy-start(bf16[64,2816]{1,0:T(8,128)(2,1)} %copy-done.11) | copy-start | bytes 1081348
  97.9 4.3 %copy-start.20 = (bf16[256,256]{1,0:T(8,128)(2,1)S(1)}, bf16[256,256]{1,0:T(8,128)(2,1)}, u32[]{:S(2)}) copy-start(bf16[256,256]{1,0:T(8,128)(2,1)} %copy-done.19) | copy-start | bytes 393220
  97.9 4.3 %copy-start.22 = (bf16[256,256]{1,0:T(8,128)(2,1)S(1)}, bf16[256,256]{1,0:T(8,128)(2,1)}, u32[]{:S(2)}) copy-start(bf16[256,256]{1,0:T(8,128)(2,1)} %copy-done.21) | copy-start | bytes 393220
  97.9 12.5 %collective-permute-start.7 = (f32[256,256]{1,0:T(8,128)S(1)}, f32[256,256]{1,0:T(8,128)S(1)}, u32[]{:S(2)}, u32[]{:S(2)}) collective-permute-start(f32[256,256]{1,0:T(8,128)S(1)} %get-tuple-element.35), channel_id=1, source_target_pairs={{0,1},{1,0},{2,3},{3,2},{4,5},{5,4},{6,7},{7,6},{8,9},{9,8},{10,11... | collective-permute-start | bytes 786440 | tf_op jit(solution)/shard_map/ppermute | solution.py:286
  101.6 10.2 %collective-permute-start.16 = (f32[256,256]{1,0:T(8,128)S(1)}, f32[256,256]{1,0:T(8,128)S(1)}, u32[]{:S(2)}, u32[]{:S(2)}) collective-permute-start(f32[256,256]{1,0:T(8,128)S(1)} %get-tuple-element.37), channel_id=1, source_target_pairs={{0,1},{1,0},{2,3},{3,2},{4,5},{5,4},{6,7},{7,6},{8,9},{9,8},{10,11... | collective-permute-start | bytes 786440 | tf_op jit(solution)/shard_map/ppermute | solution.py:286
  104.5 10.6 %copy-start.1 = (bf16[2,128,2816]{2,1,0:T(8,128)(2,1)S(1)}, bf16[2,128,2816]{2,1,0:T(8,128)(2,1)}, u32[]{:S(2)}) copy-start(bf16[2,128,2816]{2,1,0:T(8,128)(2,1)} %param.6) | copy-start | bytes 4325380
  104.5 10.6 %copy-start.25 = (bf16[256,256]{1,0:T(8,128)(2,1)S(1)}, bf16[256,256]{1,0:T(8,128)(2,1)}, u32[]{:S(2)}) copy-start(bf16[256,256]{1,0:T(8,128)(2,1)} %copy-done.24) | copy-start | bytes 393220
  104.5 10.6 %copy-start.27 = (bf16[256,256]{1,0:T(8,128)(2,1)S(1)}, bf16[256,256]{1,0:T(8,128)(2,1)}, u32[]{:S(2)}) copy-start(bf16[256,256]{1,0:T(8,128)(2,1)} %copy-done.26) | copy-start | bytes 393220
  104.6 9.2 %collective-permute-start.29 = (bf16[64,1280]{1,0:T(8,128)(2,1)S(1)}, bf16[64,1280]{1,0:T(8,128)(2,1)S(1)}, u32[]{:S(2)}, u32[]{:S(2)}) collective-permute-start(bf16[64,1280]{1,0:T(8,128)(2,1)S(1)} %get-tuple-element.48), channel_id=1, source_target_pairs={{0,8},{2,10},{4,12},{6,14},{8,0},{10,2},{12,4},{14,6},{16,24},{18,... | collective-permute-start | bytes 491528 | tf_op jit(solution)/shard_map/ppermute | solution.py:225
  107.3 33.5 %collective-permute-start.23 = (bf16[64,1536]{1,0:T(8,128)(2,1)S(1)}, bf16[64,1536]{1,0:T(8,128)(2,1)S(1)}, u32[]{:S(2)}, u32[]{:S(2)}) collective-permute-start(bf16[64,1536]{1,0:T(8,128)(2,1)S(1)} %get-tuple-element.44), channel_id=1, source_target_pairs={{0,8},{2,10},{4,12},{6,14},{8,0},{10,2},{12,4},{14,6},{16,24},{18,... | collective-permute-start | bytes 589832 | tf_op jit(solution)/shard_map/ppermute | solution.py:225
  109.3 31.6 %collective-permute-start.24 = (bf16[64,1536]{1,0:T(8,128)(2,1)S(1)}, bf16[64,1536]{1,0:T(8,128)(2,1)S(1)}, u32[]{:S(2)}, u32[]{:S(2)}) collective-permute-start(bf16[64,1536]{1,0:T(8,128)(2,1)S(1)} %get-tuple-element.45), channel_id=1, source_target_pairs={{0,16},{2,18},{4,20},{6,22},{8,24},{10,26},{12,28},{14,30},{16,0},... | collective-permute-start | bytes 589832 | tf_op jit(solution)/shard_map/ppermute | solution.py:225
  110.4 30.5 %collective-permute-start.25 = (bf16[64,1536]{1,0:T(8,128)(2,1)S(1)}, bf16[64,1536]{1,0:T(8,128)(2,1)S(1)}, u32[]{:S(2)}, u32[]{:S(2)}) collective-permute-start(bf16[64,1536]{1,0:T(8,128)(2,1)S(1)} %get-tuple-element.46), channel_id=1, source_target_pairs={{0,24},{2,26},{4,28},{6,30},{8,16},{10,18},{12,20},{14,22},{16,8},... | collective-permute-start | bytes 589832 | tf_op jit(solution)/shard_map/ppermute | solution.py:225
  111.8 29.1 %collective-permute-start.30 = (bf16[64,1280]{1,0:T(8,128)(2,1)S(1)}, bf16[64,1280]{1,0:T(8,128)(2,1)S(1)}, u32[]{:S(2)}, u32[]{:S(2)}) collective-permute-start(bf16[64,1280]{1,0:T(8,128)(2,1)S(1)} %get-tuple-element.49), channel_id=1, source_target_pairs={{0,16},{2,18},{4,20},{6,22},{8,24},{10,26},{12,28},{14,30},{16,0},... | collective-permute-start | bytes 491528 | tf_op jit(solution)/shard_map/ppermute | solution.py:225
  113.8 27.1 %collective-permute-start.31 = (bf16[64,1280]{1,0:T(8,128)(2,1)S(1)}, bf16[64,1280]{1,0:T(8,128)(2,1)S(1)}, u32[]{:S(2)}, u32[]{:S(2)}) collective-permute-start(bf16[64,1280]{1,0:T(8,128)(2,1)S(1)} %get-tuple-element.50), channel_id=1, source_target_pairs={{0,24},{2,26},{4,28},{6,30},{8,16},{10,18},{12,20},{14,22},{16,8},... | collective-permute-start | bytes 491528 | tf_op jit(solution)/shard_map/ppermute | solution.py:225
  115.2 25.7 %copy-start.15 = (f32[64,2816]{1,0:T(8,128)S(1)}, f32[64,2816]{1,0:T(8,128)}, u32[]{:S(2)}) copy-start(f32[64,2816]{1,0:T(8,128)} %refs_9_.1) | copy-start | bytes 2162692
  115.2 25.7 %copy-start.16 = (f32[64,2816]{1,0:T(8,128)S(1)}, f32[64,2816]{1,0:T(8,128)}, u32[]{:S(2)}) copy-start(f32[64,2816]{1,0:T(8,128)} %refs_10_.1) | copy-start | bytes 2162692
  119.6 21.3 %copy-start.2 = (f32[64,2816]{1,0:T(8,128)S(1)}, f32[64,2816]{1,0:T(8,128)}, u32[]{:S(2)}) copy-start(f32[64,2816]{1,0:T(8,128)} %refs_8_.1) | copy-start | bytes 2162692
  (10 other events, 7.5 us)

commit v2 on v1

--- a/solution.py
+++ b/solution.py
@@ -61,20 +61,33 @@
     )
 
 
-def select_kernel(zs, rows, me_ref, og_ref, *refs):
-    outs, turned = refs[:4], refs[4]
+def select_kernel(zs, rows, me_ref, rep_ref, og_ref, own, near, far, rest, turned):
     turned[...] = og_ref[...].T
-    me = me_ref[0]
-    for m in range(4):
+    me, rep = me_ref[0], rep_ref[0]
+
+    def block(s, m):
+        start = pl.multiple_of((me ^ (4 * s) ^ m) * rows, rows)
+        return turned[pl.ds(start, rows), :]
+
+    for s in range(zs):
+        own[s * rows : (s + 1) * rows, :] = block(s, 0)
+        near[s * rows : (s + 1) * rows, :] = block(s, 1)
+    for m in (2, 3):
+        for i in range(zs // 2):
+            first = ((m - 2) * (zs // 2) + i) * rows
+            far[first : first + rows, :] = block(rep * (zs // 2) + i, m)
         for s in range(zs):
-            start = pl.multiple_of(((me ^ (4 * s)) ^ m) * rows, rows)
-            outs[m][s * rows : (s + 1) * rows, :] = turned[pl.ds(start, rows), :]
-
-
-def turn_kernel(*refs):
-    count = len(refs) // 2
-    for source, target in zip(refs[:count], refs[count:]):
-        target[...] = source[...].T
+            first = ((m - 2) * zs + s) * rows
+            rest[first : first + rows, :] = block(s, m)
+
+
+def turn_kernel(first, second, own, near, rest, first_t, second_t, left_near, left_far):
+    first_t[...] = first[...].T
+    second_t[...] = second[...].T
+    width = own.shape[0]
+    left_near[:, :width] = own[...].T
+    left_near[:, width:] = near[...].T
+    left_far[...] = rest[...].T
 
 
 def each_tile(width, body):
@@ -82,14 +95,22 @@
         body(slice(start, start + TILE))
 
 
-def grads_kernel(zs, rows, *refs):
-    lefts, rights, outs = refs[:4], refs[4:8], refs[8 : 8 + zs]
+def grads_kernel(zs, rows, rep_ref, *refs):
+    own, near, far, far_x, cross, cross_x = refs[:6]
+    rights, outs, left = refs[6:10], refs[10 : 10 + zs], refs[10 + zs]
+    count = own.shape[1]
+    half = zs * rows // 2
+    mine = pl.ds(pl.multiple_of(rep_ref[0] * half, half), half)
+    other = pl.ds(pl.multiple_of((1 - rep_ref[0]) * half, half), half)
+    left[:, :count] = own[...]
+    left[:, count : 2 * count] = near[...]
+    left[mine, 2 * count : 3 * count] = far[:half, :]
+    left[other, 2 * count : 3 * count] = far_x[:half, :]
+    left[mine, 3 * count :] = cross[half:, :]
+    left[other, 3 * count :] = cross_x[half:, :]
 
     def body(at):
-        total = None
-        for left, right in zip(lefts, rights):
-            term = jnp.dot(left[...], right[:, at], preferred_element_type=jnp.float32)
-            total = term if total is None else total + term
+        total = jnp.dot(left[...], stacked(rights, at), preferred_element_type=jnp.float32)
         for s in range(zs):
             outs[s][:, at] = total[s * rows : (s + 1) * rows, :].astype(outs[s].dtype)
 
@@ -115,12 +136,9 @@
 
 
 def near_kernel(zs, me_ref, rep_ref, *refs):
-    turned, (one, two), chunks = refs[:2], refs[2:4], refs[4 : 4 + 2 * zs]
-    keep, send, early, left, total = refs[4 + 2 * zs :]
+    turned, left, chunks = refs[:2], refs[2], refs[3 : 3 + 2 * zs]
+    keep, send, early, total = refs[3 + 2 * zs :]
     out_rows(zs, me_ref, rep_ref, turned, chunks, keep, send, total)
-    width = one.shape[0]
-    left[:, :width] = one[...].T
-    left[:, width:] = two[...].T
     order = chunks[0::2] + chunks[1::2]
 
     def body(at):
@@ -137,12 +155,8 @@
     out_rows(zs, me_ref, rep_ref, turned, chunks, keep, send, total)
 
 
-def back_kernel(zs, *refs):
-    (one, two, gate_ref, up_ref, early), chunks = refs[:5], refs[5 : 5 + 2 * zs]
-    gate_out, up_out, left = refs[5 + 2 * zs :]
-    width = one.shape[0]
-    left[:, :width] = one[...].T
-    left[:, width:] = two[...].T
+def back_kernel(zs, left, gate_ref, up_ref, early, *refs):
+    chunks, (gate_out, up_out) = refs[: 2 * zs], refs[2 * zs :]
     order = chunks[0::2] + chunks[1::2]
 
     def body(at):
@@ -235,22 +249,37 @@
     cotangent = out_grad.reshape(tokens, depth)
 
     chunk = {0: lax.optimization_barrier(master.astype(jnp.bfloat16))}
-    for s in spread:
-        chunk[4 * s] = swap(chunk[0], 4 * s)
-    for s in range(zs):
-        chunk[4 * s + 2] = swap(chunk[4 * s], 2)
+    chunk[2] = swap(chunk[0], 2)
+    chunk[4] = swap(chunk[0], 4)
+    chunk[8] = swap(chunk[0], 8)
+    chunk[12] = swap(chunk[8], 4)
+    chunk[6] = swap(chunk[2], 4)
+    chunk[10] = swap(chunk[8], 2)
+    chunk[14] = swap(chunk[12], 2)
     for s in range(zs):
         chunk[4 * s + 1] = swap(chunk[4 * s], 1)
         chunk[4 * s + 3] = swap(chunk[4 * s + 2], 1)
 
+    def across_rep(value):
+        return lax.ppermute(value, "rep", [(0, 1), (1, 0)])
+
     picked = call(
         functools.partial(select_kernel, zs, rows),
-        [bf16(zs * rows, tokens)] * 4,
-        [me_arr, cotangent],
+        [bf16(zs * rows, tokens)] * 3 + [bf16(2 * zs * rows, tokens)],
+        [me_arr, rep_arr, cotangent],
         [pltpu.VMEM((depth, tokens), jnp.bfloat16)],
-        smem=1,
-    )
-    lefts = [picked[0]] + [swap(picked[m], m) for m in range(1, 4)]
+        smem=2,
+    )
+    far_half = swap(picked[2], 2)
+    far_rest = across_rep(far_half)
+    lefts = [
+        picked[0],
+        swap(picked[1], 1),
+        far_half,
+        far_rest,
+        swap(far_half, 1),
+        swap(far_rest, 1),
+    ]
     hidden, sums = [], []
     for lo, hi in zip(cuts[:-1], cuts[1:]):
         own = gated(gate[:, lo:hi], up_val[:, lo:hi])
@@ -261,29 +290,32 @@
         parts = call(
             functools.partial(grads_kernel, zs, rows),
             [f32(rows, size)] + [bf16(rows, size)] * (zs - 1),
-            lefts + rights,
+            [rep_arr] + lefts + rights,
+            [pltpu.VMEM((zs * rows, 4 * tokens), jnp.bfloat16)],
+            smem=1,
             flops=8 * zs * rows * tokens * size,
         )
         sums.extend([parts[0]] + [swap(parts[s], 4 * s) for s in spread])
-    turned = call(turn_kernel, [bf16(h.shape[1], tokens) for h in hidden], hidden)
+    first_t, second_t, left_near, left_far = call(
+        turn_kernel,
+        [bf16(h.shape[1], tokens) for h in hidden] + [bf16(tokens, depth // 2)] * 2,
+        hidden + [picked[0], picked[1], picked[3]],
+    )
+    turned = [first_t, second_t]
 
     near = [chunk[4 * s + m] for s in range(zs) for m in (0, 1)]
     far = [chunk[4 * s + m] for s in range(zs) for m in (2, 3)]
     deep, half = depth // 2, depth // 4
     work = 2 * tokens * deep * width
-    left = [pltpu.VMEM((tokens, deep), jnp.bfloat16)]
     product = [pltpu.VMEM((deep, tokens), jnp.float32)]
     keep_near, send_near, early = call(
         functools.partial(near_kernel, zs),
         [f32(half, tokens), f32(half, tokens), f32(tokens, width)],
-        [me_arr, rep_arr, *turned, picked[0], picked[1], *near],
-        left + product,
+        [me_arr, rep_arr, *turned, left_near, *near],
+        product,
         smem=2,
         flops=2 * work,
     )
-
-    def across_rep(value):
-        return lax.ppermute(value, "rep", [(0, 1), (1, 0)])
 
     got_near = across_rep(send_near)
     keep_far, send_far = call(
@@ -298,8 +330,7 @@
     gate_grad, up_grad = call(
         functools.partial(back_kernel, zs),
         [bf16(tokens, width)] * 2,
-        [picked[2], picked[3], gate, up_val, early, *far],
-        left,
+        [left_far, gate, up_val, early, *far],
         flops=work,
     )
     (out,) = call(

time: 143 us -> 118 us (0.83)
  local copies, waits for them, and re-layouts: 20.1 us -> 1.16 us
  waiting for transfers between devices: 69.7 us -> 77.5 us
  Pallas kernels: 17.7 us -> 11.3 us
  starting transfers between devices: 29 us -> 24.1 us
  other arithmetic: 5.1 us -> 3.25 us
    unnamed x84 -> x12, local copies, waits for them, and re-layouts: 20.1 us -> 1.16 us
    pallas_call x9, Pallas kernels: 17.7 us -> 11.3 us  [call(): pl.pallas_call(kernel, out_shape=list(outs), in_specs=[SMEM] * smem + [VM...]
    ppermute x30 -> x31, starting transfers between devices: 26.8 us -> 20.5 us  [swap(): return lax.ppermute(value, 'dp', [(i, i ^ m) for i in range(n)])]
    ppermute x30 -> x31, waiting for transfers between devices: 69.7 us -> 73.7 us  [swap(): return lax.ppermute(value, 'dp', [(i, i ^ m) for i in range(n)])]
    ppermute x2 -> x3, waiting for transfers between devices: 0.01 us -> 3.72 us  [across_rep(): return lax.ppermute(value, 'rep', [(0, 1), (1, 0)])]
    ppermute x2 -> x3, starting transfers between devices: 2.16 us -> 3.65 us  [across_rep(): return lax.ppermute(value, 'rep', [(0, 1), (1, 0)])]
  transfers between devices with their start and end apart: 32 -> 34, of which waited for: 6 -> 13; matrix products, arithmetic and copies ran while one was open for 2% -> 3% of each run, Pallas kernels for 11% -> 8%
where the time goes in v2:
time: 118 us
  waiting for transfers between devices  77.5 us (66%)
  starting transfers between devices  24.1 us (20%)
  Pallas kernels  11.3 us (10%)
  other arithmetic  3.25 us (3%)
    ppermute x31, waiting for transfers between devices, swap(): return lax.ppermute(value, 'dp', [(i, i ^ m) for i in range(n)])  73.7 us
    ppermute x31, starting transfers between devices, swap(): return lax.ppermute(value, 'dp', [(i, i ^ m) for i in range(n)])  20.5 us
    pallas_call x9, Pallas kernels, call(): pl.pallas_call(kernel, out_shape=list(outs), in_specs=[SMEM] * smem + [VM...  11.3 us
    ppermute x3, waiting for transfers between devices, across_rep(): return lax.ppermute(value, 'rep', [(0, 1), (1, 0)])  3.72 us
    ppermute x3, starting transfers between devices, across_rep(): return lax.ppermute(value, 'rep', [(0, 1), (1, 0)])  3.65 us
  transfers between devices with their start and end apart: 34, of which 13 were waited for; matrix products, arithmetic and copies ran while one was open for 3% of the time, Pallas kernels for 8%

profile of v2, /device:TPU:0, one launch (start us, length us, event | category | flops | bytes accessed | tf_op | source)
XLA Modules:
  0.0 118.1 jit_solution(3397386308662189099)
XLA Ops:
  0.7 1.1 copy-done.5
  1.8 0.2 shard_map.109
  2.0 3.1 %collective-permute-start.18 = (bf16[256,256]{1,0:T(8,128)(2,1)S(1)}, bf16[256,256]{1,0:T(8,128)(2,1)S(1)}, u32[]{:S(2)}, u32[]{:S(2)}) collective-permute-start(bf16[256,256]{1,0:T(8,128)(2,1)S(1)} %get-tuple-element.46), channel_id=1, source_target_pairs={{0,4},{2,6},{4,0},{6,2},{8,12},{10,14},{12,8},{14,10},{16,20},{18,... | collective-permute-start | bytes 393224 | tf_op jit(solution)/shard_map/ppermute | solution.py:239
  5.1 0.0 collective-permute-start.17
  5.1 1.3 %convert_element_type.27.refs_3_ = bf16[64,2816]{1,0:T(8,128)(2,1)S(1)} convert(f32[64,2816]{1,0:T(8,128)} %refs_8_.1) | non-fusion elementwise | flops 180224 | bytes 1081344 | tf_op jit(solution)/shard_map/convert_element_type | solution.py:251
  6.4 0.5 collective-permute-start
  6.8 1.6 %collective-permute-start.1 = (bf16[64,2816]{1,0:T(8,128)(2,1)S(1)}, bf16[64,2816]{1,0:T(8,128)(2,1)S(1)}, u32[]{:S(2)}, u32[]{:S(2)}) collective-permute-start(bf16[64,2816]{1,0:T(8,128)(2,1)S(1)} %convert_element_type.27.refs_3_), channel_id=1, source_target_pairs={{0,8},{2,10},{4,12},{6,14},{8,0},{10,2},{12,4},{14,6},{16,24},{18,... | collective-permute-start | bytes 1081352 | tf_op jit(solution)/shard_map/ppermute | solution.py:239
  8.4 2.6 %collective-permute-start.3 = (bf16[64,2816]{1,0:T(8,128)(2,1)S(1)}, bf16[64,2816]{1,0:T(8,128)(2,1)S(1)}, u32[]{:S(2)}, u32[]{:S(2)}) collective-permute-start(bf16[64,2816]{1,0:T(8,128)(2,1)S(1)} %convert_element_type.27.refs_3_), channel_id=1, source_target_pairs={{0,16},{2,18},{4,20},{6,22},{8,24},{10,26},{12,28},{14,30},{16,0},... | collective-permute-start | bytes 1081352 | tf_op jit(solution)/shard_map/ppermute | solution.py:239
  11.0 0.0 collective-permute-done.18.refs_2_
  11.0 1.5 %collective-permute-start.19 = (bf16[256,256]{1,0:T(8,128)(2,1)S(1)}, bf16[256,256]{1,0:T(8,128)(2,1)S(1)}, u32[]{:S(2)}, u32[]{:S(2)}) collective-permute-start(bf16[256,256]{1,0:T(8,128)(2,1)S(1)} %collective-permute-done.18.refs_2_), channel_id=1, source_target_pairs={{0,1},{1,0},{2,3},{3,2},{4,5},{5,4},{6,7},{7,6},{8,9},{9,8},{10,11... | collective-permute-start | bytes 393224 | tf_op jit(solution)/shard_map/ppermute | solution.py:264
  12.5 0.0 collective-permute-done.17.refs_1_
  12.5 0.0 collective-permute-start.20
  12.5 1.5 %fusion.9.second.refs_6_ = bf16[256,1280]{1,0:T(8,128)(2,1)S(1)} fusion(bf16[256,2816]{1,0:T(8,128)(2,1)S(1)} %bitcast.8, bf16[256,2816]{1,0:T(8,128)(2,1)} %bitcast.11), kind=kLoop, calls=%fused_computation.13 | loop fusion | flops 2621440 | bytes 1966080 | tf_op jit(solution)/shard_map/convert_element_type | solution.py:28
  14.0 2.0 %collective-permute-done.19.refs_3_ = bf16[256,256]{1,0:T(8,128)(2,1)S(1)} collective-permute-done((bf16[256,256]{1,0:T(8,128)(2,1)S(1)}, bf16[256,256]{1,0:T(8,128)(2,1)S(1)}, u32[]{:S(2)}, u32[]{:S(2)}) %collective-permute-start.19) | collective-permute-done | bytes 131104 | tf_op jit(solution)/shard_map/ppermute | solution.py:264
  16.0 0.5 collective-permute-start.29
  16.5 1.5 %collective-permute-start.8 = (bf16[64,2816]{1,0:T(8,128)(2,1)S(1)}, bf16[64,2816]{1,0:T(8,128)(2,1)S(1)}, u32[]{:S(2)}, u32[]{:S(2)}) collective-permute-start(bf16[64,2816]{1,0:T(8,128)(2,1)S(1)} %convert_element_type.27.refs_3_), channel_id=1, source_target_pairs={{0,4},{2,6},{4,0},{6,2},{8,12},{10,14},{12,8},{14,10},{16,20},{18,... | collective-permute-start | bytes 1081352 | tf_op jit(solution)/shard_map/ppermute | solution.py:239
  18.0 0.0 collective-permute-start.21
  18.0 6.9 %collective-permute-done.1.refs_5_ = bf16[64,2816]{1,0:T(8,128)(2,1)S(1)} collective-permute-done((bf16[64,2816]{1,0:T(8,128)(2,1)S(1)}, bf16[64,2816]{1,0:T(8,128)(2,1)S(1)}, u32[]{:S(2)}, u32[]{:S(2)}) %collective-permute-start.1) | collective-permute-done | bytes 360480 | tf_op jit(solution)/shard_map/ppermute | solution.py:239
  24.9 0.0 collective-permute-start.2
  24.9 2.4 %collective-permute-done.3.refs_7_ = bf16[64,2816]{1,0:T(8,128)(2,1)S(1)} collective-permute-done((bf16[64,2816]{1,0:T(8,128)(2,1)S(1)}, bf16[64,2816]{1,0:T(8,128)(2,1)S(1)}, u32[]{:S(2)}, u32[]{:S(2)}) %collective-permute-start.3) | collective-permute-done | bytes 360480 | tf_op jit(solution)/shard_map/ppermute | solution.py:239
  27.2 0.5 fusion.4.first.refs_6_
  27.7 11.3 %collective-permute-done.8.refs_2_.refs_0_ = bf16[64,2816]{1,0:T(8,128)(2,1)S(1)} collective-permute-done((bf16[64,2816]{1,0:T(8,128)(2,1)S(1)}, bf16[64,2816]{1,0:T(8,128)(2,1)S(1)}, u32[]{:S(2)}, u32[]{:S(2)}) %collective-permute-start.8) | collective-permute-done | bytes 360480 | tf_op jit(solution)/shard_map/ppermute | solution.py:239
  39.0 0.5 collective-permute-start.23
  39.5 0.4 collective-permute-start.5
  40.0 0.0 collective-permute-done.29.refs_8_
  40.0 1.6 %collective-permute-start.10 = (bf16[64,2816]{1,0:T(8,128)(2,1)S(1)}, bf16[64,2816]{1,0:T(8,128)(2,1)S(1)}, u32[]{:S(2)}, u32[]{:S(2)}) collective-permute-start(bf16[64,2816]{1,0:T(8,128)(2,1)S(1)} %collective-permute-done.8.refs_2_.refs_0_), channel_id=1, source_target_pairs={{0,8},{2,10},{4,12},{6,14},{8,0},{10,2},{12,4},{14,6},{16,24},{18,... | collective-permute-start | bytes 1081352 | tf_op jit(solution)/shard_map/ppermute | solution.py:239
  41.6 0.0 collective-permute-done.2.refs_6_
  41.6 1.5 %collective-permute-start.12 = (bf16[64,2816]{1,0:T(8,128)(2,1)S(1)}, bf16[64,2816]{1,0:T(8,128)(2,1)S(1)}, u32[]{:S(2)}, u32[]{:S(2)}) collective-permute-start(bf16[64,2816]{1,0:T(8,128)(2,1)S(1)} %collective-permute-done.3.refs_7_), channel_id=1, source_target_pairs={{0,4},{2,6},{4,0},{6,2},{8,12},{10,14},{12,8},{14,10},{16,20},{18,... | collective-permute-start | bytes 1081352 | tf_op jit(solution)/shard_map/ppermute | solution.py:239
  43.1 0.0 collective-permute-done.4.refs_8_
  43.1 0.0 collective-permute-start.9
  43.1 7.7 %collective-permute-done.5.refs_9_ = bf16[64,2816]{1,0:T(8,128)(2,1)S(1)} collective-permute-done((bf16[64,2816]{1,0:T(8,128)(2,1)S(1)}, bf16[64,2816]{1,0:T(8,128)(2,1)S(1)}, u32[]{:S(2)}, u32[]{:S(2)}) %collective-permute-start.5) | collective-permute-done | bytes 360480 | tf_op jit(solution)/shard_map/ppermute | solution.py:239
  50.8 0.0 collective-permute-start.6
  50.8 4.3 %collective-permute-done.10.refs_4_.refs_2_ = bf16[64,2816]{1,0:T(8,128)(2,1)S(1)} collective-permute-done((bf16[64,2816]{1,0:T(8,128)(2,1)S(1)}, bf16[64,2816]{1,0:T(8,128)(2,1)S(1)}, u32[]{:S(2)}, u32[]{:S(2)}) %collective-permute-start.10) | collective-permute-done | bytes 360480 | tf_op jit(solution)/shard_map/ppermute | solution.py:239
  55.2 8.9 %collective-permute-done.12.refs_6_.refs_4_ = bf16[64,2816]{1,0:T(8,128)(2,1)S(1)} collective-permute-done((bf16[64,2816]{1,0:T(8,128)(2,1)S(1)}, bf16[64,2816]{1,0:T(8,128)(2,1)S(1)}, u32[]{:S(2)}, u32[]{:S(2)}) %collective-permute-start.12) | collective-permute-done | bytes 360480 | tf_op jit(solution)/shard_map/ppermute | solution.py:239
  64.1 0.5 collective-permute-start.14
  64.6 0.2 collective-permute-start.28
  64.8 0.0 collective-permute-done.6.refs_10_
  64.8 0.3 collective-permute-start.22
  65.1 0.2 collective-permute-start.24
  65.3 0.4 collective-permute-done.13.refs_7_.refs_5_
  65.7 0.1 collective-permute-start.30
  65.9 9.0 %collective-permute-done.14.refs_8_.refs_6_ = bf16[64,2816]{1,0:T(8,128)(2,1)S(1)} collective-permute-done((bf16[64,2816]{1,0:T(8,128)(2,1)S(1)}, bf16[64,2816]{1,0:T(8,128)(2,1)S(1)}, u32[]{:S(2)}, u32[]{:S(2)}) %collective-permute-start.14) | collective-permute-done | bytes 360480 | tf_op jit(solution)/shard_map/ppermute | solution.py:239
  74.9 0.0 collective-permute-start.15
  74.9 0.6 shard_map.110
  75.5 1.8 %shard_map.111 = (f32[256,256]{1,0:T(8,128)S(1)}, f32[256,256]{1,0:T(8,128)S(1)}, f32[256,2816]{1,0:T(8,128)S(1)}) custom-call(s32[1]{0:T(128)} %bitcast.me_ref, s32[1]{0:T(128)} %bitcast.1.rep_ref, bf16[1536,256]{1,0:T(8,128)(2,1)S(1)} %get-tuple-element.35.refs_0_, bf16[1280,256]{1,0:T(8,128)(2,1)S(1)} %get-tuple-element.36.refs_1_, ...), custom_call_target="tpu_custom_call" | custom-call | flops 1476395008 | bytes 7995400 | tf_op jit(solution)/shard_map/pallas_call | solution.py:213
  77.2 1.6 %collective-permute-start.7 = (f32[256,256]{1,0:T(8,128)S(1)}, f32[256,256]{1,0:T(8,128)S(1)}, u32[]{:S(2)}, u32[]{:S(2)}) collective-permute-start(f32[256,256]{1,0:T(8,128)S(1)} %get-tuple-element.39), channel_id=1, source_target_pairs={{0,1},{1,0},{2,3},{3,2},{4,5},{5,4},{6,7},{7,6},{8,9},{9,8},{10,11... | collective-permute-start | bytes 786440 | tf_op jit(solution)/shard_map/ppermute | solution.py:264
  78.8 1.0 shard_map.112
  79.8 0.0 collective-permute-done.28.refs_7_
  79.8 0.6 collective-permute-start.16
  80.4 0.0 collective-permute-done.30.refs_9_
  80.4 0.9 shard_map.116
  81.3 0.5 collective-permute-start.31
  81.8 1.0 shard_map.115
  82.9 1.6 %collective-permute-start.25 = (bf16[64,1536]{1,0:T(8,128)(2,1)S(1)}, bf16[64,1536]{1,0:T(8,128)(2,1)S(1)}, u32[]{:S(2)}, u32[]{:S(2)}) collective-permute-start(bf16[64,1536]{1,0:T(8,128)(2,1)S(1)} %get-tuple-element.48), channel_id=1, source_target_pairs={{0,8},{2,10},{4,12},{6,14},{8,0},{10,2},{12,4},{14,6},{16,24},{18,... | collective-permute-start | bytes 589832 | tf_op jit(solution)/shard_map/ppermute | solution.py:239
  84.5 0.3 collective-permute-start.26
  84.8 1.7 %collective-permute-done.7.refs_1_ = f32[256,256]{1,0:T(8,128)S(1)} collective-permute-done((f32[256,256]{1,0:T(8,128)S(1)}, f32[256,256]{1,0:T(8,128)S(1)}, u32[]{:S(2)}, u32[]{:S(2)}) %collective-permute-start.7) | collective-permute-done | bytes 262176 | tf_op jit(solution)/shard_map/ppermute | solution.py:264
  86.5 1.2 %collective-permute-start.27 = (bf16[64,1536]{1,0:T(8,128)(2,1)S(1)}, bf16[64,1536]{1,0:T(8,128)(2,1)S(1)}, u32[]{:S(2)}, u32[]{:S(2)}) collective-permute-start(bf16[64,1536]{1,0:T(8,128)(2,1)S(1)} %get-tuple-element.50), channel_id=1, source_target_pairs={{0,24},{2,26},{4,28},{6,30},{8,16},{10,18},{12,20},{14,22},{16,8},... | collective-permute-start | bytes 589832 | tf_op jit(solution)/shard_map/ppermute | solution.py:239
  87.7 3.8 %collective-permute-done.31.refs_5_ = bf16[64,1280]{1,0:T(8,128)(2,1)S(1)} collective-permute-done((bf16[64,1280]{1,0:T(8,128)(2,1)S(1)}, bf16[64,1280]{1,0:T(8,128)(2,1)S(1)}, u32[]{:S(2)}, u32[]{:S(2)}) %collective-permute-start.31) | collective-permute-done | bytes 163872 | tf_op jit(solution)/shard_map/ppermute | solution.py:239
  91.6 0.1 collective-permute-done.16.refs_3_
  91.6 1.6 %collective-permute-start.33 = (bf16[64,1280]{1,0:T(8,128)(2,1)S(1)}, bf16[64,1280]{1,0:T(8,128)(2,1)S(1)}, u32[]{:S(2)}, u32[]{:S(2)}) collective-permute-start(bf16[64,1280]{1,0:T(8,128)(2,1)S(1)} %get-tuple-element.54), channel_id=1, source_target_pairs={{0,24},{2,26},{4,28},{6,30},{8,16},{10,18},{12,20},{14,22},{16,8},... | collective-permute-start | bytes 491528 | tf_op jit(solution)/shard_map/ppermute | solution.py:239
  93.2 3.2 %shard_map.114 = (bf16[256,2816]{1,0:T(8,128)(2,1)}, bf16[256,2816]{1,0:T(8,128)(2,1)}) custom-call(bf16[256,512]{1,0:T(8,128)(2,1)S(1)} %get-tuple-element.42.left, bf16[256,2816]{1,0:T(8,128)(2,1)S(1)} %bitcast.13, bf16[256,2816]{1,0:T(8,128)(2,1)S(1)} %bitcast.10, f32[256,2816]{1,0:T(8,128)S(1)} %get-tuple-element.43.early, ...), custom_call_target="tpu_custom_call" | custom-call | flops 738197504 | bytes 11796480 | tf_op jit(solution)/shard_map/pallas_call | solution.py:213
  96.5 0.9 shard_map.113
  97.4 19.0 %collective-permute-done.32.refs_6_ = bf16[64,1280]{1,0:T(8,128)(2,1)S(1)} collective-permute-done((bf16[64,1280]{1,0:T(8,128)(2,1)S(1)}, bf16[64,1280]{1,0:T(8,128)(2,1)S(1)}, u32[]{:S(2)}, u32[]{:S(2)}) %collective-permute-start.32) | collective-permute-done | bytes 163872 | tf_op jit(solution)/shard_map/ppermute | solution.py:239
  116.4 1.7 %shard_map.117 = (f32[64,2816]{1,0:T(8,128)}, f32[64,2816]{1,0:T(8,128)}, f32[64,2816]{1,0:T(8,128)}) custom-call(f32[64,1536]{1,0:T(8,128)S(1)} %get-tuple-element.47.refs_0_, bf16[64,1536]{1,0:T(8,128)(2,1)S(1)} %collective-permute-done.25.refs_1_, bf16[64,1536]{1,0:T(8,128)(2,1)S(1)} %collective-permute-done.26.refs_2_, ...), custom_call_target="tpu_custom_call" | custom-call | bytes 6127616 | tf_op jit(solution)/shard_map/pallas_call | solution.py:213
  (28 shorter events, 0.1 us)
Async XLA Ops:
  0.6 11.9 %copy-start = (bf16[2,128,2816]{2,1,0:T(8,128)(2,1)S(1)}, bf16[2,128,2816]{2,1,0:T(8,128)(2,1)}, u32[]{:S(2)}) copy-start(bf16[2,128,2816]{2,1,0:T(8,128)(2,1)} %param.7) | copy-start | bytes 4325380
  0.6 1.2 copy-start.5
  2.0 9.0 %collective-permute-start.18 = (bf16[256,256]{1,0:T(8,128)(2,1)S(1)}, bf16[256,256]{1,0:T(8,128)(2,1)S(1)}, u32[]{:S(2)}, u32[]{:S(2)}) collective-permute-start(bf16[256,256]{1,0:T(8,128)(2,1)S(1)} %get-tuple-element.46), channel_id=1, source_target_pairs={{0,4},{2,6},{4,0},{6,2},{8,12},{10,14},{12,8},{14,10},{16,20},{18,... | collective-permute-start | bytes 393224 | tf_op jit(solution)/shard_map/ppermute | solution.py:239
  5.1 22.1 %copy-start.1 = (bf16[2,128,2816]{2,1,0:T(8,128)(2,1)S(1)}, bf16[2,128,2816]{2,1,0:T(8,128)(2,1)}, u32[]{:S(2)}) copy-start(bf16[2,128,2816]{2,1,0:T(8,128)(2,1)} %param.6) | copy-start | bytes 4325380
  5.1 7.4 %collective-permute-start.17 = (bf16[256,256]{1,0:T(8,128)(2,1)S(1)}, bf16[256,256]{1,0:T(8,128)(2,1)S(1)}, u32[]{:S(2)}, u32[]{:S(2)}) collective-permute-start(bf16[256,256]{1,0:T(8,128)(2,1)S(1)} %get-tuple-element.33.near), channel_id=1, source_target_pairs={{0,2},{2,0},{4,6},{6,4},{8,10},{10,8},{12,14},{14,12},{16,18},{18,... | collective-permute-start | bytes 393224 | tf_op jit(solution)/shard_map/ppermute | solution.py:239
  6.4 11.6 %collective-permute-start = (bf16[64,2816]{1,0:T(8,128)(2,1)S(1)}, bf16[64,2816]{1,0:T(8,128)(2,1)S(1)}, u32[]{:S(2)}, u32[]{:S(2)}) collective-permute-start(bf16[64,2816]{1,0:T(8,128)(2,1)S(1)} %convert_element_type.27.refs_3_), channel_id=1, source_target_pairs={{0,2},{2,0},{4,6},{6,4},{8,10},{10,8},{12,14},{14,12},{16,18},{18,... | collective-permute-start | bytes 1081352 | tf_op jit(solution)/shard_map/ppermute | solution.py:239
  6.8 18.0 %collective-permute-start.1 = (bf16[64,2816]{1,0:T(8,128)(2,1)S(1)}, bf16[64,2816]{1,0:T(8,128)(2,1)S(1)}, u32[]{:S(2)}, u32[]{:S(2)}) collective-permute-start(bf16[64,2816]{1,0:T(8,128)(2,1)S(1)} %convert_element_type.27.refs_3_), channel_id=1, source_target_pairs={{0,8},{2,10},{4,12},{6,14},{8,0},{10,2},{12,4},{14,6},{16,24},{18,... | collective-permute-start | bytes 1081352 | tf_op jit(solution)/shard_map/ppermute | solution.py:239
  8.4 18.8 %collective-permute-start.3 = (bf16[64,2816]{1,0:T(8,128)(2,1)S(1)}, bf16[64,2816]{1,0:T(8,128)(2,1)S(1)}, u32[]{:S(2)}, u32[]{:S(2)}) collective-permute-start(bf16[64,2816]{1,0:T(8,128)(2,1)S(1)} %convert_element_type.27.refs_3_), channel_id=1, source_target_pairs={{0,16},{2,18},{4,20},{6,22},{8,24},{10,26},{12,28},{14,30},{16,0},... | collective-permute-start | bytes 1081352 | tf_op jit(solution)/shard_map/ppermute | solution.py:239
  11.0 5.0 %collective-permute-start.19 = (bf16[256,256]{1,0:T(8,128)(2,1)S(1)}, bf16[256,256]{1,0:T(8,128)(2,1)S(1)}, u32[]{:S(2)}, u32[]{:S(2)}) collective-permute-start(bf16[256,256]{1,0:T(8,128)(2,1)S(1)} %collective-permute-done.18.refs_2_), channel_id=1, source_target_pairs={{0,1},{1,0},{2,3},{3,2},{4,5},{5,4},{6,7},{7,6},{8,9},{9,8},{10,11... | collective-permute-start | bytes 393224 | tf_op jit(solution)/shard_map/ppermute | solution.py:264
  12.5 4.0 %collective-permute-start.20 = (bf16[256,256]{1,0:T(8,128)(2,1)S(1)}, bf16[256,256]{1,0:T(8,128)(2,1)S(1)}, u32[]{:S(2)}, u32[]{:S(2)}) collective-permute-start(bf16[256,256]{1,0:T(8,128)(2,1)S(1)} %collective-permute-done.18.refs_2_), channel_id=1, source_target_pairs={{0,2},{2,0},{4,6},{6,4},{8,10},{10,8},{12,14},{14,12},{16,18},{18,... | collective-permute-start | bytes 393224 | tf_op jit(solution)/shard_map/ppermute | solution.py:239
  16.0 24.0 %collective-permute-start.29 = (bf16[256,1280]{1,0:T(8,128)(2,1)S(1)}, bf16[256,1280]{1,0:T(8,128)(2,1)S(1)}, u32[]{:S(2)}, u32[]{:S(2)}) collective-permute-start(bf16[256,1280]{1,0:T(8,128)(2,1)S(1)} %fusion.9.second.refs_6_), channel_id=1, source_target_pairs={{0,4},{2,6},{4,0},{6,2},{8,12},{10,14},{12,8},{14,10},{16,20},{18,... | collective-permute-start | bytes 1966088 | tf_op jit(solution)/shard_map/ppermute | solution.py:239
  16.5 22.6 %collective-permute-start.8 = (bf16[64,2816]{1,0:T(8,128)(2,1)S(1)}, bf16[64,2816]{1,0:T(8,128)(2,1)S(1)}, u32[]{:S(2)}, u32[]{:S(2)}) collective-permute-start(bf16[64,2816]{1,0:T(8,128)(2,1)S(1)} %convert_element_type.27.refs_3_), channel_id=1, source_target_pairs={{0,4},{2,6},{4,0},{6,2},{8,12},{10,14},{12,8},{14,10},{16,20},{18,... | collective-permute-start | bytes 1081352 | tf_op jit(solution)/shard_map/ppermute | solution.py:239
  18.0 21.5 %collective-permute-start.21 = (bf16[256,256]{1,0:T(8,128)(2,1)S(1)}, bf16[256,256]{1,0:T(8,128)(2,1)S(1)}, u32[]{:S(2)}, u32[]{:S(2)}) collective-permute-start(bf16[256,256]{1,0:T(8,128)(2,1)S(1)} %collective-permute-done.19.refs_3_), channel_id=1, source_target_pairs={{0,2},{2,0},{4,6},{6,4},{8,10},{10,8},{12,14},{14,12},{16,18},{18,... | collective-permute-start | bytes 393224 | tf_op jit(solution)/shard_map/ppermute | solution.py:239
  24.9 16.7 %collective-permute-start.2 = (bf16[64,2816]{1,0:T(8,128)(2,1)S(1)}, bf16[64,2816]{1,0:T(8,128)(2,1)S(1)}, u32[]{:S(2)}, u32[]{:S(2)}) collective-permute-start(bf16[64,2816]{1,0:T(8,128)(2,1)S(1)} %collective-permute-done.1.refs_5_), channel_id=1, source_target_pairs={{0,2},{2,0},{4,6},{6,4},{8,10},{10,8},{12,14},{14,12},{16,18},{18,... | collective-permute-start | bytes 1081352 | tf_op jit(solution)/shard_map/ppermute | solution.py:239
  27.2 15.9 %collective-permute-start.4 = (bf16[64,2816]{1,0:T(8,128)(2,1)S(1)}, bf16[64,2816]{1,0:T(8,128)(2,1)S(1)}, u32[]{:S(2)}, u32[]{:S(2)}) collective-permute-start(bf16[64,2816]{1,0:T(8,128)(2,1)S(1)} %collective-permute-done.3.refs_7_), channel_id=1, source_target_pairs={{0,2},{2,0},{4,6},{6,4},{8,10},{10,8},{12,14},{14,12},{16,18},{18,... | collective-permute-start | bytes 1081352 | tf_op jit(solution)/shard_map/ppermute | solution.py:239
  39.0 25.5 %collective-permute-start.23 = (bf16[256,1536]{1,0:T(8,128)(2,1)S(1)}, bf16[256,1536]{1,0:T(8,128)(2,1)S(1)}, u32[]{:S(2)}, u32[]{:S(2)}) collective-permute-start(bf16[256,1536]{1,0:T(8,128)(2,1)S(1)} %fusion.4.first.refs_6_), channel_id=1, source_target_pairs={{0,4},{2,6},{4,0},{6,2},{8,12},{10,14},{12,8},{14,10},{16,20},{18,... | collective-permute-start | bytes 2359304 | tf_op jit(solution)/shard_map/ppermute | solution.py:239
  39.5 11.3 %collective-permute-start.5 = (bf16[64,2816]{1,0:T(8,128)(2,1)S(1)}, bf16[64,2816]{1,0:T(8,128)(2,1)S(1)}, u32[]{:S(2)}, u32[]{:S(2)}) collective-permute-start(bf16[64,2816]{1,0:T(8,128)(2,1)S(1)} %collective-permute-done.3.refs_7_), channel_id=1, source_target_pairs={{0,8},{2,10},{4,12},{6,14},{8,0},{10,2},{12,4},{14,6},{16,24},{18,... | collective-permute-start | bytes 1081352 | tf_op jit(solution)/shard_map/ppermute | solution.py:239
  40.0 15.2 %collective-permute-start.10 = (bf16[64,2816]{1,0:T(8,128)(2,1)S(1)}, bf16[64,2816]{1,0:T(8,128)(2,1)S(1)}, u32[]{:S(2)}, u32[]{:S(2)}) collective-permute-start(bf16[64,2816]{1,0:T(8,128)(2,1)S(1)} %collective-permute-done.8.refs_2_.refs_0_), channel_id=1, source_target_pairs={{0,8},{2,10},{4,12},{6,14},{8,0},{10,2},{12,4},{14,6},{16,24},{18,... | collective-permute-start | bytes 1081352 | tf_op jit(solution)/shard_map/ppermute | solution.py:239
  41.6 22.5 %collective-permute-start.12 = (bf16[64,2816]{1,0:T(8,128)(2,1)S(1)}, bf16[64,2816]{1,0:T(8,128)(2,1)S(1)}, u32[]{:S(2)}, u32[]{:S(2)}) collective-permute-start(bf16[64,2816]{1,0:T(8,128)(2,1)S(1)} %collective-permute-done.3.refs_7_), channel_id=1, source_target_pairs={{0,4},{2,6},{4,0},{6,2},{8,12},{10,14},{12,8},{14,10},{16,20},{18,... | collective-permute-start | bytes 1081352 | tf_op jit(solution)/shard_map/ppermute | solution.py:239
  43.1 21.0 %collective-permute-start.9 = (bf16[64,2816]{1,0:T(8,128)(2,1)S(1)}, bf16[64,2816]{1,0:T(8,128)(2,1)S(1)}, u32[]{:S(2)}, u32[]{:S(2)}) collective-permute-start(bf16[64,2816]{1,0:T(8,128)(2,1)S(1)} %collective-permute-done.8.refs_2_.refs_0_), channel_id=1, source_target_pairs={{0,2},{2,0},{4,6},{6,4},{8,10},{10,8},{12,14},{14,12},{16,18},{18,... | collective-permute-start | bytes 1081352 | tf_op jit(solution)/shard_map/ppermute | solution.py:239
  50.8 14.0 %collective-permute-start.6 = (bf16[64,2816]{1,0:T(8,128)(2,1)S(1)}, bf16[64,2816]{1,0:T(8,128)(2,1)S(1)}, u32[]{:S(2)}, u32[]{:S(2)}) collective-permute-start(bf16[64,2816]{1,0:T(8,128)(2,1)S(1)} %collective-permute-done.5.refs_9_), channel_id=1, source_target_pairs={{0,2},{2,0},{4,6},{6,4},{8,10},{10,8},{12,14},{14,12},{16,18},{18,... | collective-permute-start | bytes 1081352 | tf_op jit(solution)/shard_map/ppermute | solution.py:239
  55.1 9.9 %collective-permute-start.11 = (bf16[64,2816]{1,0:T(8,128)(2,1)S(1)}, bf16[64,2816]{1,0:T(8,128)(2,1)S(1)}, u32[]{:S(2)}, u32[]{:S(2)}) collective-permute-start(bf16[64,2816]{1,0:T(8,128)(2,1)S(1)} %collective-permute-done.10.refs_4_.refs_2_), channel_id=1, source_target_pairs={{0,2},{2,0},{4,6},{6,4},{8,10},{10,8},{12,14},{14,12},{16,18},{18,... | collective-permute-start | bytes 1081352 | tf_op jit(solution)/shard_map/ppermute | solution.py:239
  64.0 1.7 %collective-permute-start.13 = (bf16[64,2816]{1,0:T(8,128)(2,1)S(1)}, bf16[64,2816]{1,0:T(8,128)(2,1)S(1)}, u32[]{:S(2)}, u32[]{:S(2)}) collective-permute-start(bf16[64,2816]{1,0:T(8,128)(2,1)S(1)} %collective-permute-done.12.refs_6_.refs_4_), channel_id=1, source_target_pairs={{0,2},{2,0},{4,6},{6,4},{8,10},{10,8},{12,14},{14,12},{16,18},{18,... | collective-permute-start | bytes 1081352 | tf_op jit(solution)/shard_map/ppermute | solution.py:239
  64.1 10.8 %collective-permute-start.14 = (bf16[64,2816]{1,0:T(8,128)(2,1)S(1)}, bf16[64,2816]{1,0:T(8,128)(2,1)S(1)}, u32[]{:S(2)}, u32[]{:S(2)}) collective-permute-start(bf16[64,2816]{1,0:T(8,128)(2,1)S(1)} %collective-permute-done.5.refs_9_), channel_id=1, source_target_pairs={{0,4},{2,6},{4,0},{6,2},{8,12},{10,14},{12,8},{14,10},{16,20},{18,... | collective-permute-start | bytes 1081352 | tf_op jit(solution)/shard_map/ppermute | solution.py:239
  64.6 15.2 %collective-permute-start.28 = (bf16[256,1280]{1,0:T(8,128)(2,1)S(1)}, bf16[256,1280]{1,0:T(8,128)(2,1)S(1)}, u32[]{:S(2)}, u32[]{:S(2)}) collective-permute-start(bf16[256,1280]{1,0:T(8,128)(2,1)S(1)} %fusion.9.second.refs_6_), channel_id=1, source_target_pairs={{0,2},{2,0},{4,6},{6,4},{8,10},{10,8},{12,14},{14,12},{16,18},{18,... | collective-permute-start | bytes 1966088 | tf_op jit(solution)/shard_map/ppermute | solution.py:239
  64.8 17.0 %collective-permute-start.22 = (bf16[256,1536]{1,0:T(8,128)(2,1)S(1)}, bf16[256,1536]{1,0:T(8,128)(2,1)S(1)}, u32[]{:S(2)}, u32[]{:S(2)}) collective-permute-start(bf16[256,1536]{1,0:T(8,128)(2,1)S(1)} %fusion.4.first.refs_6_), channel_id=1, source_target_pairs={{0,2},{2,0},{4,6},{6,4},{8,10},{10,8},{12,14},{14,12},{16,18},{18,... | collective-permute-start | bytes 2359304 | tf_op jit(solution)/shard_map/ppermute | solution.py:239
  65.1 16.8 %collective-permute-start.24 = (bf16[256,1536]{1,0:T(8,128)(2,1)S(1)}, bf16[256,1536]{1,0:T(8,128)(2,1)S(1)}, u32[]{:S(2)}, u32[]{:S(2)}) collective-permute-start(bf16[256,1536]{1,0:T(8,128)(2,1)S(1)} %collective-permute-done.23.refs_8_), channel_id=1, source_target_pairs={{0,2},{2,0},{4,6},{6,4},{8,10},{10,8},{12,14},{14,12},{16,18},{18,... | collective-permute-start | bytes 2359304 | tf_op jit(solution)/shard_map/ppermute | solution.py:239
  65.7 14.7 %collective-permute-start.30 = (bf16[256,1280]{1,0:T(8,128)(2,1)S(1)}, bf16[256,1280]{1,0:T(8,128)(2,1)S(1)}, u32[]{:S(2)}, u32[]{:S(2)}) collective-permute-start(bf16[256,1280]{1,0:T(8,128)(2,1)S(1)} %collective-permute-done.29.refs_8_), channel_id=1, source_target_pairs={{0,2},{2,0},{4,6},{6,4},{8,10},{10,8},{12,14},{14,12},{16,18},{18,... | collective-permute-start | bytes 1966088 | tf_op jit(solution)/shard_map/ppermute | solution.py:239
  74.9 2.3 %collective-permute-start.15 = (bf16[64,2816]{1,0:T(8,128)(2,1)S(1)}, bf16[64,2816]{1,0:T(8,128)(2,1)S(1)}, u32[]{:S(2)}, u32[]{:S(2)}) collective-permute-start(bf16[64,2816]{1,0:T(8,128)(2,1)S(1)} %collective-permute-done.14.refs_8_.refs_6_), channel_id=1, source_target_pairs={{0,2},{2,0},{4,6},{6,4},{8,10},{10,8},{12,14},{14,12},{16,18},{18,... | collective-permute-start | bytes 1081352 | tf_op jit(solution)/shard_map/ppermute | solution.py:239
  77.2 9.2 %collective-permute-start.7 = (f32[256,256]{1,0:T(8,128)S(1)}, f32[256,256]{1,0:T(8,128)S(1)}, u32[]{:S(2)}, u32[]{:S(2)}) collective-permute-start(f32[256,256]{1,0:T(8,128)S(1)} %get-tuple-element.39), channel_id=1, source_target_pairs={{0,1},{1,0},{2,3},{3,2},{4,5},{5,4},{6,7},{7,6},{8,9},{9,8},{10,11... | collective-permute-start | bytes 786440 | tf_op jit(solution)/shard_map/ppermute | solution.py:264
  79.8 11.8 %collective-permute-start.16 = (f32[256,256]{1,0:T(8,128)S(1)}, f32[256,256]{1,0:T(8,128)S(1)}, u32[]{:S(2)}, u32[]{:S(2)}) collective-permute-start(f32[256,256]{1,0:T(8,128)S(1)} %get-tuple-element.41), channel_id=1, source_target_pairs={{0,1},{1,0},{2,3},{3,2},{4,5},{5,4},{6,7},{7,6},{8,9},{9,8},{10,11... | collective-permute-start | bytes 786440 | tf_op jit(solution)/shard_map/ppermute | solution.py:264
  81.3 10.2 %collective-permute-start.31 = (bf16[64,1280]{1,0:T(8,128)(2,1)S(1)}, bf16[64,1280]{1,0:T(8,128)(2,1)S(1)}, u32[]{:S(2)}, u32[]{:S(2)}) collective-permute-start(bf16[64,1280]{1,0:T(8,128)(2,1)S(1)} %get-tuple-element.52), channel_id=1, source_target_pairs={{0,8},{2,10},{4,12},{6,14},{8,0},{10,2},{12,4},{14,6},{16,24},{18,... | collective-permute-start | bytes 491528 | tf_op jit(solution)/shard_map/ppermute | solution.py:239
  82.9 33.5 %collective-permute-start.25 = (bf16[64,1536]{1,0:T(8,128)(2,1)S(1)}, bf16[64,1536]{1,0:T(8,128)(2,1)S(1)}, u32[]{:S(2)}, u32[]{:S(2)}) collective-permute-start(bf16[64,1536]{1,0:T(8,128)(2,1)S(1)} %get-tuple-element.48), channel_id=1, source_target_pairs={{0,8},{2,10},{4,12},{6,14},{8,0},{10,2},{12,4},{14,6},{16,24},{18,... | collective-permute-start | bytes 589832 | tf_op jit(solution)/shard_map/ppermute | solution.py:239
  84.5 31.9 %collective-permute-start.26 = (bf16[64,1536]{1,0:T(8,128)(2,1)S(1)}, bf16[64,1536]{1,0:T(8,128)(2,1)S(1)}, u32[]{:S(2)}, u32[]{:S(2)}) collective-permute-start(bf16[64,1536]{1,0:T(8,128)(2,1)S(1)} %get-tuple-element.49), channel_id=1, source_target_pairs={{0,16},{2,18},{4,20},{6,22},{8,24},{10,26},{12,28},{14,30},{16,0},... | collective-permute-start | bytes 589832 | tf_op jit(solution)/shard_map/ppermute | solution.py:239
  86.5 29.9 %collective-permute-start.27 = (bf16[64,1536]{1,0:T(8,128)(2,1)S(1)}, bf16[64,1536]{1,0:T(8,128)(2,1)S(1)}, u32[]{:S(2)}, u32[]{:S(2)}) collective-permute-start(bf16[64,1536]{1,0:T(8,128)(2,1)S(1)} %get-tuple-element.50), channel_id=1, source_target_pairs={{0,24},{2,26},{4,28},{6,30},{8,16},{10,18},{12,20},{14,22},{16,8},... | collective-permute-start | bytes 589832 | tf_op jit(solution)/shard_map/ppermute | solution.py:239
  91.5 24.8 %collective-permute-start.32 = (bf16[64,1280]{1,0:T(8,128)(2,1)S(1)}, bf16[64,1280]{1,0:T(8,128)(2,1)S(1)}, u32[]{:S(2)}, u32[]{:S(2)}) collective-permute-start(bf16[64,1280]{1,0:T(8,128)(2,1)S(1)} %get-tuple-element.53), channel_id=1, source_target_pairs={{0,16},{2,18},{4,20},{6,22},{8,24},{10,26},{12,28},{14,30},{16,0},... | collective-permute-start | bytes 491528 | tf_op jit(solution)/shard_map/ppermute | solution.py:239
  91.6 24.7 %collective-permute-start.33 = (bf16[64,1280]{1,0:T(8,128)(2,1)S(1)}, bf16[64,1280]{1,0:T(8,128)(2,1)S(1)}, u32[]{:S(2)}, u32[]{:S(2)}) collective-permute-start(bf16[64,1280]{1,0:T(8,128)(2,1)S(1)} %get-tuple-element.54), channel_id=1, source_target_pairs={{0,24},{2,26},{4,28},{6,30},{8,16},{10,18},{12,20},{14,22},{16,8},... | collective-permute-start | bytes 491528 | tf_op jit(solution)/shard_map/ppermute | solution.py:239
  93.2 23.1 %copy-start.3 = (f32[64,2816]{1,0:T(8,128)S(1)}, f32[64,2816]{1,0:T(8,128)}, u32[]{:S(2)}) copy-start(f32[64,2816]{1,0:T(8,128)} %refs_9_.1) | copy-start | bytes 2162692
  93.2 23.2 %copy-start.4 = (f32[64,2816]{1,0:T(8,128)S(1)}, f32[64,2816]{1,0:T(8,128)}, u32[]{:S(2)}) copy-start(f32[64,2816]{1,0:T(8,128)} %refs_10_.1) | copy-start | bytes 2162692
  96.5 19.9 %copy-start.2 = (f32[64,2816]{1,0:T(8,128)S(1)}, f32[64,2816]{1,0:T(8,128)}, u32[]{:S(2)}) copy-start(f32[64,2816]{1,0:T(8,128)} %refs_8_.1) | copy-start | bytes 2162692

commit v3 on v2

--- a/solution.py
+++ b/solution.py
@@ -81,9 +81,11 @@
             rest[first : first + rows, :] = block(s, m)
 
 
-def turn_kernel(first, second, own, near, rest, first_t, second_t, left_near, left_far):
-    first_t[...] = first[...].T
-    second_t[...] = second[...].T
+def turn_kernel(count, *refs):
+    hidden, (own, near, rest) = refs[:count], refs[count : count + 3]
+    turned, (left_near, left_far) = refs[count + 3 : 2 * count + 3], refs[2 * count + 3 :]
+    for source, target in zip(hidden, turned):
+        target[...] = source[...].T
     width = own.shape[0]
     left_near[:, :width] = own[...].T
     left_near[:, width:] = near[...].T
@@ -95,11 +97,11 @@
         body(slice(start, start + TILE))
 
 
-def grads_kernel(zs, rows, rep_ref, *refs):
+def grads_kernel(rows, rep_ref, *refs):
     own, near, far, far_x, cross, cross_x = refs[:6]
-    rights, outs, left = refs[6:10], refs[10 : 10 + zs], refs[10 + zs]
+    rights, (mine_out, side, across, left) = refs[6:10], refs[10:]
     count = own.shape[1]
-    half = zs * rows // 2
+    half = 2 * rows
     mine = pl.ds(pl.multiple_of(rep_ref[0] * half, half), half)
     other = pl.ds(pl.multiple_of((1 - rep_ref[0]) * half, half), half)
     left[:, :count] = own[...]
@@ -111,110 +113,176 @@
 
     def body(at):
         total = jnp.dot(left[...], stacked(rights, at), preferred_element_type=jnp.float32)
-        for s in range(zs):
-            outs[s][:, at] = total[s * rows : (s + 1) * rows, :].astype(outs[s].dtype)
+        mine_out[:, at] = total[:rows]
+        side[:rows, at] = total[rows : 2 * rows].astype(side.dtype)
+        side[rows:, at] = total[3 * rows :].astype(side.dtype)
+        across[:, at] = total[2 * rows : 3 * rows]
 
     each_tile(rights[0].shape[1], body)
+
+
+def add_kernel(across, side, out):
+    rows = across.shape[0]
+    out[...] = (across[...] + side[rows:, :].astype(jnp.float32)).astype(out.dtype)
 
 
 def stacked(chunks, at):
     return jnp.concatenate([chunk[:, at] for chunk in chunks], axis=0)
 
 
-def out_rows(zs, me_ref, rep_ref, turned, chunks, keep, send, total):
+def flipped(zs, me_ref, rep_ref):
+    return ((me_ref[0] // (2 * zs)) ^ rep_ref[0]) & 1
+
+
+def out_rows(turned, chunks):
     base, value = 0, None
     for piece in turned:
         at = slice(base, base + piece.shape[0])
         term = jnp.dot(stacked(chunks, at), piece[...], preferred_element_type=jnp.float32)
         value = term if value is None else value + term
         base = at.stop
-    total[...] = value
+    return value
+
+
+def back_term(left, chunks, at):
+    order = chunks[0::2] + chunks[1::2]
+    return jnp.dot(left[...], stacked(order, at), preferred_element_type=jnp.float32)
+
+
+def near_kernel(zs, pieces, me_ref, rep_ref, *refs):
+    turned, left, chunks = refs[:pieces], refs[pieces], refs[pieces + 1 : pieces + 1 + 2 * zs]
+    keep, send, early, total = refs[pieces + 1 + 2 * zs :]
+    total[...] = out_rows(turned, chunks)
     half = keep.shape[0]
-    flip = ((me_ref[0] // (2 * zs)) ^ rep_ref[0]) & 1
+    flip = flipped(zs, me_ref, rep_ref)
     keep[...] = total[pl.ds(pl.multiple_of(flip * half, half), half), :]
     send[...] = total[pl.ds(pl.multiple_of((1 - flip) * half, half), half), :]
 
-
-def near_kernel(zs, me_ref, rep_ref, *refs):
-    turned, left, chunks = refs[:2], refs[2], refs[3 : 3 + 2 * zs]
-    keep, send, early, total = refs[3 + 2 * zs :]
-    out_rows(zs, me_ref, rep_ref, turned, chunks, keep, send, total)
-    order = chunks[0::2] + chunks[1::2]
-
     def body(at):
-        early[:, at] = jnp.dot(
-            left[...], stacked(order, at), preferred_element_type=jnp.float32
+        early[:, at] = back_term(left, chunks, at)
+
+    each_tile(early.shape[1], body)
+
+
+def middle_kernel(zs, pieces, me_ref, rep_ref, *refs):
+    turned, chunks = refs[:pieces], refs[pieces : pieces + 2 * (zs - 1)]
+    keep, send, hold = refs[pieces + 2 * (zs - 1) :]
+    value = out_rows(turned, chunks)
+    span = keep.shape[0]
+    flip = flipped(zs, me_ref, rep_ref)
+    hold[...] = value[span : 2 * span]
+
+    @pl.when(flip == 0)
+    def _():
+        keep[...] = value[:span]
+        send[...] = value[2 * span :]
+
+    @pl.when(flip == 1)
+    def _():
+        keep[...] = value[2 * span :]
+        send[...] = value[:span]
+
+
+def last_kernel(zs, pieces, me_ref, rep_ref, *refs):
+    turned, (hold, one, two, keep, send) = refs[:pieces], refs[pieces:]
+    value = out_rows(turned, (one, two))
+    flip = flipped(zs, me_ref, rep_ref)
+
+    @pl.when(flip == 0)
+    def _():
+        keep[...] = hold[...]
+        send[...] = value
+
+    @pl.when(flip == 1)
+    def _():
+        keep[...] = value
+        send[...] = hold[...]
+
+
+def store_tile(index, at, sems, pairs):
+    copies = []
+    for k, (source, target) in enumerate(pairs):
+        copy = pltpu.make_async_copy(
+            source.at[:, at], target.at[:, at], sems.at[index * len(pairs) + k]
         )
-
-    each_tile(early.shape[1], body)
-
-
-def far_kernel(zs, me_ref, rep_ref, *refs):
-    turned, chunks = refs[:2], refs[2 : 2 + 2 * zs]
-    keep, send, total = refs[2 + 2 * zs :]
-    out_rows(zs, me_ref, rep_ref, turned, chunks, keep, send, total)
-
-
-def back_kernel(zs, left, gate_ref, up_ref, early, *refs):
-    chunks, (gate_out, up_out) = refs[: 2 * zs], refs[2 * zs :]
-    order = chunks[0::2] + chunks[1::2]
-
+        copy.start()
+        copies.append(copy)
+    return copies
+
+
+def slopes_kernel(gate_ref, up_ref, gate_slope, up_slope):
     def body(at):
-        hid_grad = early[:, at] + jnp.dot(
-            left[...], stacked(order, at), preferred_element_type=jnp.float32
-        )
         gate = gate_ref[:, at].astype(jnp.float32)
-        up_val = up_ref[:, at].astype(jnp.float32)
         sig = jax.nn.sigmoid(gate)
-        gate_out[:, at] = (
-            hid_grad * up_val * sig * (1.0 + gate * (1.0 - sig))
-        ).astype(jnp.bfloat16)
-        up_out[:, at] = (hid_grad * gate * sig).astype(jnp.bfloat16)
+        gate_slope[:, at] = up_ref[:, at].astype(jnp.float32) * sig * (1.0 + gate * (1.0 - sig))
+        up_slope[:, at] = gate * sig
+
+    each_tile(gate_ref.shape[1], body)
+
+
+def back_kernel(zs, left, gate_slope, up_slope, early, *refs):
+    chunks, (gate_out, up_out, gate_tiles, up_tiles, sems) = refs[: 2 * zs], refs[2 * zs :]
+    copies = []
+
+    def body(at):
+        hid_grad = early[:, at] + back_term(left, chunks, at)
+        gate_tiles[:, at] = (hid_grad * gate_slope[:, at]).astype(jnp.bfloat16)
+        up_tiles[:, at] = (hid_grad * up_slope[:, at]).astype(jnp.bfloat16)
+        pairs = ((gate_tiles, gate_out), (up_tiles, up_out))
+        copies.extend(store_tile(len(copies) // 2, at, sems, pairs))
 
     each_tile(gate_out.shape[1], body)
+    for copy in copies:
+        copy.wait()
 
 
 def merge_kernel(zs, rows, me_ref, *refs):
-    parts, out, placed = refs[:4], refs[4], refs[5]
+    keep, got, middle, got_middle, last, got_last, out, placed = refs
     me = me_ref[0]
-    for far in range(2):
-        value = parts[2 * far][...] + parts[2 * far + 1][...]
-        for s in range(zs // 2):
+
+    def place(value, first, far):
+        for s in range(value.shape[0] // (2 * rows)):
             for core in range(2):
-                block = me ^ (4 * s + 2 * far + core)
+                block = me ^ (4 * (first + s) + 2 * far + core)
                 start = pl.multiple_of((block % (2 * zs)) * rows, rows)
-                first = (2 * s + core) * rows
-                placed[pl.ds(start, rows), :] = value[first : first + rows, :]
+                at = (2 * s + core) * rows
+                placed[pl.ds(start, rows), :] = value[at : at + rows, :]
+
+    place(keep[...] + got[...], 0, 0)
+    place(middle[...] + got_middle[...], 0, 1)
+    place(last[...] + got_last[...], 1, 1)
     out[...] = placed[...].T.astype(out.dtype)
 
 
-def adamw_kernel(zs, total, *refs):
-    pieces, states, outs = refs[: 2 * zs], refs[2 * zs : 2 * zs + 3], refs[2 * zs + 3 :]
-    base = 0
-    for p in range(2):
-        own, others = pieces[p * zs], pieces[p * zs + 1 : (p + 1) * zs]
+def adamw_kernel(total, pieces, *refs):
+    parts, states = refs[: 3 * pieces], refs[3 * pieces : 3 * pieces + 3]
+    outs, values, sems = refs[3 * pieces + 3 :][:3], refs[3 * pieces + 6 : -1], refs[-1]
+    rows = outs[0].shape[0]
+    base, copies = 0, []
+    for p in range(pieces):
+        own, side, passed = parts[3 * p : 3 * p + 3]
         at = slice(base, base + own.shape[1])
         base = at.stop
-        grad = own[...]
-        for other in others:
-            grad = grad + other[...].astype(jnp.float32)
-        for out, value in zip(
-            outs, adamw(grad / jnp.float32(total), *[state[:, at] for state in states])
-        ):
-            out[:, at] = value
+        grad = own[...] + side[:rows, :].astype(jnp.float32) + passed[...].astype(jnp.float32)
+        results = adamw(grad / jnp.float32(total), *[state[:, at] for state in states])
+        for tile, value in zip(values, results):
+            tile[:, at] = value
+        copies.extend(store_tile(p, at, sems, tuple(zip(values, outs))))
+    for copy in copies:
+        copy.wait()
 
 
 def estimate(flops, moved):
     return pl.CostEstimate(flops=int(flops), bytes_accessed=int(moved), transcendentals=0)
 
 
-def call(kernel, outs, ins, scratch=(), smem=0, flops=0):
+def call(kernel, outs, ins, scratch=(), smem=0, flops=0, copied=False):
     moved = sum(v.size * v.dtype.itemsize for v in list(ins) + list(outs))
     return pl.pallas_call(
         kernel,
         out_shape=list(outs),
         in_specs=[SMEM] * smem + [VMEM] * (len(ins) - smem),
-        out_specs=[VMEM] * len(outs),
+        out_specs=[pl.BlockSpec(memory_space=pl.ANY) if copied else VMEM] * len(outs),
         scratch_shapes=list(scratch),
         compiler_params=pltpu.CompilerParams(vmem_limit_bytes=24 << 20),
         cost_estimate=estimate(flops, moved),
@@ -232,8 +300,8 @@
     me_arr = jnp.full((1,), lax.axis_index("dp"), jnp.int32)
     rep_arr = jnp.full((1,), lax.axis_index("rep"), jnp.int32)
     tiles = width // TILE
-    cuts = [0, (tiles + 1) // 2 * TILE, width]
-    spread = range(1, zs)
+    pieces = len(SHARES)
+    cuts = [tiles * sum(SHARES[:p]) // sum(SHARES) * TILE for p in range(pieces + 1)]
 
     def swap(value, m):
         return lax.ppermute(value, "dp", [(i, i ^ m) for i in range(n)])
@@ -273,12 +341,7 @@
     far_half = swap(picked[2], 2)
     far_rest = across_rep(far_half)
     lefts = [
-        picked[0],
-        swap(picked[1], 1),
-        far_half,
-        far_rest,
-        swap(far_half, 1),
-        swap(far_rest, 1),
+        picked[0], swap(picked[1], 1), far_half, far_rest, swap(far_half, 1), swap(far_rest, 1)
     ]
     hidden, sums = [], []
     for lo, hi in zip(cuts[:-1], cuts[1:]):
@@ -287,63 +350,75 @@
         across = swap(own, 2)
         rights = [own, swap(own, 1), across, swap(across, 1)]
         size = hi - lo
-        parts = call(
-            functools.partial(grads_kernel, zs, rows),
-            [f32(rows, size)] + [bf16(rows, size)] * (zs - 1),
+        own_sum, side, across_sum = call(
+            functools.partial(grads_kernel, rows),
+            [f32(rows, size), bf16(2 * rows, size), f32(rows, size)],
             [rep_arr] + lefts + rights,
             [pltpu.VMEM((zs * rows, 4 * tokens), jnp.bfloat16)],
             smem=1,
             flops=8 * zs * rows * tokens * size,
         )
-        sums.extend([parts[0]] + [swap(parts[s], 4 * s) for s in spread])
-    first_t, second_t, left_near, left_far = call(
-        turn_kernel,
+        side = swap(side, 4)
+        (passed,) = call(add_kernel, [bf16(rows, size)], [across_sum, side])
+        sums.extend([own_sum, side, swap(passed, 8)])
+    *turned, left_near, left_far = call(
+        functools.partial(turn_kernel, pieces),
         [bf16(h.shape[1], tokens) for h in hidden] + [bf16(tokens, depth // 2)] * 2,
         hidden + [picked[0], picked[1], picked[3]],
     )
-    turned = [first_t, second_t]
 
     near = [chunk[4 * s + m] for s in range(zs) for m in (0, 1)]
     far = [chunk[4 * s + m] for s in range(zs) for m in (2, 3)]
     deep, half = depth // 2, depth // 4
+    last = 2 * rows
     work = 2 * tokens * deep * width
-    product = [pltpu.VMEM((deep, tokens), jnp.float32)]
-    keep_near, send_near, early = call(
-        functools.partial(near_kernel, zs),
+    keep, send, early = call(
+        functools.partial(near_kernel, zs, pieces),
         [f32(half, tokens), f32(half, tokens), f32(tokens, width)],
         [me_arr, rep_arr, *turned, left_near, *near],
-        product,
+        [pltpu.VMEM((deep, tokens), jnp.float32)],
         smem=2,
         flops=2 * work,
     )
-
-    got_near = across_rep(send_near)
-    keep_far, send_far = call(
-        functools.partial(far_kernel, zs),
-        [f32(half, tokens), f32(half, tokens)],
-        [me_arr, rep_arr, *turned, *far],
-        product,
+    got = across_rep(send)
+    middle, send_middle, hold = call(
+        functools.partial(middle_kernel, zs, pieces),
+        [f32(last, tokens)] * 3,
+        [me_arr, rep_arr, *turned, *far[:-2]],
         smem=2,
         flops=work,
     )
-    got_far = across_rep(send_far)
+    got_middle = across_rep(send_middle)
+    keep_last, send_last = call(
+        functools.partial(last_kernel, zs, pieces),
+        [f32(last, tokens)] * 2,
+        [me_arr, rep_arr, *turned, hold, *far[-2:]],
+        smem=2,
+        flops=work // zs,
+    )
+    got_last = across_rep(send_last)
+    slopes = call(slopes_kernel, [f32(tokens, width)] * 2, [gate, up_val])
     gate_grad, up_grad = call(
         functools.partial(back_kernel, zs),
         [bf16(tokens, width)] * 2,
-        [left_far, gate, up_val, early, *far],
+        [left_far, *slopes, early, *far],
+        [pltpu.VMEM((tokens, width), jnp.bfloat16)] * 2 + [pltpu.SemaphoreType.DMA((2 * tiles,))],
         flops=work,
+        copied=True,
     )
     (out,) = call(
         functools.partial(merge_kernel, zs, rows),
         [bf16(tokens, 2 * half)],
-        [me_arr, keep_near, got_near, keep_far, got_far],
+        [me_arr, keep, got, middle, got_middle, keep_last, got_last],
         [pltpu.VMEM((2 * half, tokens), jnp.float32)],
         smem=1,
     )
     master_new, first, second = call(
-        functools.partial(adamw_kernel, zs, total),
+        functools.partial(adamw_kernel, total, pieces),
         [f32(rows, width)] * 3,
         sums + [master, moment_one, moment_two],
+        [pltpu.VMEM((rows, width), jnp.float32)] * 3 + [pltpu.SemaphoreType.DMA((3 * pieces,))],
+        copied=True,
     )
     return (
         out.reshape(micro, span, 2 * half),
@@ -353,6 +428,9 @@
         first,
         second,
     )
+
+
+SHARES = (4, 4, 3)
 
 
 def small(n, reps, width):

time: 118 us -> 121 us (1.025)
  starting transfers between devices: 24.1 us -> 31.9 us
  waiting for transfers between devices: 77.5 us -> 71.3 us
    ppermute x31 -> x34, starting transfers between devices: 20.5 us -> 28.7 us  [swap(): return lax.ppermute(value, 'dp', [(i, i ^ m) for i in range(n)])]
    ppermute x3 -> x4, waiting for transfers between devices: 3.72 us -> 0.01 us  [across_rep(): return lax.ppermute(value, 'rep', [(0, 1), (1, 0)])]
    ppermute x31 -> x34, waiting for transfers between devices: 73.7 us -> 71.3 us  [swap(): return lax.ppermute(value, 'dp', [(i, i ^ m) for i in range(n)])]
    ppermute x3 -> x4, starting transfers between devices: 3.65 us -> 3.2 us  [across_rep(): return lax.ppermute(value, 'rep', [(0, 1), (1, 0)])]
    pallas_call x9 -> x15, Pallas kernels: 11.3 us -> 11.7 us  [call(): pl.pallas_call(kernel, out_shape=list(outs), in_specs=[SMEM] * smem + [VM...]
  transfers between devices with their start and end apart: 34 -> 38, of which waited for: 13 -> 13; matrix products, arithmetic and copies ran while one was open for 3% -> 3% of each run, Pallas kernels for 8% -> 9%
where the time goes in v3:
time: 121 us
  waiting for transfers between devices  71.3 us (59%)
  starting transfers between devices  31.9 us (26%)
  Pallas kernels  11.7 us (10%)
  other arithmetic  4.24 us (4%)
    ppermute x34, waiting for transfers between devices, swap(): return lax.ppermute(value, 'dp', [(i, i ^ m) for i in range(n)])  71.3 us
    ppermute x34, starting transfers between devices, swap(): return lax.ppermute(value, 'dp', [(i, i ^ m) for i in range(n)])  28.7 us
    pallas_call x15, Pallas kernels, call(): pl.pallas_call(kernel, out_shape=list(outs), in_specs=[SMEM] * smem + [VM...  11.7 us
    ppermute x4, starting transfers between devices, across_rep(): return lax.ppermute(value, 'rep', [(0, 1), (1, 0)])  3.2 us
    convert_element_type x2, other arithmetic, gated(): (gate * jax.nn.sigmoid(gate) * up_val.astype(jnp.float32)).astype(jnp.bfl...  3.09 us
  transfers between devices with their start and end apart: 38, of which 13 were waited for; matrix products, arithmetic and copies ran while one was open for 3% of the time, Pallas kernels for 9%

profile of v3, /device:TPU:0, one launch (start us, length us, event | category | flops | bytes accessed | tf_op | source)
XLA Modules:
  0.0 121.2 jit_solution(12290086706204687378)
XLA Ops:
  0.7 1.1 copy-done.5
  1.8 0.2 shard_map.109
  2.0 3.1 %collective-permute-start.19 = (bf16[256,256]{1,0:T(8,128)(2,1)S(1)}, bf16[256,256]{1,0:T(8,128)(2,1)S(1)}, u32[]{:S(2)}, u32[]{:S(2)}) collective-permute-start(bf16[256,256]{1,0:T(8,128)(2,1)S(1)} %get-tuple-element.59), channel_id=1, source_target_pairs={{0,4},{2,6},{4,0},{6,2},{8,12},{10,14},{12,8},{14,10},{16,20},{18,... | collective-permute-start | bytes 393224 | tf_op jit(solution)/shard_map/ppermute | solution.py:307
  5.1 1.1 convert_element_type.39.refs_4_
  6.3 0.1 collective-permute-start
  6.3 1.6 %collective-permute-start.1 = (bf16[64,2816]{1,0:T(8,128)(2,1)S(1)}, bf16[64,2816]{1,0:T(8,128)(2,1)S(1)}, u32[]{:S(2)}, u32[]{:S(2)}) collective-permute-start(bf16[64,2816]{1,0:T(8,128)(2,1)S(1)} %convert_element_type.39.refs_4_), channel_id=1, source_target_pairs={{0,8},{2,10},{4,12},{6,14},{8,0},{10,2},{12,4},{14,6},{16,24},{18,... | collective-permute-start | bytes 1081352 | tf_op jit(solution)/shard_map/ppermute | solution.py:307
  8.0 0.2 collective-permute-start.18
  8.1 0.5 collective-permute-done.19.refs_2_
  8.6 1.7 %collective-permute-start.20 = (bf16[256,256]{1,0:T(8,128)(2,1)S(1)}, bf16[256,256]{1,0:T(8,128)(2,1)S(1)}, u32[]{:S(2)}, u32[]{:S(2)}) collective-permute-start(bf16[256,256]{1,0:T(8,128)(2,1)S(1)} %collective-permute-done.19.refs_2_), channel_id=1, source_target_pairs={{0,1},{1,0},{2,3},{3,2},{4,5},{5,4},{6,7},{7,6},{8,9},{9,8},{10,11... | collective-permute-start | bytes 393224 | tf_op jit(solution)/shard_map/ppermute | solution.py:332
  10.3 1.3 %fusion.14.refs_2_.refs_6_ = bf16[256,768]{1,0:T(8,128)(2,1)S(1)} fusion(bf16[256,2816]{1,0:T(8,128)(2,1)S(1)} %bitcast.8, bf16[256,2816]{1,0:T(8,128)(2,1)} %bitcast.11), kind=kLoop, calls=%fused_computation.20 | loop fusion | flops 1572864 | bytes 1179648 | tf_op jit(solution)/shard_map/convert_element_type | solution.py:28
  11.6 0.0 collective-permute-done.18.refs_1_
  11.6 2.7 %collective-permute-start.3 = (bf16[64,2816]{1,0:T(8,128)(2,1)S(1)}, bf16[64,2816]{1,0:T(8,128)(2,1)S(1)}, u32[]{:S(2)}, u32[]{:S(2)}) collective-permute-start(bf16[64,2816]{1,0:T(8,128)(2,1)S(1)} %convert_element_type.39.refs_4_), channel_id=1, source_target_pairs={{0,16},{2,18},{4,20},{6,22},{8,24},{10,26},{12,28},{14,30},{16,0},... | collective-permute-start | bytes 1081352 | tf_op jit(solution)/shard_map/ppermute | solution.py:307
  14.2 0.0 collective-permute-done.20.refs_3_
  14.2 1.5 %collective-permute-start.8 = (bf16[64,2816]{1,0:T(8,128)(2,1)S(1)}, bf16[64,2816]{1,0:T(8,128)(2,1)S(1)}, u32[]{:S(2)}, u32[]{:S(2)}) collective-permute-start(bf16[64,2816]{1,0:T(8,128)(2,1)S(1)} %convert_element_type.39.refs_4_), channel_id=1, source_target_pairs={{0,4},{2,6},{4,0},{6,2},{8,12},{10,14},{12,8},{14,10},{16,20},{18,... | collective-permute-start | bytes 1081352 | tf_op jit(solution)/shard_map/ppermute | solution.py:307
  15.8 0.0 collective-permute-done.21.refs_4_
  15.8 0.0 collective-permute-start.33
  15.8 0.0 collective-permute-done.refs_5_
  15.8 0.5 collective-permute-start.22
  16.3 1.8 %fusion.8 = (bf16[256,1024]{1,0:T(8,128)(2,1)S(1)}, bf16[256,1024]{1,0:T(8,128)(2,1)S(1)}) fusion(bf16[256,2816]{1,0:T(8,128)(2,1)S(1)} %bitcast.9, bf16[256,2816]{1,0:T(8,128)(2,1)} %bitcast.12), kind=kLoop, calls=%fused_computation.12 | loop fusion | flops 4194304 | bytes 3145728 | tf_op jit(solution)/shard_map/convert_element_type | solution.py:28
  18.1 2.6 %collective-permute-done.1.refs_6_ = bf16[64,2816]{1,0:T(8,128)(2,1)S(1)} collective-permute-done((bf16[64,2816]{1,0:T(8,128)(2,1)S(1)}, bf16[64,2816]{1,0:T(8,128)(2,1)S(1)}, u32[]{:S(2)}, u32[]{:S(2)}) %collective-permute-start.1) | collective-permute-done | bytes 360480 | tf_op jit(solution)/shard_map/ppermute | solution.py:307
  20.7 0.0 collective-permute-start.23
  20.7 10.4 %collective-permute-done.3.refs_8_ = bf16[64,2816]{1,0:T(8,128)(2,1)S(1)} collective-permute-done((bf16[64,2816]{1,0:T(8,128)(2,1)S(1)}, bf16[64,2816]{1,0:T(8,128)(2,1)S(1)}, u32[]{:S(2)}, u32[]{:S(2)}) %collective-permute-start.3) | collective-permute-done | bytes 360480 | tf_op jit(solution)/shard_map/ppermute | solution.py:307
  31.1 1.5 %collective-permute-start.24 = (bf16[256,1024]{1,0:T(8,128)(2,1)S(1)}, bf16[256,1024]{1,0:T(8,128)(2,1)S(1)}, u32[]{:S(2)}, u32[]{:S(2)}) collective-permute-start(bf16[256,1024]{1,0:T(8,128)(2,1)S(1)} %get-tuple-element.73.refs_0_.refs_6_), channel_id=1, source_target_pairs={{0,4},{2,6},{4,0},{6,2},{8,12},{10,14},{12,8},{14,10},{16,20},{18,... | collective-permute-start | bytes 1572872 | tf_op jit(solution)/shard_map/ppermute | solution.py:307
  32.7 0.5 collective-permute-start.34
  33.2 1.6 %collective-permute-start.29 = (bf16[256,1024]{1,0:T(8,128)(2,1)S(1)}, bf16[256,1024]{1,0:T(8,128)(2,1)S(1)}, u32[]{:S(2)}, u32[]{:S(2)}) collective-permute-start(bf16[256,1024]{1,0:T(8,128)(2,1)S(1)} %get-tuple-element.72.refs_1_.refs_6_), channel_id=1, source_target_pairs={{0,4},{2,6},{4,0},{6,2},{8,12},{10,14},{12,8},{14,10},{16,20},{18,... | collective-permute-start | bytes 1572872 | tf_op jit(solution)/shard_map/ppermute | solution.py:307
  34.8 19.6 %collective-permute-done.34.refs_8_ = bf16[256,768]{1,0:T(8,128)(2,1)S(1)} collective-permute-done((bf16[256,768]{1,0:T(8,128)(2,1)S(1)}, bf16[256,768]{1,0:T(8,128)(2,1)S(1)}, u32[]{:S(2)}, u32[]{:S(2)}) %collective-permute-start.34) | collective-permute-done | bytes 393248 | tf_op jit(solution)/shard_map/ppermute | solution.py:307
  54.4 0.5 collective-permute-start.4
  54.9 0.7 collective-permute-start.5
  55.6 8.7 %collective-permute-done.29.refs_8_ = bf16[256,1024]{1,0:T(8,128)(2,1)S(1)} collective-permute-done((bf16[256,1024]{1,0:T(8,128)(2,1)S(1)}, bf16[256,1024]{1,0:T(8,128)(2,1)S(1)}, u32[]{:S(2)}, u32[]{:S(2)}) %collective-permute-start.29) | collective-permute-done | bytes 524320 | tf_op jit(solution)/shard_map/ppermute | solution.py:307
  64.3 0.7 collective-permute-start.10
  65.0 1.8 %collective-permute-start.12 = (bf16[64,2816]{1,0:T(8,128)(2,1)S(1)}, bf16[64,2816]{1,0:T(8,128)(2,1)S(1)}, u32[]{:S(2)}, u32[]{:S(2)}) collective-permute-start(bf16[64,2816]{1,0:T(8,128)(2,1)S(1)} %collective-permute-done.3.refs_8_), channel_id=1, source_target_pairs={{0,4},{2,6},{4,0},{6,2},{8,12},{10,14},{12,8},{14,10},{16,20},{18,... | collective-permute-start | bytes 1081352 | tf_op jit(solution)/shard_map/ppermute | solution.py:307
  66.8 0.2 collective-permute-start.25
  67.0 0.3 collective-permute-start.30
  67.3 6.1 %collective-permute-done.10.refs_5_.refs_2_ = bf16[64,2816]{1,0:T(8,128)(2,1)S(1)} collective-permute-done((bf16[64,2816]{1,0:T(8,128)(2,1)S(1)}, bf16[64,2816]{1,0:T(8,128)(2,1)S(1)}, u32[]{:S(2)}, u32[]{:S(2)}) %collective-permute-start.10) | collective-permute-done | bytes 360480 | tf_op jit(solution)/shard_map/ppermute | solution.py:307
  73.4 1.5 %collective-permute-start.15 = (bf16[64,2816]{1,0:T(8,128)(2,1)S(1)}, bf16[64,2816]{1,0:T(8,128)(2,1)S(1)}, u32[]{:S(2)}, u32[]{:S(2)}) collective-permute-start(bf16[64,2816]{1,0:T(8,128)(2,1)S(1)} %collective-permute-done.5.refs_10_), channel_id=1, source_target_pairs={{0,4},{2,6},{4,0},{6,2},{8,12},{10,14},{12,8},{14,10},{16,20},{18,... | collective-permute-start | bytes 1081352 | tf_op jit(solution)/shard_map/ppermute | solution.py:307
  74.9 0.6 shard_map.121
  75.6 0.8 collective-permute-done.12.refs_7_.refs_4_
  76.4 1.3 %collective-permute-start.36 = (bf16[128,768]{1,0:T(8,128)(2,1)S(1)}, bf16[128,768]{1,0:T(8,128)(2,1)S(1)}, u32[]{:S(2)}, u32[]{:S(2)}) collective-permute-start(bf16[128,768]{1,0:T(8,128)(2,1)S(1)} %get-tuple-element.67), channel_id=1, source_target_pairs={{0,8},{2,10},{4,12},{6,14},{8,0},{10,2},{12,4},{14,6},{16,24},{18,... | collective-permute-start | bytes 589832 | tf_op jit(solution)/shard_map/ppermute | solution.py:307
  77.7 5.3 %collective-permute-done.36.side.refs_7_ = bf16[128,768]{1,0:T(8,128)(2,1)S(1)} collective-permute-done((bf16[128,768]{1,0:T(8,128)(2,1)S(1)}, bf16[128,768]{1,0:T(8,128)(2,1)S(1)}, u32[]{:S(2)}, u32[]{:S(2)}) %collective-permute-start.36) | collective-permute-done | bytes 196640 | tf_op jit(solution)/shard_map/ppermute | solution.py:307
  82.9 0.5 collective-permute-start.13
  83.5 0.7 shard_map.117
  84.2 1.2 collective-permute-start.26
  85.4 0.8 shard_map.119
  86.2 0.9 collective-permute-start.31
  87.2 0.6 shard_map.110
  87.7 1.8 %shard_map.111 = (f32[256,256]{1,0:T(8,128)S(1)}, f32[256,256]{1,0:T(8,128)S(1)}, f32[256,2816]{1,0:T(8,128)S(1)}) custom-call(s32[1]{0:T(128)} %bitcast.me_ref, s32[1]{0:T(128)} %bitcast.1.rep_ref, bf16[1024,256]{1,0:T(8,128)(2,1)S(1)} %get-tuple-element.42.refs_0_, bf16[1024,256]{1,0:T(8,128)(2,1)S(1)} %get-tuple-element.43.refs_1_, ...), custom_call_target="tpu_custom_call" | custom-call | flops 1476395008 | bytes 7995400 | tf_op jit(solution)/shard_map/pallas_call | solution.py:281
  89.5 4.0 %collective-permute-done.26.side.refs_1_ = bf16[128,1024]{1,0:T(8,128)(2,1)S(1)} collective-permute-done((bf16[128,1024]{1,0:T(8,128)(2,1)S(1)}, bf16[128,1024]{1,0:T(8,128)(2,1)S(1)}, u32[]{:S(2)}, u32[]{:S(2)}) %collective-permute-start.26) | collective-permute-done | bytes 262176 | tf_op jit(solution)/shard_map/ppermute | solution.py:307
  93.5 0.5 collective-permute-start.7
  94.0 4.1 %collective-permute-done.31.side.refs_4_ = bf16[128,1024]{1,0:T(8,128)(2,1)S(1)} collective-permute-done((bf16[128,1024]{1,0:T(8,128)(2,1)S(1)}, bf16[128,1024]{1,0:T(8,128)(2,1)S(1)}, u32[]{:S(2)}, u32[]{:S(2)}) %collective-permute-start.31) | collective-permute-done | bytes 262176 | tf_op jit(solution)/shard_map/ppermute | solution.py:307
  98.1 2.8 %collective-permute-start.37 = (bf16[64,768]{1,0:T(8,128)(2,1)S(1)}, bf16[64,768]{1,0:T(8,128)(2,1)S(1)}, u32[]{:S(2)}, u32[]{:S(2)}) collective-permute-start(bf16[64,768]{1,0:T(8,128)(2,1)S(1)} %shard_map.122), channel_id=1, source_target_pairs={{0,16},{2,18},{4,20},{6,22},{8,24},{10,26},{12,28},{14,30},{16,0},... | collective-permute-start | bytes 294920 | tf_op jit(solution)/shard_map/ppermute | solution.py:307
  101.0 0.2 collective-permute-start.27
  101.2 2.8 %collective-permute-start.32 = (bf16[64,1024]{1,0:T(8,128)(2,1)S(1)}, bf16[64,1024]{1,0:T(8,128)(2,1)S(1)}, u32[]{:S(2)}, u32[]{:S(2)}) collective-permute-start(bf16[64,1024]{1,0:T(8,128)(2,1)S(1)} %shard_map.120), channel_id=1, source_target_pairs={{0,16},{2,18},{4,20},{6,22},{8,24},{10,26},{12,28},{14,30},{16,0},... | collective-permute-start | bytes 393224 | tf_op jit(solution)/shard_map/ppermute | solution.py:307
  104.0 0.7 shard_map.112
  104.7 0.0 copy-start.1
  104.7 0.6 collective-permute-start.14
  105.3 0.4 shard_map.113
  105.7 5.9 %collective-permute-done.37.refs_8_ = bf16[64,768]{1,0:T(8,128)(2,1)S(1)} collective-permute-done((bf16[64,768]{1,0:T(8,128)(2,1)S(1)}, bf16[64,768]{1,0:T(8,128)(2,1)S(1)}, u32[]{:S(2)}, u32[]{:S(2)}) %collective-permute-start.37) | collective-permute-done | bytes 98336 | tf_op jit(solution)/shard_map/ppermute | solution.py:307
  111.6 0.4 collective-permute-start.17
  112.0 1.1 shard_map.115
  113.1 1.3 %collective-permute-done.27.refs_2_ = bf16[64,1024]{1,0:T(8,128)(2,1)S(1)} collective-permute-done((bf16[64,1024]{1,0:T(8,128)(2,1)S(1)}, bf16[64,1024]{1,0:T(8,128)(2,1)S(1)}, u32[]{:S(2)}, u32[]{:S(2)}) %collective-permute-start.27) | collective-permute-done | bytes 131104 | tf_op jit(solution)/shard_map/ppermute | solution.py:307
  114.4 2.0 %collective-permute-done.32.refs_5_ = bf16[64,1024]{1,0:T(8,128)(2,1)S(1)} collective-permute-done((bf16[64,1024]{1,0:T(8,128)(2,1)S(1)}, bf16[64,1024]{1,0:T(8,128)(2,1)S(1)}, u32[]{:S(2)}, u32[]{:S(2)}) %collective-permute-start.32) | collective-permute-done | bytes 131104 | tf_op jit(solution)/shard_map/ppermute | solution.py:307
  116.5 1.7 %shard_map.123 = (f32[64,2816]{1,0:T(8,128)}, f32[64,2816]{1,0:T(8,128)}, f32[64,2816]{1,0:T(8,128)}) custom-call(f32[64,1024]{1,0:T(8,128)S(1)} %get-tuple-element.60.refs_0_, bf16[128,1024]{1,0:T(8,128)(2,1)S(1)} %collective-permute-done.26.side.refs_1_, bf16[64,1024]{1,0:T(8,128)(2,1)S(1)} %collective-permute-done.27.refs_2_, ...), custom_call_target="tpu_custom_call" | custom-call | bytes 6127616 | tf_op jit(solution)/shard_map/pallas_call | solution.py:281
  118.1 2.1 %shard_map.116 = (bf16[256,2816]{1,0:T(8,128)(2,1)}, bf16[256,2816]{1,0:T(8,128)(2,1)}) custom-call(bf16[256,512]{1,0:T(8,128)(2,1)S(1)} %get-tuple-element.53.left, f32[256,2816]{1,0:T(8,128)S(1)} %get-tuple-element.54.gate_slope, f32[256,2816]{1,0:T(8,128)S(1)} %get-tuple-element.55.up_slope, f32[256,2816]{1,0:T(8,128)S(1)} %get-tuple-element.56.early, ...), custom_call_target="tpu_custom_call" | custom-call | flops 738197504 | bytes 14680064 | tf_op jit(solution)/shard_map/pallas_call | solution.py:281
  120.3 0.9 shard_map.114
  (42 shorter events, 0.2 us)
Async XLA Ops:
  0.6 9.7 %copy-start = (bf16[2,128,2816]{2,1,0:T(8,128)(2,1)S(1)}, bf16[2,128,2816]{2,1,0:T(8,128)(2,1)}, u32[]{:S(2)}) copy-start(bf16[2,128,2816]{2,1,0:T(8,128)(2,1)} %param.7) | copy-start | bytes 4325380
  0.6 1.2 copy-start.5
  2.0 6.6 %collective-permute-start.19 = (bf16[256,256]{1,0:T(8,128)(2,1)S(1)}, bf16[256,256]{1,0:T(8,128)(2,1)S(1)}, u32[]{:S(2)}, u32[]{:S(2)}) collective-permute-start(bf16[256,256]{1,0:T(8,128)(2,1)S(1)} %get-tuple-element.59), channel_id=1, source_target_pairs={{0,4},{2,6},{4,0},{6,2},{8,12},{10,14},{12,8},{14,10},{16,20},{18,... | collective-permute-start | bytes 393224 | tf_op jit(solution)/shard_map/ppermute | solution.py:307
  6.3 9.5 %collective-permute-start = (bf16[64,2816]{1,0:T(8,128)(2,1)S(1)}, bf16[64,2816]{1,0:T(8,128)(2,1)S(1)}, u32[]{:S(2)}, u32[]{:S(2)}) collective-permute-start(bf16[64,2816]{1,0:T(8,128)(2,1)S(1)} %convert_element_type.39.refs_4_), channel_id=1, source_target_pairs={{0,2},{2,0},{4,6},{6,4},{8,10},{10,8},{12,14},{14,12},{16,18},{18,... | collective-permute-start | bytes 1081352 | tf_op jit(solution)/shard_map/ppermute | solution.py:307
  6.3 14.4 %collective-permute-start.1 = (bf16[64,2816]{1,0:T(8,128)(2,1)S(1)}, bf16[64,2816]{1,0:T(8,128)(2,1)S(1)}, u32[]{:S(2)}, u32[]{:S(2)}) collective-permute-start(bf16[64,2816]{1,0:T(8,128)(2,1)S(1)} %convert_element_type.39.refs_4_), channel_id=1, source_target_pairs={{0,8},{2,10},{4,12},{6,14},{8,0},{10,2},{12,4},{14,6},{16,24},{18,... | collective-permute-start | bytes 1081352 | tf_op jit(solution)/shard_map/ppermute | solution.py:307
  8.0 3.6 %collective-permute-start.18 = (bf16[256,256]{1,0:T(8,128)(2,1)S(1)}, bf16[256,256]{1,0:T(8,128)(2,1)S(1)}, u32[]{:S(2)}, u32[]{:S(2)}) collective-permute-start(bf16[256,256]{1,0:T(8,128)(2,1)S(1)} %get-tuple-element.40.refs_4_), channel_id=1, source_target_pairs={{0,2},{2,0},{4,6},{6,4},{8,10},{10,8},{12,14},{14,12},{16,18},{18,... | collective-permute-start | bytes 393224 | tf_op jit(solution)/shard_map/ppermute | solution.py:307
  8.6 5.6 %collective-permute-start.20 = (bf16[256,256]{1,0:T(8,128)(2,1)S(1)}, bf16[256,256]{1,0:T(8,128)(2,1)S(1)}, u32[]{:S(2)}, u32[]{:S(2)}) collective-permute-start(bf16[256,256]{1,0:T(8,128)(2,1)S(1)} %collective-permute-done.19.refs_2_), channel_id=1, source_target_pairs={{0,1},{1,0},{2,3},{3,2},{4,5},{5,4},{6,7},{7,6},{8,9},{9,8},{10,11... | collective-permute-start | bytes 393224 | tf_op jit(solution)/shard_map/ppermute | solution.py:332
  10.3 5.5 %collective-permute-start.21 = (bf16[256,256]{1,0:T(8,128)(2,1)S(1)}, bf16[256,256]{1,0:T(8,128)(2,1)S(1)}, u32[]{:S(2)}, u32[]{:S(2)}) collective-permute-start(bf16[256,256]{1,0:T(8,128)(2,1)S(1)} %collective-permute-done.19.refs_2_), channel_id=1, source_target_pairs={{0,2},{2,0},{4,6},{6,4},{8,10},{10,8},{12,14},{14,12},{16,18},{18,... | collective-permute-start | bytes 393224 | tf_op jit(solution)/shard_map/ppermute | solution.py:307
  11.6 19.6 %collective-permute-start.3 = (bf16[64,2816]{1,0:T(8,128)(2,1)S(1)}, bf16[64,2816]{1,0:T(8,128)(2,1)S(1)}, u32[]{:S(2)}, u32[]{:S(2)}) collective-permute-start(bf16[64,2816]{1,0:T(8,128)(2,1)S(1)} %convert_element_type.39.refs_4_), channel_id=1, source_target_pairs={{0,16},{2,18},{4,20},{6,22},{8,24},{10,26},{12,28},{14,30},{16,0},... | collective-permute-start | bytes 1081352 | tf_op jit(solution)/shard_map/ppermute | solution.py:307
  14.2 18.4 %collective-permute-start.8 = (bf16[64,2816]{1,0:T(8,128)(2,1)S(1)}, bf16[64,2816]{1,0:T(8,128)(2,1)S(1)}, u32[]{:S(2)}, u32[]{:S(2)}) collective-permute-start(bf16[64,2816]{1,0:T(8,128)(2,1)S(1)} %convert_element_type.39.refs_4_), channel_id=1, source_target_pairs={{0,4},{2,6},{4,0},{6,2},{8,12},{10,14},{12,8},{14,10},{16,20},{18,... | collective-permute-start | bytes 1081352 | tf_op jit(solution)/shard_map/ppermute | solution.py:307
  15.8 17.4 %collective-permute-start.33 = (bf16[256,768]{1,0:T(8,128)(2,1)S(1)}, bf16[256,768]{1,0:T(8,128)(2,1)S(1)}, u32[]{:S(2)}, u32[]{:S(2)}) collective-permute-start(bf16[256,768]{1,0:T(8,128)(2,1)S(1)} %fusion.14.refs_2_.refs_6_), channel_id=1, source_target_pairs={{0,2},{2,0},{4,6},{6,4},{8,10},{10,8},{12,14},{14,12},{16,18},{18,... | collective-permute-start | bytes 1179656 | tf_op jit(solution)/shard_map/ppermute | solution.py:307
  15.8 17.4 %collective-permute-start.22 = (bf16[256,256]{1,0:T(8,128)(2,1)S(1)}, bf16[256,256]{1,0:T(8,128)(2,1)S(1)}, u32[]{:S(2)}, u32[]{:S(2)}) collective-permute-start(bf16[256,256]{1,0:T(8,128)(2,1)S(1)} %collective-permute-done.20.refs_3_), channel_id=1, source_target_pairs={{0,2},{2,0},{4,6},{6,4},{8,10},{10,8},{12,14},{14,12},{16,18},{18,... | collective-permute-start | bytes 393224 | tf_op jit(solution)/shard_map/ppermute | solution.py:307
  20.7 33.6 %collective-permute-start.23 = (bf16[256,1024]{1,0:T(8,128)(2,1)S(1)}, bf16[256,1024]{1,0:T(8,128)(2,1)S(1)}, u32[]{:S(2)}, u32[]{:S(2)}) collective-permute-start(bf16[256,1024]{1,0:T(8,128)(2,1)S(1)} %get-tuple-element.73.refs_0_.refs_6_), channel_id=1, source_target_pairs={{0,2},{2,0},{4,6},{6,4},{8,10},{10,8},{12,14},{14,12},{16,18},{18,... | collective-permute-start | bytes 1572872 | tf_op jit(solution)/shard_map/ppermute | solution.py:307
  31.1 23.7 %collective-permute-start.24 = (bf16[256,1024]{1,0:T(8,128)(2,1)S(1)}, bf16[256,1024]{1,0:T(8,128)(2,1)S(1)}, u32[]{:S(2)}, u32[]{:S(2)}) collective-permute-start(bf16[256,1024]{1,0:T(8,128)(2,1)S(1)} %get-tuple-element.73.refs_0_.refs_6_), channel_id=1, source_target_pairs={{0,4},{2,6},{4,0},{6,2},{8,12},{10,14},{12,8},{14,10},{16,20},{18,... | collective-permute-start | bytes 1572872 | tf_op jit(solution)/shard_map/ppermute | solution.py:307
  32.7 21.7 %collective-permute-start.34 = (bf16[256,768]{1,0:T(8,128)(2,1)S(1)}, bf16[256,768]{1,0:T(8,128)(2,1)S(1)}, u32[]{:S(2)}, u32[]{:S(2)}) collective-permute-start(bf16[256,768]{1,0:T(8,128)(2,1)S(1)} %fusion.14.refs_2_.refs_6_), channel_id=1, source_target_pairs={{0,4},{2,6},{4,0},{6,2},{8,12},{10,14},{12,8},{14,10},{16,20},{18,... | collective-permute-start | bytes 1179656 | tf_op jit(solution)/shard_map/ppermute | solution.py:307
  33.2 22.5 %collective-permute-start.28 = (bf16[256,1024]{1,0:T(8,128)(2,1)S(1)}, bf16[256,1024]{1,0:T(8,128)(2,1)S(1)}, u32[]{:S(2)}, u32[]{:S(2)}) collective-permute-start(bf16[256,1024]{1,0:T(8,128)(2,1)S(1)} %get-tuple-element.72.refs_1_.refs_6_), channel_id=1, source_target_pairs={{0,2},{2,0},{4,6},{6,4},{8,10},{10,8},{12,14},{14,12},{16,18},{18,... | collective-permute-start | bytes 1572872 | tf_op jit(solution)/shard_map/ppermute | solution.py:307
  33.2 31.1 %collective-permute-start.29 = (bf16[256,1024]{1,0:T(8,128)(2,1)S(1)}, bf16[256,1024]{1,0:T(8,128)(2,1)S(1)}, u32[]{:S(2)}, u32[]{:S(2)}) collective-permute-start(bf16[256,1024]{1,0:T(8,128)(2,1)S(1)} %get-tuple-element.72.refs_1_.refs_6_), channel_id=1, source_target_pairs={{0,4},{2,6},{4,0},{6,2},{8,12},{10,14},{12,8},{14,10},{16,20},{18,... | collective-permute-start | bytes 1572872 | tf_op jit(solution)/shard_map/ppermute | solution.py:307
  54.4 10.7 %collective-permute-start.2 = (bf16[64,2816]{1,0:T(8,128)(2,1)S(1)}, bf16[64,2816]{1,0:T(8,128)(2,1)S(1)}, u32[]{:S(2)}, u32[]{:S(2)}) collective-permute-start(bf16[64,2816]{1,0:T(8,128)(2,1)S(1)} %collective-permute-done.1.refs_6_), channel_id=1, source_target_pairs={{0,2},{2,0},{4,6},{6,4},{8,10},{10,8},{12,14},{14,12},{16,18},{18,... | collective-permute-start | bytes 1081352 | tf_op jit(solution)/shard_map/ppermute | solution.py:307
  54.4 10.7 %collective-permute-start.4 = (bf16[64,2816]{1,0:T(8,128)(2,1)S(1)}, bf16[64,2816]{1,0:T(8,128)(2,1)S(1)}, u32[]{:S(2)}, u32[]{:S(2)}) collective-permute-start(bf16[64,2816]{1,0:T(8,128)(2,1)S(1)} %collective-permute-done.3.refs_8_), channel_id=1, source_target_pairs={{0,2},{2,0},{4,6},{6,4},{8,10},{10,8},{12,14},{14,12},{16,18},{18,... | collective-permute-start | bytes 1081352 | tf_op jit(solution)/shard_map/ppermute | solution.py:307
  54.9 11.9 %collective-permute-start.5 = (bf16[64,2816]{1,0:T(8,128)(2,1)S(1)}, bf16[64,2816]{1,0:T(8,128)(2,1)S(1)}, u32[]{:S(2)}, u32[]{:S(2)}) collective-permute-start(bf16[64,2816]{1,0:T(8,128)(2,1)S(1)} %collective-permute-done.3.refs_8_), channel_id=1, source_target_pairs={{0,8},{2,10},{4,12},{6,14},{8,0},{10,2},{12,4},{14,6},{16,24},{18,... | collective-permute-start | bytes 1081352 | tf_op jit(solution)/shard_map/ppermute | solution.py:307
  55.6 11.3 %collective-permute-start.9 = (bf16[64,2816]{1,0:T(8,128)(2,1)S(1)}, bf16[64,2816]{1,0:T(8,128)(2,1)S(1)}, u32[]{:S(2)}, u32[]{:S(2)}) collective-permute-start(bf16[64,2816]{1,0:T(8,128)(2,1)S(1)} %collective-permute-done.8.refs_3_.refs_0_), channel_id=1, source_target_pairs={{0,2},{2,0},{4,6},{6,4},{8,10},{10,8},{12,14},{14,12},{16,18},{18,... | collective-permute-start | bytes 1081352 | tf_op jit(solution)/shard_map/ppermute | solution.py:307
  64.3 9.1 %collective-permute-start.10 = (bf16[64,2816]{1,0:T(8,128)(2,1)S(1)}, bf16[64,2816]{1,0:T(8,128)(2,1)S(1)}, u32[]{:S(2)}, u32[]{:S(2)}) collective-permute-start(bf16[64,2816]{1,0:T(8,128)(2,1)S(1)} %collective-permute-done.8.refs_3_.refs_0_), channel_id=1, source_target_pairs={{0,8},{2,10},{4,12},{6,14},{8,0},{10,2},{12,4},{14,6},{16,24},{18,... | collective-permute-start | bytes 1081352 | tf_op jit(solution)/shard_map/ppermute | solution.py:307
  65.0 9.9 %collective-permute-start.35 = (bf16[256,768]{1,0:T(8,128)(2,1)S(1)}, bf16[256,768]{1,0:T(8,128)(2,1)S(1)}, u32[]{:S(2)}, u32[]{:S(2)}) collective-permute-start(bf16[256,768]{1,0:T(8,128)(2,1)S(1)} %collective-permute-done.34.refs_8_), channel_id=1, source_target_pairs={{0,2},{2,0},{4,6},{6,4},{8,10},{10,8},{12,14},{14,12},{16,18},{18,... | collective-permute-start | bytes 1179656 | tf_op jit(solution)/shard_map/ppermute | solution.py:307
  65.0 11.3 %collective-permute-start.12 = (bf16[64,2816]{1,0:T(8,128)(2,1)S(1)}, bf16[64,2816]{1,0:T(8,128)(2,1)S(1)}, u32[]{:S(2)}, u32[]{:S(2)}) collective-permute-start(bf16[64,2816]{1,0:T(8,128)(2,1)S(1)} %collective-permute-done.3.refs_8_), channel_id=1, source_target_pairs={{0,4},{2,6},{4,0},{6,2},{8,12},{10,14},{12,8},{14,10},{16,20},{18,... | collective-permute-start | bytes 1081352 | tf_op jit(solution)/shard_map/ppermute | solution.py:307
  66.8 16.2 %collective-permute-start.25 = (bf16[256,1024]{1,0:T(8,128)(2,1)S(1)}, bf16[256,1024]{1,0:T(8,128)(2,1)S(1)}, u32[]{:S(2)}, u32[]{:S(2)}) collective-permute-start(bf16[256,1024]{1,0:T(8,128)(2,1)S(1)} %collective-permute-done.24.refs_8_), channel_id=1, source_target_pairs={{0,2},{2,0},{4,6},{6,4},{8,10},{10,8},{12,14},{14,12},{16,18},{18,... | collective-permute-start | bytes 1572872 | tf_op jit(solution)/shard_map/ppermute | solution.py:307
  67.0 17.3 %collective-permute-start.30 = (bf16[256,1024]{1,0:T(8,128)(2,1)S(1)}, bf16[256,1024]{1,0:T(8,128)(2,1)S(1)}, u32[]{:S(2)}, u32[]{:S(2)}) collective-permute-start(bf16[256,1024]{1,0:T(8,128)(2,1)S(1)} %collective-permute-done.29.refs_8_), channel_id=1, source_target_pairs={{0,2},{2,0},{4,6},{6,4},{8,10},{10,8},{12,14},{14,12},{16,18},{18,... | collective-permute-start | bytes 1572872 | tf_op jit(solution)/shard_map/ppermute | solution.py:307
  73.4 12.0 %collective-permute-start.15 = (bf16[64,2816]{1,0:T(8,128)(2,1)S(1)}, bf16[64,2816]{1,0:T(8,128)(2,1)S(1)}, u32[]{:S(2)}, u32[]{:S(2)}) collective-permute-start(bf16[64,2816]{1,0:T(8,128)(2,1)S(1)} %collective-permute-done.5.refs_10_), channel_id=1, source_target_pairs={{0,4},{2,6},{4,0},{6,2},{8,12},{10,14},{12,8},{14,10},{16,20},{18,... | collective-permute-start | bytes 1081352 | tf_op jit(solution)/shard_map/ppermute | solution.py:307
  74.9 11.3 %collective-permute-start.6 = (bf16[64,2816]{1,0:T(8,128)(2,1)S(1)}, bf16[64,2816]{1,0:T(8,128)(2,1)S(1)}, u32[]{:S(2)}, u32[]{:S(2)}) collective-permute-start(bf16[64,2816]{1,0:T(8,128)(2,1)S(1)} %collective-permute-done.5.refs_10_), channel_id=1, source_target_pairs={{0,2},{2,0},{4,6},{6,4},{8,10},{10,8},{12,14},{14,12},{16,18},{18,... | collective-permute-start | bytes 1081352 | tf_op jit(solution)/shard_map/ppermute | solution.py:307
  76.4 6.6 %collective-permute-start.36 = (bf16[128,768]{1,0:T(8,128)(2,1)S(1)}, bf16[128,768]{1,0:T(8,128)(2,1)S(1)}, u32[]{:S(2)}, u32[]{:S(2)}) collective-permute-start(bf16[128,768]{1,0:T(8,128)(2,1)S(1)} %get-tuple-element.67), channel_id=1, source_target_pairs={{0,8},{2,10},{4,12},{6,14},{8,0},{10,2},{12,4},{14,6},{16,24},{18,... | collective-permute-start | bytes 589832 | tf_op jit(solution)/shard_map/ppermute | solution.py:307
  82.9 18.0 %collective-permute-start.11 = (bf16[64,2816]{1,0:T(8,128)(2,1)S(1)}, bf16[64,2816]{1,0:T(8,128)(2,1)S(1)}, u32[]{:S(2)}, u32[]{:S(2)}) collective-permute-start(bf16[64,2816]{1,0:T(8,128)(2,1)S(1)} %collective-permute-done.10.refs_5_.refs_2_), channel_id=1, source_target_pairs={{0,2},{2,0},{4,6},{6,4},{8,10},{10,8},{12,14},{14,12},{16,18},{18,... | collective-permute-start | bytes 1081352 | tf_op jit(solution)/shard_map/ppermute | solution.py:307
  82.9 18.2 %collective-permute-start.13 = (bf16[64,2816]{1,0:T(8,128)(2,1)S(1)}, bf16[64,2816]{1,0:T(8,128)(2,1)S(1)}, u32[]{:S(2)}, u32[]{:S(2)}) collective-permute-start(bf16[64,2816]{1,0:T(8,128)(2,1)S(1)} %collective-permute-done.12.refs_7_.refs_4_), channel_id=1, source_target_pairs={{0,2},{2,0},{4,6},{6,4},{8,10},{10,8},{12,14},{14,12},{16,18},{18,... | collective-permute-start | bytes 1081352 | tf_op jit(solution)/shard_map/ppermute | solution.py:307
  84.2 9.2 %collective-permute-start.26 = (bf16[128,1024]{1,0:T(8,128)(2,1)S(1)}, bf16[128,1024]{1,0:T(8,128)(2,1)S(1)}, u32[]{:S(2)}, u32[]{:S(2)}) collective-permute-start(bf16[128,1024]{1,0:T(8,128)(2,1)S(1)} %get-tuple-element.61), channel_id=1, source_target_pairs={{0,8},{2,10},{4,12},{6,14},{8,0},{10,2},{12,4},{14,6},{16,24},{18,... | collective-permute-start | bytes 786440 | tf_op jit(solution)/shard_map/ppermute | solution.py:307
  85.4 19.3 %collective-permute-start.16 = (bf16[64,2816]{1,0:T(8,128)(2,1)S(1)}, bf16[64,2816]{1,0:T(8,128)(2,1)S(1)}, u32[]{:S(2)}, u32[]{:S(2)}) collective-permute-start(bf16[64,2816]{1,0:T(8,128)(2,1)S(1)} %collective-permute-done.15.refs_4_.refs_6_), channel_id=1, source_target_pairs={{0,2},{2,0},{4,6},{6,4},{8,10},{10,8},{12,14},{14,12},{16,18},{18,... | collective-permute-start | bytes 1081352 | tf_op jit(solution)/shard_map/ppermute | solution.py:307
  86.2 11.9 %collective-permute-start.31 = (bf16[128,1024]{1,0:T(8,128)(2,1)S(1)}, bf16[128,1024]{1,0:T(8,128)(2,1)S(1)}, u32[]{:S(2)}, u32[]{:S(2)}) collective-permute-start(bf16[128,1024]{1,0:T(8,128)(2,1)S(1)} %get-tuple-element.64), channel_id=1, source_target_pairs={{0,8},{2,10},{4,12},{6,14},{8,0},{10,2},{12,4},{14,6},{16,24},{18,... | collective-permute-start | bytes 786440 | tf_op jit(solution)/shard_map/ppermute | solution.py:307
  93.5 26.8 %collective-permute-start.7 = (f32[256,256]{1,0:T(8,128)S(1)}, f32[256,256]{1,0:T(8,128)S(1)}, u32[]{:S(2)}, u32[]{:S(2)}) collective-permute-start(f32[256,256]{1,0:T(8,128)S(1)} %get-tuple-element.47), channel_id=1, source_target_pairs={{0,1},{1,0},{2,3},{3,2},{4,5},{5,4},{6,7},{7,6},{8,9},{9,8},{10,11... | collective-permute-start | bytes 786440 | tf_op jit(solution)/shard_map/ppermute | solution.py:332
  98.1 13.5 %collective-permute-start.37 = (bf16[64,768]{1,0:T(8,128)(2,1)S(1)}, bf16[64,768]{1,0:T(8,128)(2,1)S(1)}, u32[]{:S(2)}, u32[]{:S(2)}) collective-permute-start(bf16[64,768]{1,0:T(8,128)(2,1)S(1)} %shard_map.122), channel_id=1, source_target_pairs={{0,16},{2,18},{4,20},{6,22},{8,24},{10,26},{12,28},{14,30},{16,0},... | collective-permute-start | bytes 294920 | tf_op jit(solution)/shard_map/ppermute | solution.py:307
  101.0 13.5 %collective-permute-start.27 = (bf16[64,1024]{1,0:T(8,128)(2,1)S(1)}, bf16[64,1024]{1,0:T(8,128)(2,1)S(1)}, u32[]{:S(2)}, u32[]{:S(2)}) collective-permute-start(bf16[64,1024]{1,0:T(8,128)(2,1)S(1)} %shard_map.118), channel_id=1, source_target_pairs={{0,16},{2,18},{4,20},{6,22},{8,24},{10,26},{12,28},{14,30},{16,0},... | collective-permute-start | bytes 393224 | tf_op jit(solution)/shard_map/ppermute | solution.py:307
  101.2 15.3 %collective-permute-start.32 = (bf16[64,1024]{1,0:T(8,128)(2,1)S(1)}, bf16[64,1024]{1,0:T(8,128)(2,1)S(1)}, u32[]{:S(2)}, u32[]{:S(2)}) collective-permute-start(bf16[64,1024]{1,0:T(8,128)(2,1)S(1)} %shard_map.120), channel_id=1, source_target_pairs={{0,16},{2,18},{4,20},{6,22},{8,24},{10,26},{12,28},{14,30},{16,0},... | collective-permute-start | bytes 393224 | tf_op jit(solution)/shard_map/ppermute | solution.py:307
  104.7 7.3 %copy-start.1 = (bf16[2,128,2816]{2,1,0:T(8,128)(2,1)S(1)}, bf16[2,128,2816]{2,1,0:T(8,128)(2,1)}, u32[]{:S(2)}) copy-start(bf16[2,128,2816]{2,1,0:T(8,128)(2,1)} %param.6) | copy-start | bytes 4325380
  104.7 15.5 %collective-permute-start.14 = (f32[128,256]{1,0:T(8,128)S(1)}, f32[128,256]{1,0:T(8,128)S(1)}, u32[]{:S(2)}, u32[]{:S(2)}) collective-permute-start(f32[128,256]{1,0:T(8,128)S(1)} %get-tuple-element.49), channel_id=1, source_target_pairs={{0,1},{1,0},{2,3},{3,2},{4,5},{5,4},{6,7},{7,6},{8,9},{9,8},{10,11... | collective-permute-start | bytes 393224 | tf_op jit(solution)/shard_map/ppermute | solution.py:332
  111.6 4.8 %copy-start.2 = (f32[64,2816]{1,0:T(8,128)S(1)}, f32[64,2816]{1,0:T(8,128)}, u32[]{:S(2)}) copy-start(f32[64,2816]{1,0:T(8,128)} %refs_9_.1) | copy-start | bytes 2162692
  111.6 4.8 %copy-start.3 = (f32[64,2816]{1,0:T(8,128)S(1)}, f32[64,2816]{1,0:T(8,128)}, u32[]{:S(2)}) copy-start(f32[64,2816]{1,0:T(8,128)} %refs_10_.1) | copy-start | bytes 2162692
  111.6 4.8 %copy-start.4 = (f32[64,2816]{1,0:T(8,128)S(1)}, f32[64,2816]{1,0:T(8,128)}, u32[]{:S(2)}) copy-start(f32[64,2816]{1,0:T(8,128)} %refs_11_.1) | copy-start | bytes 2162692
  111.6 8.7 %collective-permute-start.17 = (f32[128,256]{1,0:T(8,128)S(1)}, f32[128,256]{1,0:T(8,128)S(1)}, u32[]{:S(2)}, u32[]{:S(2)}) collective-permute-start(f32[128,256]{1,0:T(8,128)S(1)} %get-tuple-element.52), channel_id=1, source_target_pairs={{0,1},{1,0},{2,3},{3,2},{4,5},{5,4},{6,7},{7,6},{8,9},{9,8},{10,11... | collective-permute-start | bytes 393224 | tf_op jit(solution)/shard_map/ppermute | solution.py:332

commit v4 on v3

--- a/solution.py
+++ b/solution.py
@@ -19,7 +19,8 @@
 def adamw(main_grad, master, moment_one, moment_two):
     first = 0.9 * moment_one + 0.1 * main_grad
     second = 0.95 * moment_two + 0.05 * main_grad * main_grad
-    update = first / (1.0 - first_power) / (jnp.sqrt(second / (1.0 - second_power)) + 1e-08)
+    scaled = first * (1.0 / (1.0 - first_power))
+    update = scaled / (jnp.sqrt(second * (1.0 / (1.0 - second_power))) + 1e-08)
     return master - 0.003 * (update + 0.1 * master), first, second
 
 
@@ -97,9 +98,9 @@
         body(slice(start, start + TILE))
 
 
-def grads_kernel(rows, rep_ref, *refs):
+def grads_kernel(rows, final, rep_ref, *refs):
     own, near, far, far_x, cross, cross_x = refs[:6]
-    rights, (mine_out, side, across, left) = refs[6:10], refs[10:]
+    rights, (mine_out, side, across, *third), left = refs[6:10], refs[10:-1], refs[-1]
     count = own.shape[1]
     half = 2 * rows
     mine = pl.ds(pl.multiple_of(rep_ref[0] * half, half), half)
@@ -113,10 +114,14 @@
 
     def body(at):
         total = jnp.dot(left[...], stacked(rights, at), preferred_element_type=jnp.float32)
-        mine_out[:, at] = total[:rows]
-        side[:rows, at] = total[rows : 2 * rows].astype(side.dtype)
-        side[rows:, at] = total[3 * rows :].astype(side.dtype)
-        across[:, at] = total[2 * rows : 3 * rows]
+        parts = [total[s * rows : (s + 1) * rows] for s in range(4)]
+        mine_out[:, at] = parts[0]
+        side[:rows, at] = parts[1].astype(side.dtype)
+        across[:, at] = parts[2].astype(across.dtype)
+        if final:
+            third[0][:, at] = parts[3].astype(side.dtype)
+        else:
+            side[rows:, at] = parts[3].astype(side.dtype)
 
     each_tile(rights[0].shape[1], body)
 
@@ -246,25 +251,29 @@
                 block = me ^ (4 * (first + s) + 2 * far + core)
                 start = pl.multiple_of((block % (2 * zs)) * rows, rows)
                 at = (2 * s + core) * rows
-                placed[pl.ds(start, rows), :] = value[at : at + rows, :]
+                placed[pl.ds(start, rows), :] = value[at : at + rows, :].astype(placed.dtype)
 
     place(keep[...] + got[...], 0, 0)
     place(middle[...] + got_middle[...], 0, 1)
     place(last[...] + got_last[...], 1, 1)
-    out[...] = placed[...].T.astype(out.dtype)
-
-
-def adamw_kernel(total, pieces, *refs):
-    parts, states = refs[: 3 * pieces], refs[3 * pieces : 3 * pieces + 3]
-    outs, values, sems = refs[3 * pieces + 3 :][:3], refs[3 * pieces + 6 : -1], refs[-1]
+    out[...] = placed[...].T
+
+
+def adamw_kernel(total, counts, *refs):
+    given = sum(counts)
+    parts, states = refs[:given], refs[given : given + 3]
+    outs, values, sems = refs[given + 3 : given + 6], refs[given + 6 : -1], refs[-1]
     rows = outs[0].shape[0]
     base, copies = 0, []
-    for p in range(pieces):
-        own, side, passed = parts[3 * p : 3 * p + 3]
+    for p, count in enumerate(counts):
+        first = sum(counts[:p])
+        own, *others = parts[first : first + count]
         at = slice(base, base + own.shape[1])
         base = at.stop
-        grad = own[...] + side[:rows, :].astype(jnp.float32) + passed[...].astype(jnp.float32)
-        results = adamw(grad / jnp.float32(total), *[state[:, at] for state in states])
+        grad = own[...]
+        for other in others:
+            grad = grad + other[:rows, :].astype(jnp.float32)
+        results = adamw(grad * jnp.float32(1.0 / total), *[state[:, at] for state in states])
         for tile, value in zip(values, results):
             tile[:, at] = value
         copies.extend(store_tile(p, at, sems, tuple(zip(values, outs))))
@@ -344,23 +353,27 @@
         picked[0], swap(picked[1], 1), far_half, far_rest, swap(far_half, 1), swap(far_rest, 1)
     ]
     hidden, sums = [], []
-    for lo, hi in zip(cuts[:-1], cuts[1:]):
+    for p, (lo, hi) in enumerate(zip(cuts[:-1], cuts[1:])):
         own = gated(gate[:, lo:hi], up_val[:, lo:hi])
         hidden.append(own)
         across = swap(own, 2)
         rights = [own, swap(own, 1), across, swap(across, 1)]
         size = hi - lo
-        own_sum, side, across_sum = call(
-            functools.partial(grads_kernel, rows),
-            [f32(rows, size), bf16(2 * rows, size), f32(rows, size)],
+        final = p == pieces - 1
+        own_sum, side, across, *third = call(
+            functools.partial(grads_kernel, rows, final),
+            [f32(rows, size)]
+            + ([bf16(rows, size)] * 3 if final else [bf16(2 * rows, size), f32(rows, size)]),
             [rep_arr] + lefts + rights,
             [pltpu.VMEM((zs * rows, 4 * tokens), jnp.bfloat16)],
             smem=1,
             flops=8 * zs * rows * tokens * size,
         )
         side = swap(side, 4)
-        (passed,) = call(add_kernel, [bf16(rows, size)], [across_sum, side])
-        sums.extend([own_sum, side, swap(passed, 8)])
+        if not final:
+            (across,) = call(add_kernel, [bf16(rows, size)], [across, side])
+        across = swap(across, 8)
+        sums.append([own_sum, side, across, *[swap(value, 12) for value in third]])
     *turned, left_near, left_far = call(
         functools.partial(turn_kernel, pieces),
         [bf16(h.shape[1], tokens) for h in hidden] + [bf16(tokens, depth // 2)] * 2,
@@ -410,13 +423,13 @@
         functools.partial(merge_kernel, zs, rows),
         [bf16(tokens, 2 * half)],
         [me_arr, keep, got, middle, got_middle, keep_last, got_last],
-        [pltpu.VMEM((2 * half, tokens), jnp.float32)],
+        [pltpu.VMEM((2 * half, tokens), jnp.bfloat16)],
         smem=1,
     )
     master_new, first, second = call(
-        functools.partial(adamw_kernel, total, pieces),
+        functools.partial(adamw_kernel, total, [len(parts) for parts in sums]),
         [f32(rows, width)] * 3,
-        sums + [master, moment_one, moment_two],
+        [v for parts in sums for v in parts] + [master, moment_one, moment_two],
         [pltpu.VMEM((rows, width), jnp.float32)] * 3 + [pltpu.SemaphoreType.DMA((3 * pieces,))],
         copied=True,
     )

time: 121 us -> 123 us (1.017)
  starting transfers between devices: 31.9 us -> 37.1 us
  waiting for transfers between devices: 71.3 us -> 67.8 us
    ppermute x34 -> x35, waiting for transfers between devices: 71.3 us -> 67.8 us  [swap(): return lax.ppermute(value, 'dp', [(i, i ^ m) for i in range(n)])]
    ppermute x34 -> x35, starting transfers between devices: 28.7 us -> 32.3 us  [swap(): return lax.ppermute(value, 'dp', [(i, i ^ m) for i in range(n)])]
    ppermute x4, starting transfers between devices: 3.2 us -> 4.82 us  [across_rep(): return lax.ppermute(value, 'rep', [(0, 1), (1, 0)])]
    pallas_call x15 -> x14, Pallas kernels: 11.7 us -> 11.6 us  [call(): pl.pallas_call(kernel, out_shape=list(outs), in_specs=[SMEM] * smem + [VM...]
  transfers between devices with their start and end apart: 38 -> 39, of which waited for: 13 -> 11; matrix products, arithmetic and copies ran while one was open for 3% -> 3% of each run, Pallas kernels for 9% -> 9%
where the time goes in v4:
time: 123 us
  waiting for transfers between devices  67.8 us (55%)
  starting transfers between devices  37.1 us (30%)
  Pallas kernels  11.6 us (9%)
  other arithmetic  4.24 us (3%)
    ppermute x35, waiting for transfers between devices, swap(): return lax.ppermute(value, 'dp', [(i, i ^ m) for i in range(n)])  67.8 us
    ppermute x35, starting transfers between devices, swap(): return lax.ppermute(value, 'dp', [(i, i ^ m) for i in range(n)])  32.3 us
    pallas_call x14, Pallas kernels, call(): pl.pallas_call(kernel, out_shape=list(outs), in_specs=[SMEM] * smem + [VM...  11.6 us
    ppermute x4, starting transfers between devices, across_rep(): return lax.ppermute(value, 'rep', [(0, 1), (1, 0)])  4.82 us
    convert_element_type x2, other arithmetic, gated(): (gate * jax.nn.sigmoid(gate) * up_val.astype(jnp.float32)).astype(jnp.bfl...  3.09 us
  transfers between devices with their start and end apart: 39, of which 11 were waited for; matrix products, arithmetic and copies ran while one was open for 3% of the time, Pallas kernels for 9%

profile of v4, /device:TPU:0, one launch (start us, length us, event | category | flops | bytes accessed | tf_op | source)
XLA Modules:
  0.0 122.8 jit_solution(16745474140385424054)
XLA Ops:
  0.7 1.1 copy-done.5
  1.8 0.2 shard_map.109
  2.0 3.1 %collective-permute-start.19 = (bf16[256,256]{1,0:T(8,128)(2,1)S(1)}, bf16[256,256]{1,0:T(8,128)(2,1)S(1)}, u32[]{:S(2)}, u32[]{:S(2)}) collective-permute-start(bf16[256,256]{1,0:T(8,128)(2,1)S(1)} %get-tuple-element.60), channel_id=1, source_target_pairs={{0,4},{2,6},{4,0},{6,2},{8,12},{10,14},{12,8},{14,10},{16,20},{18,... | collective-permute-start | bytes 393224 | tf_op jit(solution)/shard_map/ppermute | solution.py:316
  5.1 1.1 convert_element_type.39.refs_4_
  6.3 0.1 collective-permute-start
  6.3 1.6 %collective-permute-start.1 = (bf16[64,2816]{1,0:T(8,128)(2,1)S(1)}, bf16[64,2816]{1,0:T(8,128)(2,1)S(1)}, u32[]{:S(2)}, u32[]{:S(2)}) collective-permute-start(bf16[64,2816]{1,0:T(8,128)(2,1)S(1)} %convert_element_type.39.refs_4_), channel_id=1, source_target_pairs={{0,8},{2,10},{4,12},{6,14},{8,0},{10,2},{12,4},{14,6},{16,24},{18,... | collective-permute-start | bytes 1081352 | tf_op jit(solution)/shard_map/ppermute | solution.py:316
  8.0 0.2 collective-permute-start.18
  8.1 0.5 collective-permute-done.19.refs_2_
  8.6 1.7 %collective-permute-start.20 = (bf16[256,256]{1,0:T(8,128)(2,1)S(1)}, bf16[256,256]{1,0:T(8,128)(2,1)S(1)}, u32[]{:S(2)}, u32[]{:S(2)}) collective-permute-start(bf16[256,256]{1,0:T(8,128)(2,1)S(1)} %collective-permute-done.19.refs_2_), channel_id=1, source_target_pairs={{0,1},{1,0},{2,3},{3,2},{4,5},{5,4},{6,7},{7,6},{8,9},{9,8},{10,11... | collective-permute-start | bytes 393224 | tf_op jit(solution)/shard_map/ppermute | solution.py:341
  10.3 1.3 %fusion.14.refs_2_.refs_6_ = bf16[256,768]{1,0:T(8,128)(2,1)S(1)} fusion(bf16[256,2816]{1,0:T(8,128)(2,1)S(1)} %bitcast.8, bf16[256,2816]{1,0:T(8,128)(2,1)} %bitcast.11), kind=kLoop, calls=%fused_computation.20 | loop fusion | flops 1572864 | bytes 1179648 | tf_op jit(solution)/shard_map/convert_element_type | solution.py:29
  11.6 0.0 collective-permute-done.18.refs_1_
  11.6 2.7 %collective-permute-start.3 = (bf16[64,2816]{1,0:T(8,128)(2,1)S(1)}, bf16[64,2816]{1,0:T(8,128)(2,1)S(1)}, u32[]{:S(2)}, u32[]{:S(2)}) collective-permute-start(bf16[64,2816]{1,0:T(8,128)(2,1)S(1)} %convert_element_type.39.refs_4_), channel_id=1, source_target_pairs={{0,16},{2,18},{4,20},{6,22},{8,24},{10,26},{12,28},{14,30},{16,0},... | collective-permute-start | bytes 1081352 | tf_op jit(solution)/shard_map/ppermute | solution.py:316
  14.2 0.0 collective-permute-done.20.refs_3_
  14.2 1.5 %collective-permute-start.8 = (bf16[64,2816]{1,0:T(8,128)(2,1)S(1)}, bf16[64,2816]{1,0:T(8,128)(2,1)S(1)}, u32[]{:S(2)}, u32[]{:S(2)}) collective-permute-start(bf16[64,2816]{1,0:T(8,128)(2,1)S(1)} %convert_element_type.39.refs_4_), channel_id=1, source_target_pairs={{0,4},{2,6},{4,0},{6,2},{8,12},{10,14},{12,8},{14,10},{16,20},{18,... | collective-permute-start | bytes 1081352 | tf_op jit(solution)/shard_map/ppermute | solution.py:316
  15.8 0.0 collective-permute-done.21.refs_4_
  15.8 0.0 collective-permute-start.33
  15.8 0.0 collective-permute-done.refs_5_
  15.8 0.5 collective-permute-start.22
  16.3 1.8 %fusion.8 = (bf16[256,1024]{1,0:T(8,128)(2,1)S(1)}, bf16[256,1024]{1,0:T(8,128)(2,1)S(1)}) fusion(bf16[256,2816]{1,0:T(8,128)(2,1)S(1)} %bitcast.9, bf16[256,2816]{1,0:T(8,128)(2,1)} %bitcast.12), kind=kLoop, calls=%fused_computation.12 | loop fusion | flops 4194304 | bytes 3145728 | tf_op jit(solution)/shard_map/convert_element_type | solution.py:29
  18.1 2.6 %collective-permute-done.1.refs_6_ = bf16[64,2816]{1,0:T(8,128)(2,1)S(1)} collective-permute-done((bf16[64,2816]{1,0:T(8,128)(2,1)S(1)}, bf16[64,2816]{1,0:T(8,128)(2,1)S(1)}, u32[]{:S(2)}, u32[]{:S(2)}) %collective-permute-start.1) | collective-permute-done | bytes 360480 | tf_op jit(solution)/shard_map/ppermute | solution.py:316
  20.7 0.0 collective-permute-start.23
  20.7 10.4 %collective-permute-done.3.refs_8_ = bf16[64,2816]{1,0:T(8,128)(2,1)S(1)} collective-permute-done((bf16[64,2816]{1,0:T(8,128)(2,1)S(1)}, bf16[64,2816]{1,0:T(8,128)(2,1)S(1)}, u32[]{:S(2)}, u32[]{:S(2)}) %collective-permute-start.3) | collective-permute-done | bytes 360480 | tf_op jit(solution)/shard_map/ppermute | solution.py:316
  31.1 1.5 %collective-permute-start.24 = (bf16[256,1024]{1,0:T(8,128)(2,1)S(1)}, bf16[256,1024]{1,0:T(8,128)(2,1)S(1)}, u32[]{:S(2)}, u32[]{:S(2)}) collective-permute-start(bf16[256,1024]{1,0:T(8,128)(2,1)S(1)} %get-tuple-element.75.refs_0_.refs_6_), channel_id=1, source_target_pairs={{0,4},{2,6},{4,0},{6,2},{8,12},{10,14},{12,8},{14,10},{16,20},{18,... | collective-permute-start | bytes 1572872 | tf_op jit(solution)/shard_map/ppermute | solution.py:316
  32.7 0.5 collective-permute-start.34
  33.2 1.6 %collective-permute-start.29 = (bf16[256,1024]{1,0:T(8,128)(2,1)S(1)}, bf16[256,1024]{1,0:T(8,128)(2,1)S(1)}, u32[]{:S(2)}, u32[]{:S(2)}) collective-permute-start(bf16[256,1024]{1,0:T(8,128)(2,1)S(1)} %get-tuple-element.74.refs_1_.refs_6_), channel_id=1, source_target_pairs={{0,4},{2,6},{4,0},{6,2},{8,12},{10,14},{12,8},{14,10},{16,20},{18,... | collective-permute-start | bytes 1572872 | tf_op jit(solution)/shard_map/ppermute | solution.py:316
  34.8 19.6 %collective-permute-done.34.refs_8_ = bf16[256,768]{1,0:T(8,128)(2,1)S(1)} collective-permute-done((bf16[256,768]{1,0:T(8,128)(2,1)S(1)}, bf16[256,768]{1,0:T(8,128)(2,1)S(1)}, u32[]{:S(2)}, u32[]{:S(2)}) %collective-permute-start.34) | collective-permute-done | bytes 393248 | tf_op jit(solution)/shard_map/ppermute | solution.py:316
  54.4 0.5 collective-permute-start.4
  54.9 0.7 collective-permute-start.5
  55.6 8.7 %collective-permute-done.29.refs_8_ = bf16[256,1024]{1,0:T(8,128)(2,1)S(1)} collective-permute-done((bf16[256,1024]{1,0:T(8,128)(2,1)S(1)}, bf16[256,1024]{1,0:T(8,128)(2,1)S(1)}, u32[]{:S(2)}, u32[]{:S(2)}) %collective-permute-start.29) | collective-permute-done | bytes 524320 | tf_op jit(solution)/shard_map/ppermute | solution.py:316
  64.3 0.7 collective-permute-start.10
  65.0 1.7 %collective-permute-start.12 = (bf16[64,2816]{1,0:T(8,128)(2,1)S(1)}, bf16[64,2816]{1,0:T(8,128)(2,1)S(1)}, u32[]{:S(2)}, u32[]{:S(2)}) collective-permute-start(bf16[64,2816]{1,0:T(8,128)(2,1)S(1)} %collective-permute-done.3.refs_8_), channel_id=1, source_target_pairs={{0,4},{2,6},{4,0},{6,2},{8,12},{10,14},{12,8},{14,10},{16,20},{18,... | collective-permute-start | bytes 1081352 | tf_op jit(solution)/shard_map/ppermute | solution.py:316
  66.7 0.5 collective-permute-start.30
  67.2 0.1 collective-permute-start.35
  67.3 6.1 %collective-permute-done.10.refs_5_.refs_2_ = bf16[64,2816]{1,0:T(8,128)(2,1)S(1)} collective-permute-done((bf16[64,2816]{1,0:T(8,128)(2,1)S(1)}, bf16[64,2816]{1,0:T(8,128)(2,1)S(1)}, u32[]{:S(2)}, u32[]{:S(2)}) %collective-permute-start.10) | collective-permute-done | bytes 360480 | tf_op jit(solution)/shard_map/ppermute | solution.py:316
  73.4 1.5 %collective-permute-start.15 = (bf16[64,2816]{1,0:T(8,128)(2,1)S(1)}, bf16[64,2816]{1,0:T(8,128)(2,1)S(1)}, u32[]{:S(2)}, u32[]{:S(2)}) collective-permute-start(bf16[64,2816]{1,0:T(8,128)(2,1)S(1)} %collective-permute-done.5.refs_10_), channel_id=1, source_target_pairs={{0,4},{2,6},{4,0},{6,2},{8,12},{10,14},{12,8},{14,10},{16,20},{18,... | collective-permute-start | bytes 1081352 | tf_op jit(solution)/shard_map/ppermute | solution.py:316
  74.9 0.5 collective-permute-start.11
  75.4 0.6 shard_map.121
  76.1 0.1 collective-permute-start.13
  76.2 1.2 collective-permute-start.36
  77.4 4.4 %collective-permute-done.15.refs_4_.refs_6_ = bf16[64,2816]{1,0:T(8,128)(2,1)S(1)} collective-permute-done((bf16[64,2816]{1,0:T(8,128)(2,1)S(1)}, bf16[64,2816]{1,0:T(8,128)(2,1)S(1)}, u32[]{:S(2)}, u32[]{:S(2)}) %collective-permute-start.15) | collective-permute-done | bytes 360480 | tf_op jit(solution)/shard_map/ppermute | solution.py:316
  81.8 0.8 shard_map.117
  82.5 0.8 shard_map.119
  83.3 1.2 collective-permute-start.26
  84.5 0.9 collective-permute-start.31
  85.4 0.6 shard_map.110
  86.0 1.8 %shard_map.111 = (f32[256,256]{1,0:T(8,128)S(1)}, f32[256,256]{1,0:T(8,128)S(1)}, f32[256,2816]{1,0:T(8,128)S(1)}) custom-call(s32[1]{0:T(128)} %bitcast.me_ref, s32[1]{0:T(128)} %bitcast.1.rep_ref, bf16[1024,256]{1,0:T(8,128)(2,1)S(1)} %get-tuple-element.43.refs_0_, bf16[1024,256]{1,0:T(8,128)(2,1)S(1)} %get-tuple-element.44.refs_1_, ...), custom_call_target="tpu_custom_call" | custom-call | flops 1476395008 | bytes 7995400 | tf_op jit(solution)/shard_map/pallas_call | solution.py:290
  87.7 1.0 collective-permute-start.7
  88.7 3.9 %collective-permute-done.26.side.refs_1_ = bf16[128,1024]{1,0:T(8,128)(2,1)S(1)} collective-permute-done((bf16[128,1024]{1,0:T(8,128)(2,1)S(1)}, bf16[128,1024]{1,0:T(8,128)(2,1)S(1)}, u32[]{:S(2)}, u32[]{:S(2)}) %collective-permute-start.26) | collective-permute-done | bytes 262176 | tf_op jit(solution)/shard_map/ppermute | solution.py:316
  92.5 3.4 %collective-permute-start.37 = (bf16[64,768]{1,0:T(8,128)(2,1)S(1)}, bf16[64,768]{1,0:T(8,128)(2,1)S(1)}, u32[]{:S(2)}, u32[]{:S(2)}) collective-permute-start(bf16[64,768]{1,0:T(8,128)(2,1)S(1)} %get-tuple-element.69), channel_id=1, source_target_pairs={{0,16},{2,18},{4,20},{6,22},{8,24},{10,26},{12,28},{14,30},{16,0},... | collective-permute-start | bytes 294920 | tf_op jit(solution)/shard_map/ppermute | solution.py:316
  95.9 3.9 %collective-permute-done.31.side.refs_4_ = bf16[128,1024]{1,0:T(8,128)(2,1)S(1)} collective-permute-done((bf16[128,1024]{1,0:T(8,128)(2,1)S(1)}, bf16[128,1024]{1,0:T(8,128)(2,1)S(1)}, u32[]{:S(2)}, u32[]{:S(2)}) %collective-permute-start.31) | collective-permute-done | bytes 262176 | tf_op jit(solution)/shard_map/ppermute | solution.py:316
  99.8 3.0 %collective-permute-start.38 = (bf16[64,768]{1,0:T(8,128)(2,1)S(1)}, bf16[64,768]{1,0:T(8,128)(2,1)S(1)}, u32[]{:S(2)}, u32[]{:S(2)}) collective-permute-start(bf16[64,768]{1,0:T(8,128)(2,1)S(1)} %get-tuple-element.70), channel_id=1, source_target_pairs={{0,24},{2,26},{4,28},{6,30},{8,16},{10,18},{12,20},{14,22},{16,8},... | collective-permute-start | bytes 294920 | tf_op jit(solution)/shard_map/ppermute | solution.py:316
  102.9 0.1 collective-permute-start.27
  103.0 2.9 %collective-permute-start.32 = (bf16[64,1024]{1,0:T(8,128)(2,1)S(1)}, bf16[64,1024]{1,0:T(8,128)(2,1)S(1)}, u32[]{:S(2)}, u32[]{:S(2)}) collective-permute-start(bf16[64,1024]{1,0:T(8,128)(2,1)S(1)} %shard_map.120), channel_id=1, source_target_pairs={{0,16},{2,18},{4,20},{6,22},{8,24},{10,26},{12,28},{14,30},{16,0},... | collective-permute-start | bytes 393224 | tf_op jit(solution)/shard_map/ppermute | solution.py:316
  105.9 0.7 shard_map.112
  106.6 0.0 copy-start.1
  106.6 0.4 shard_map.113
  107.0 0.6 collective-permute-start.14
  107.6 1.6 %collective-permute-start.17 = (f32[128,256]{1,0:T(8,128)S(1)}, f32[128,256]{1,0:T(8,128)S(1)}, u32[]{:S(2)}, u32[]{:S(2)}) collective-permute-start(f32[128,256]{1,0:T(8,128)S(1)} %get-tuple-element.53), channel_id=1, source_target_pairs={{0,1},{1,0},{2,3},{3,2},{4,5},{5,4},{6,7},{7,6},{8,9},{9,8},{10,11... | collective-permute-start | bytes 393224 | tf_op jit(solution)/shard_map/ppermute | solution.py:341
  109.2 1.1 shard_map.115
  110.3 5.4 %collective-permute-done.27.refs_2_ = bf16[64,1024]{1,0:T(8,128)(2,1)S(1)} collective-permute-done((bf16[64,1024]{1,0:T(8,128)(2,1)S(1)}, bf16[64,1024]{1,0:T(8,128)(2,1)S(1)}, u32[]{:S(2)}, u32[]{:S(2)}) %collective-permute-start.27) | collective-permute-done | bytes 131104 | tf_op jit(solution)/shard_map/ppermute | solution.py:316
  115.7 2.3 %collective-permute-done.32.refs_5_ = bf16[64,1024]{1,0:T(8,128)(2,1)S(1)} collective-permute-done((bf16[64,1024]{1,0:T(8,128)(2,1)S(1)}, bf16[64,1024]{1,0:T(8,128)(2,1)S(1)}, u32[]{:S(2)}, u32[]{:S(2)}) %collective-permute-start.32) | collective-permute-done | bytes 131104 | tf_op jit(solution)/shard_map/ppermute | solution.py:316
  118.1 1.7 %shard_map.122 = (f32[64,2816]{1,0:T(8,128)}, f32[64,2816]{1,0:T(8,128)}, f32[64,2816]{1,0:T(8,128)}) custom-call(f32[64,1024]{1,0:T(8,128)S(1)} %get-tuple-element.61.refs_0_, bf16[128,1024]{1,0:T(8,128)(2,1)S(1)} %collective-permute-done.26.side.refs_1_, bf16[64,1024]{1,0:T(8,128)(2,1)S(1)} %collective-permute-done.27.refs_2_, ...), custom_call_target="tpu_custom_call" | custom-call | bytes 6127616 | tf_op jit(solution)/shard_map/pallas_call | solution.py:290
  119.7 2.1 %shard_map.116 = (bf16[256,2816]{1,0:T(8,128)(2,1)}, bf16[256,2816]{1,0:T(8,128)(2,1)}) custom-call(bf16[256,512]{1,0:T(8,128)(2,1)S(1)} %get-tuple-element.54.left, f32[256,2816]{1,0:T(8,128)S(1)} %get-tuple-element.55.gate_slope, f32[256,2816]{1,0:T(8,128)S(1)} %get-tuple-element.56.up_slope, f32[256,2816]{1,0:T(8,128)S(1)} %get-tuple-element.57.early, ...), custom_call_target="tpu_custom_call" | custom-call | flops 738197504 | bytes 14680064 | tf_op jit(solution)/shard_map/pallas_call | solution.py:290
  121.9 0.9 shard_map.114
  (43 shorter events, 0.2 us)
Async XLA Ops:
  0.6 9.7 %copy-start = (bf16[2,128,2816]{2,1,0:T(8,128)(2,1)S(1)}, bf16[2,128,2816]{2,1,0:T(8,128)(2,1)}, u32[]{:S(2)}) copy-start(bf16[2,128,2816]{2,1,0:T(8,128)(2,1)} %param.7) | copy-start | bytes 4325380
  0.6 1.2 copy-start.5
  2.0 6.6 %collective-permute-start.19 = (bf16[256,256]{1,0:T(8,128)(2,1)S(1)}, bf16[256,256]{1,0:T(8,128)(2,1)S(1)}, u32[]{:S(2)}, u32[]{:S(2)}) collective-permute-start(bf16[256,256]{1,0:T(8,128)(2,1)S(1)} %get-tuple-element.60), channel_id=1, source_target_pairs={{0,4},{2,6},{4,0},{6,2},{8,12},{10,14},{12,8},{14,10},{16,20},{18,... | collective-permute-start | bytes 393224 | tf_op jit(solution)/shard_map/ppermute | solution.py:316
  6.3 9.5 %collective-permute-start = (bf16[64,2816]{1,0:T(8,128)(2,1)S(1)}, bf16[64,2816]{1,0:T(8,128)(2,1)S(1)}, u32[]{:S(2)}, u32[]{:S(2)}) collective-permute-start(bf16[64,2816]{1,0:T(8,128)(2,1)S(1)} %convert_element_type.39.refs_4_), channel_id=1, source_target_pairs={{0,2},{2,0},{4,6},{6,4},{8,10},{10,8},{12,14},{14,12},{16,18},{18,... | collective-permute-start | bytes 1081352 | tf_op jit(solution)/shard_map/ppermute | solution.py:316
  6.3 14.4 %collective-permute-start.1 = (bf16[64,2816]{1,0:T(8,128)(2,1)S(1)}, bf16[64,2816]{1,0:T(8,128)(2,1)S(1)}, u32[]{:S(2)}, u32[]{:S(2)}) collective-permute-start(bf16[64,2816]{1,0:T(8,128)(2,1)S(1)} %convert_element_type.39.refs_4_), channel_id=1, source_target_pairs={{0,8},{2,10},{4,12},{6,14},{8,0},{10,2},{12,4},{14,6},{16,24},{18,... | collective-permute-start | bytes 1081352 | tf_op jit(solution)/shard_map/ppermute | solution.py:316
  8.0 3.6 %collective-permute-start.18 = (bf16[256,256]{1,0:T(8,128)(2,1)S(1)}, bf16[256,256]{1,0:T(8,128)(2,1)S(1)}, u32[]{:S(2)}, u32[]{:S(2)}) collective-permute-start(bf16[256,256]{1,0:T(8,128)(2,1)S(1)} %get-tuple-element.41.refs_4_), channel_id=1, source_target_pairs={{0,2},{2,0},{4,6},{6,4},{8,10},{10,8},{12,14},{14,12},{16,18},{18,... | collective-permute-start | bytes 393224 | tf_op jit(solution)/shard_map/ppermute | solution.py:316
  8.6 5.6 %collective-permute-start.20 = (bf16[256,256]{1,0:T(8,128)(2,1)S(1)}, bf16[256,256]{1,0:T(8,128)(2,1)S(1)}, u32[]{:S(2)}, u32[]{:S(2)}) collective-permute-start(bf16[256,256]{1,0:T(8,128)(2,1)S(1)} %collective-permute-done.19.refs_2_), channel_id=1, source_target_pairs={{0,1},{1,0},{2,3},{3,2},{4,5},{5,4},{6,7},{7,6},{8,9},{9,8},{10,11... | collective-permute-start | bytes 393224 | tf_op jit(solution)/shard_map/ppermute | solution.py:341
  10.3 5.5 %collective-permute-start.21 = (bf16[256,256]{1,0:T(8,128)(2,1)S(1)}, bf16[256,256]{1,0:T(8,128)(2,1)S(1)}, u32[]{:S(2)}, u32[]{:S(2)}) collective-permute-start(bf16[256,256]{1,0:T(8,128)(2,1)S(1)} %collective-permute-done.19.refs_2_), channel_id=1, source_target_pairs={{0,2},{2,0},{4,6},{6,4},{8,10},{10,8},{12,14},{14,12},{16,18},{18,... | collective-permute-start | bytes 393224 | tf_op jit(solution)/shard_map/ppermute | solution.py:316
  11.6 19.6 %collective-permute-start.3 = (bf16[64,2816]{1,0:T(8,128)(2,1)S(1)}, bf16[64,2816]{1,0:T(8,128)(2,1)S(1)}, u32[]{:S(2)}, u32[]{:S(2)}) collective-permute-start(bf16[64,2816]{1,0:T(8,128)(2,1)S(1)} %convert_element_type.39.refs_4_), channel_id=1, source_target_pairs={{0,16},{2,18},{4,20},{6,22},{8,24},{10,26},{12,28},{14,30},{16,0},... | collective-permute-start | bytes 1081352 | tf_op jit(solution)/shard_map/ppermute | solution.py:316
  14.2 18.4 %collective-permute-start.8 = (bf16[64,2816]{1,0:T(8,128)(2,1)S(1)}, bf16[64,2816]{1,0:T(8,128)(2,1)S(1)}, u32[]{:S(2)}, u32[]{:S(2)}) collective-permute-start(bf16[64,2816]{1,0:T(8,128)(2,1)S(1)} %convert_element_type.39.refs_4_), channel_id=1, source_target_pairs={{0,4},{2,6},{4,0},{6,2},{8,12},{10,14},{12,8},{14,10},{16,20},{18,... | collective-permute-start | bytes 1081352 | tf_op jit(solution)/shard_map/ppermute | solution.py:316
  15.8 17.4 %collective-permute-start.33 = (bf16[256,768]{1,0:T(8,128)(2,1)S(1)}, bf16[256,768]{1,0:T(8,128)(2,1)S(1)}, u32[]{:S(2)}, u32[]{:S(2)}) collective-permute-start(bf16[256,768]{1,0:T(8,128)(2,1)S(1)} %fusion.14.refs_2_.refs_6_), channel_id=1, source_target_pairs={{0,2},{2,0},{4,6},{6,4},{8,10},{10,8},{12,14},{14,12},{16,18},{18,... | collective-permute-start | bytes 1179656 | tf_op jit(solution)/shard_map/ppermute | solution.py:316
  15.8 17.4 %collective-permute-start.22 = (bf16[256,256]{1,0:T(8,128)(2,1)S(1)}, bf16[256,256]{1,0:T(8,128)(2,1)S(1)}, u32[]{:S(2)}, u32[]{:S(2)}) collective-permute-start(bf16[256,256]{1,0:T(8,128)(2,1)S(1)} %collective-permute-done.20.refs_3_), channel_id=1, source_target_pairs={{0,2},{2,0},{4,6},{6,4},{8,10},{10,8},{12,14},{14,12},{16,18},{18,... | collective-permute-start | bytes 393224 | tf_op jit(solution)/shard_map/ppermute | solution.py:316
  20.7 33.6 %collective-permute-start.23 = (bf16[256,1024]{1,0:T(8,128)(2,1)S(1)}, bf16[256,1024]{1,0:T(8,128)(2,1)S(1)}, u32[]{:S(2)}, u32[]{:S(2)}) collective-permute-start(bf16[256,1024]{1,0:T(8,128)(2,1)S(1)} %get-tuple-element.75.refs_0_.refs_6_), channel_id=1, source_target_pairs={{0,2},{2,0},{4,6},{6,4},{8,10},{10,8},{12,14},{14,12},{16,18},{18,... | collective-permute-start | bytes 1572872 | tf_op jit(solution)/shard_map/ppermute | solution.py:316
  31.1 23.7 %collective-permute-start.24 = (bf16[256,1024]{1,0:T(8,128)(2,1)S(1)}, bf16[256,1024]{1,0:T(8,128)(2,1)S(1)}, u32[]{:S(2)}, u32[]{:S(2)}) collective-permute-start(bf16[256,1024]{1,0:T(8,128)(2,1)S(1)} %get-tuple-element.75.refs_0_.refs_6_), channel_id=1, source_target_pairs={{0,4},{2,6},{4,0},{6,2},{8,12},{10,14},{12,8},{14,10},{16,20},{18,... | collective-permute-start | bytes 1572872 | tf_op jit(solution)/shard_map/ppermute | solution.py:316
  32.7 21.7 %collective-permute-start.34 = (bf16[256,768]{1,0:T(8,128)(2,1)S(1)}, bf16[256,768]{1,0:T(8,128)(2,1)S(1)}, u32[]{:S(2)}, u32[]{:S(2)}) collective-permute-start(bf16[256,768]{1,0:T(8,128)(2,1)S(1)} %fusion.14.refs_2_.refs_6_), channel_id=1, source_target_pairs={{0,4},{2,6},{4,0},{6,2},{8,12},{10,14},{12,8},{14,10},{16,20},{18,... | collective-permute-start | bytes 1179656 | tf_op jit(solution)/shard_map/ppermute | solution.py:316
  33.2 22.5 %collective-permute-start.28 = (bf16[256,1024]{1,0:T(8,128)(2,1)S(1)}, bf16[256,1024]{1,0:T(8,128)(2,1)S(1)}, u32[]{:S(2)}, u32[]{:S(2)}) collective-permute-start(bf16[256,1024]{1,0:T(8,128)(2,1)S(1)} %get-tuple-element.74.refs_1_.refs_6_), channel_id=1, source_target_pairs={{0,2},{2,0},{4,6},{6,4},{8,10},{10,8},{12,14},{14,12},{16,18},{18,... | collective-permute-start | bytes 1572872 | tf_op jit(solution)/shard_map/ppermute | solution.py:316
  33.2 31.1 %collective-permute-start.29 = (bf16[256,1024]{1,0:T(8,128)(2,1)S(1)}, bf16[256,1024]{1,0:T(8,128)(2,1)S(1)}, u32[]{:S(2)}, u32[]{:S(2)}) collective-permute-start(bf16[256,1024]{1,0:T(8,128)(2,1)S(1)} %get-tuple-element.74.refs_1_.refs_6_), channel_id=1, source_target_pairs={{0,4},{2,6},{4,0},{6,2},{8,12},{10,14},{12,8},{14,10},{16,20},{18,... | collective-permute-start | bytes 1572872 | tf_op jit(solution)/shard_map/ppermute | solution.py:316
  54.4 10.7 %collective-permute-start.2 = (bf16[64,2816]{1,0:T(8,128)(2,1)S(1)}, bf16[64,2816]{1,0:T(8,128)(2,1)S(1)}, u32[]{:S(2)}, u32[]{:S(2)}) collective-permute-start(bf16[64,2816]{1,0:T(8,128)(2,1)S(1)} %collective-permute-done.1.refs_6_), channel_id=1, source_target_pairs={{0,2},{2,0},{4,6},{6,4},{8,10},{10,8},{12,14},{14,12},{16,18},{18,... | collective-permute-start | bytes 1081352 | tf_op jit(solution)/shard_map/ppermute | solution.py:316
  54.4 12.4 %collective-permute-start.4 = (bf16[64,2816]{1,0:T(8,128)(2,1)S(1)}, bf16[64,2816]{1,0:T(8,128)(2,1)S(1)}, u32[]{:S(2)}, u32[]{:S(2)}) collective-permute-start(bf16[64,2816]{1,0:T(8,128)(2,1)S(1)} %collective-permute-done.3.refs_8_), channel_id=1, source_target_pairs={{0,2},{2,0},{4,6},{6,4},{8,10},{10,8},{12,14},{14,12},{16,18},{18,... | collective-permute-start | bytes 1081352 | tf_op jit(solution)/shard_map/ppermute | solution.py:316
  54.9 11.8 %collective-permute-start.5 = (bf16[64,2816]{1,0:T(8,128)(2,1)S(1)}, bf16[64,2816]{1,0:T(8,128)(2,1)S(1)}, u32[]{:S(2)}, u32[]{:S(2)}) collective-permute-start(bf16[64,2816]{1,0:T(8,128)(2,1)S(1)} %collective-permute-done.3.refs_8_), channel_id=1, source_target_pairs={{0,8},{2,10},{4,12},{6,14},{8,0},{10,2},{12,4},{14,6},{16,24},{18,... | collective-permute-start | bytes 1081352 | tf_op jit(solution)/shard_map/ppermute | solution.py:316
  55.6 11.6 %collective-permute-start.9 = (bf16[64,2816]{1,0:T(8,128)(2,1)S(1)}, bf16[64,2816]{1,0:T(8,128)(2,1)S(1)}, u32[]{:S(2)}, u32[]{:S(2)}) collective-permute-start(bf16[64,2816]{1,0:T(8,128)(2,1)S(1)} %collective-permute-done.8.refs_3_.refs_0_), channel_id=1, source_target_pairs={{0,2},{2,0},{4,6},{6,4},{8,10},{10,8},{12,14},{14,12},{16,18},{18,... | collective-permute-start | bytes 1081352 | tf_op jit(solution)/shard_map/ppermute | solution.py:316
  64.3 9.1 %collective-permute-start.10 = (bf16[64,2816]{1,0:T(8,128)(2,1)S(1)}, bf16[64,2816]{1,0:T(8,128)(2,1)S(1)}, u32[]{:S(2)}, u32[]{:S(2)}) collective-permute-start(bf16[64,2816]{1,0:T(8,128)(2,1)S(1)} %collective-permute-done.8.refs_3_.refs_0_), channel_id=1, source_target_pairs={{0,8},{2,10},{4,12},{6,14},{8,0},{10,2},{12,4},{14,6},{16,24},{18,... | collective-permute-start | bytes 1081352 | tf_op jit(solution)/shard_map/ppermute | solution.py:316
  65.0 9.9 %collective-permute-start.12 = (bf16[64,2816]{1,0:T(8,128)(2,1)S(1)}, bf16[64,2816]{1,0:T(8,128)(2,1)S(1)}, u32[]{:S(2)}, u32[]{:S(2)}) collective-permute-start(bf16[64,2816]{1,0:T(8,128)(2,1)S(1)} %collective-permute-done.3.refs_8_), channel_id=1, source_target_pairs={{0,4},{2,6},{4,0},{6,2},{8,12},{10,14},{12,8},{14,10},{16,20},{18,... | collective-permute-start | bytes 1081352 | tf_op jit(solution)/shard_map/ppermute | solution.py:316
  66.7 9.3 %collective-permute-start.25 = (bf16[256,1024]{1,0:T(8,128)(2,1)S(1)}, bf16[256,1024]{1,0:T(8,128)(2,1)S(1)}, u32[]{:S(2)}, u32[]{:S(2)}) collective-permute-start(bf16[256,1024]{1,0:T(8,128)(2,1)S(1)} %collective-permute-done.24.refs_8_), channel_id=1, source_target_pairs={{0,2},{2,0},{4,6},{6,4},{8,10},{10,8},{12,14},{14,12},{16,18},{18,... | collective-permute-start | bytes 1572872 | tf_op jit(solution)/shard_map/ppermute | solution.py:316
  66.7 9.5 %collective-permute-start.30 = (bf16[256,1024]{1,0:T(8,128)(2,1)S(1)}, bf16[256,1024]{1,0:T(8,128)(2,1)S(1)}, u32[]{:S(2)}, u32[]{:S(2)}) collective-permute-start(bf16[256,1024]{1,0:T(8,128)(2,1)S(1)} %collective-permute-done.29.refs_8_), channel_id=1, source_target_pairs={{0,2},{2,0},{4,6},{6,4},{8,10},{10,8},{12,14},{14,12},{16,18},{18,... | collective-permute-start | bytes 1572872 | tf_op jit(solution)/shard_map/ppermute | solution.py:316
  67.2 7.7 %collective-permute-start.35 = (bf16[256,768]{1,0:T(8,128)(2,1)S(1)}, bf16[256,768]{1,0:T(8,128)(2,1)S(1)}, u32[]{:S(2)}, u32[]{:S(2)}) collective-permute-start(bf16[256,768]{1,0:T(8,128)(2,1)S(1)} %collective-permute-done.34.refs_8_), channel_id=1, source_target_pairs={{0,2},{2,0},{4,6},{6,4},{8,10},{10,8},{12,14},{14,12},{16,18},{18,... | collective-permute-start | bytes 1179656 | tf_op jit(solution)/shard_map/ppermute | solution.py:316
  73.4 8.4 %collective-permute-start.15 = (bf16[64,2816]{1,0:T(8,128)(2,1)S(1)}, bf16[64,2816]{1,0:T(8,128)(2,1)S(1)}, u32[]{:S(2)}, u32[]{:S(2)}) collective-permute-start(bf16[64,2816]{1,0:T(8,128)(2,1)S(1)} %collective-permute-done.5.refs_10_), channel_id=1, source_target_pairs={{0,4},{2,6},{4,0},{6,2},{8,12},{10,14},{12,8},{14,10},{16,20},{18,... | collective-permute-start | bytes 1081352 | tf_op jit(solution)/shard_map/ppermute | solution.py:316
  74.9 9.6 %collective-permute-start.6 = (bf16[64,2816]{1,0:T(8,128)(2,1)S(1)}, bf16[64,2816]{1,0:T(8,128)(2,1)S(1)}, u32[]{:S(2)}, u32[]{:S(2)}) collective-permute-start(bf16[64,2816]{1,0:T(8,128)(2,1)S(1)} %collective-permute-done.5.refs_10_), channel_id=1, source_target_pairs={{0,2},{2,0},{4,6},{6,4},{8,10},{10,8},{12,14},{14,12},{16,18},{18,... | collective-permute-start | bytes 1081352 | tf_op jit(solution)/shard_map/ppermute | solution.py:316
  74.9 12.8 %collective-permute-start.11 = (bf16[64,2816]{1,0:T(8,128)(2,1)S(1)}, bf16[64,2816]{1,0:T(8,128)(2,1)S(1)}, u32[]{:S(2)}, u32[]{:S(2)}) collective-permute-start(bf16[64,2816]{1,0:T(8,128)(2,1)S(1)} %collective-permute-done.10.refs_5_.refs_2_), channel_id=1, source_target_pairs={{0,2},{2,0},{4,6},{6,4},{8,10},{10,8},{12,14},{14,12},{16,18},{18,... | collective-permute-start | bytes 1081352 | tf_op jit(solution)/shard_map/ppermute | solution.py:316
  76.1 26.8 %collective-permute-start.13 = (bf16[64,2816]{1,0:T(8,128)(2,1)S(1)}, bf16[64,2816]{1,0:T(8,128)(2,1)S(1)}, u32[]{:S(2)}, u32[]{:S(2)}) collective-permute-start(bf16[64,2816]{1,0:T(8,128)(2,1)S(1)} %collective-permute-done.12.refs_7_.refs_4_), channel_id=1, source_target_pairs={{0,2},{2,0},{4,6},{6,4},{8,10},{10,8},{12,14},{14,12},{16,18},{18,... | collective-permute-start | bytes 1081352 | tf_op jit(solution)/shard_map/ppermute | solution.py:316
  76.2 7.1 %collective-permute-start.36 = (bf16[64,768]{1,0:T(8,128)(2,1)S(1)}, bf16[64,768]{1,0:T(8,128)(2,1)S(1)}, u32[]{:S(2)}, u32[]{:S(2)}) collective-permute-start(bf16[64,768]{1,0:T(8,128)(2,1)S(1)} %get-tuple-element.68), channel_id=1, source_target_pairs={{0,8},{2,10},{4,12},{6,14},{8,0},{10,2},{12,4},{14,6},{16,24},{18,... | collective-permute-start | bytes 294920 | tf_op jit(solution)/shard_map/ppermute | solution.py:316
  81.8 21.2 %collective-permute-start.16 = (bf16[64,2816]{1,0:T(8,128)(2,1)S(1)}, bf16[64,2816]{1,0:T(8,128)(2,1)S(1)}, u32[]{:S(2)}, u32[]{:S(2)}) collective-permute-start(bf16[64,2816]{1,0:T(8,128)(2,1)S(1)} %collective-permute-done.15.refs_4_.refs_6_), channel_id=1, source_target_pairs={{0,2},{2,0},{4,6},{6,4},{8,10},{10,8},{12,14},{14,12},{16,18},{18,... | collective-permute-start | bytes 1081352 | tf_op jit(solution)/shard_map/ppermute | solution.py:316
  83.3 9.2 %collective-permute-start.26 = (bf16[128,1024]{1,0:T(8,128)(2,1)S(1)}, bf16[128,1024]{1,0:T(8,128)(2,1)S(1)}, u32[]{:S(2)}, u32[]{:S(2)}) collective-permute-start(bf16[128,1024]{1,0:T(8,128)(2,1)S(1)} %get-tuple-element.62), channel_id=1, source_target_pairs={{0,8},{2,10},{4,12},{6,14},{8,0},{10,2},{12,4},{14,6},{16,24},{18,... | collective-permute-start | bytes 786440 | tf_op jit(solution)/shard_map/ppermute | solution.py:316
  84.5 15.3 %collective-permute-start.31 = (bf16[128,1024]{1,0:T(8,128)(2,1)S(1)}, bf16[128,1024]{1,0:T(8,128)(2,1)S(1)}, u32[]{:S(2)}, u32[]{:S(2)}) collective-permute-start(bf16[128,1024]{1,0:T(8,128)(2,1)S(1)} %get-tuple-element.65), channel_id=1, source_target_pairs={{0,8},{2,10},{4,12},{6,14},{8,0},{10,2},{12,4},{14,6},{16,24},{18,... | collective-permute-start | bytes 786440 | tf_op jit(solution)/shard_map/ppermute | solution.py:316
  87.7 34.2 %collective-permute-start.7 = (f32[256,256]{1,0:T(8,128)S(1)}, f32[256,256]{1,0:T(8,128)S(1)}, u32[]{:S(2)}, u32[]{:S(2)}) collective-permute-start(f32[256,256]{1,0:T(8,128)S(1)} %get-tuple-element.48), channel_id=1, source_target_pairs={{0,1},{1,0},{2,3},{3,2},{4,5},{5,4},{6,7},{7,6},{8,9},{9,8},{10,11... | collective-permute-start | bytes 786440 | tf_op jit(solution)/shard_map/ppermute | solution.py:341
  92.5 14.5 %collective-permute-start.37 = (bf16[64,768]{1,0:T(8,128)(2,1)S(1)}, bf16[64,768]{1,0:T(8,128)(2,1)S(1)}, u32[]{:S(2)}, u32[]{:S(2)}) collective-permute-start(bf16[64,768]{1,0:T(8,128)(2,1)S(1)} %get-tuple-element.69), channel_id=1, source_target_pairs={{0,16},{2,18},{4,20},{6,22},{8,24},{10,26},{12,28},{14,30},{16,0},... | collective-permute-start | bytes 294920 | tf_op jit(solution)/shard_map/ppermute | solution.py:316
  99.8 7.8 %collective-permute-start.38 = (bf16[64,768]{1,0:T(8,128)(2,1)S(1)}, bf16[64,768]{1,0:T(8,128)(2,1)S(1)}, u32[]{:S(2)}, u32[]{:S(2)}) collective-permute-start(bf16[64,768]{1,0:T(8,128)(2,1)S(1)} %get-tuple-element.70), channel_id=1, source_target_pairs={{0,24},{2,26},{4,28},{6,30},{8,16},{10,18},{12,20},{14,22},{16,8},... | collective-permute-start | bytes 294920 | tf_op jit(solution)/shard_map/ppermute | solution.py:316
  102.9 12.8 %collective-permute-start.27 = (bf16[64,1024]{1,0:T(8,128)(2,1)S(1)}, bf16[64,1024]{1,0:T(8,128)(2,1)S(1)}, u32[]{:S(2)}, u32[]{:S(2)}) collective-permute-start(bf16[64,1024]{1,0:T(8,128)(2,1)S(1)} %shard_map.118), channel_id=1, source_target_pairs={{0,16},{2,18},{4,20},{6,22},{8,24},{10,26},{12,28},{14,30},{16,0},... | collective-permute-start | bytes 393224 | tf_op jit(solution)/shard_map/ppermute | solution.py:316
  103.0 15.1 %collective-permute-start.32 = (bf16[64,1024]{1,0:T(8,128)(2,1)S(1)}, bf16[64,1024]{1,0:T(8,128)(2,1)S(1)}, u32[]{:S(2)}, u32[]{:S(2)}) collective-permute-start(bf16[64,1024]{1,0:T(8,128)(2,1)S(1)} %shard_map.120), channel_id=1, source_target_pairs={{0,16},{2,18},{4,20},{6,22},{8,24},{10,26},{12,28},{14,30},{16,0},... | collective-permute-start | bytes 393224 | tf_op jit(solution)/shard_map/ppermute | solution.py:316
  106.6 2.6 %copy-start.1 = (bf16[2,128,2816]{2,1,0:T(8,128)(2,1)S(1)}, bf16[2,128,2816]{2,1,0:T(8,128)(2,1)}, u32[]{:S(2)}) copy-start(bf16[2,128,2816]{2,1,0:T(8,128)(2,1)} %param.6) | copy-start | bytes 4325380
  107.0 14.9 %collective-permute-start.14 = (f32[128,256]{1,0:T(8,128)S(1)}, f32[128,256]{1,0:T(8,128)S(1)}, u32[]{:S(2)}, u32[]{:S(2)}) collective-permute-start(f32[128,256]{1,0:T(8,128)S(1)} %get-tuple-element.50), channel_id=1, source_target_pairs={{0,1},{1,0},{2,3},{3,2},{4,5},{5,4},{6,7},{7,6},{8,9},{9,8},{10,11... | collective-permute-start | bytes 393224 | tf_op jit(solution)/shard_map/ppermute | solution.py:341
  107.6 10.5 %copy-start.2 = (f32[64,2816]{1,0:T(8,128)S(1)}, f32[64,2816]{1,0:T(8,128)}, u32[]{:S(2)}) copy-start(f32[64,2816]{1,0:T(8,128)} %refs_10_.1) | copy-start | bytes 2162692
  107.6 10.5 %copy-start.3 = (f32[64,2816]{1,0:T(8,128)S(1)}, f32[64,2816]{1,0:T(8,128)}, u32[]{:S(2)}) copy-start(f32[64,2816]{1,0:T(8,128)} %refs_11_.1) | copy-start | bytes 2162692
  107.6 10.5 %copy-start.4 = (f32[64,2816]{1,0:T(8,128)S(1)}, f32[64,2816]{1,0:T(8,128)}, u32[]{:S(2)}) copy-start(f32[64,2816]{1,0:T(8,128)} %refs_12_.1) | copy-start | bytes 2162692
  107.6 14.3 %collective-permute-start.17 = (f32[128,256]{1,0:T(8,128)S(1)}, f32[128,256]{1,0:T(8,128)S(1)}, u32[]{:S(2)}, u32[]{:S(2)}) collective-permute-start(f32[128,256]{1,0:T(8,128)S(1)} %get-tuple-element.53), channel_id=1, source_target_pairs={{0,1},{1,0},{2,3},{3,2},{4,5},{5,4},{6,7},{7,6},{8,9},{9,8},{10,11... | collective-permute-start | bytes 393224 | tf_op jit(solution)/shard_map/ppermute | solution.py:341

commit v5 on v4

--- a/solution.py
+++ b/solution.py
@@ -189,19 +189,21 @@
 
 
 def last_kernel(zs, pieces, me_ref, rep_ref, *refs):
-    turned, (hold, one, two, keep, send) = refs[:pieces], refs[pieces:]
+    turned, (hold, first, one, two, keep, send) = refs[:pieces], refs[pieces:]
     value = out_rows(turned, (one, two))
     flip = flipped(zs, me_ref, rep_ref)
+    span = keep.shape[0]
+    send[:span, :] = first[...].astype(send.dtype)
 
     @pl.when(flip == 0)
     def _():
         keep[...] = hold[...]
-        send[...] = value
+        send[span:, :] = value.astype(send.dtype)
 
     @pl.when(flip == 1)
     def _():
         keep[...] = value
-        send[...] = hold[...]
+        send[span:, :] = hold[...].astype(send.dtype)
 
 
 def store_tile(index, at, sems, pairs):
@@ -242,7 +244,8 @@
 
 
 def merge_kernel(zs, rows, me_ref, *refs):
-    keep, got, middle, got_middle, last, got_last, out, placed = refs
+    keep, got, middle, last, got_far, out, placed = refs
+    span = last.shape[0]
     me = me_ref[0]
 
     def place(value, first, far):
@@ -254,8 +257,8 @@
                 placed[pl.ds(start, rows), :] = value[at : at + rows, :].astype(placed.dtype)
 
     place(keep[...] + got[...], 0, 0)
-    place(middle[...] + got_middle[...], 0, 1)
-    place(last[...] + got_last[...], 1, 1)
+    place(middle[...] + got_far[:span, :].astype(jnp.float32), 0, 1)
+    place(last[...] + got_far[span:, :].astype(jnp.float32), 1, 1)
     out[...] = placed[...].T
 
 
@@ -401,15 +404,14 @@
         smem=2,
         flops=work,
     )
-    got_middle = across_rep(send_middle)
     keep_last, send_last = call(
         functools.partial(last_kernel, zs, pieces),
-        [f32(last, tokens)] * 2,
-        [me_arr, rep_arr, *turned, hold, *far[-2:]],
+        [f32(last, tokens), bf16(2 * last, tokens)],
+        [me_arr, rep_arr, *turned, hold, send_middle, *far[-2:]],
         smem=2,
         flops=work // zs,
     )
-    got_last = across_rep(send_last)
+    got_far = across_rep(send_last)
     slopes = call(slopes_kernel, [f32(tokens, width)] * 2, [gate, up_val])
     gate_grad, up_grad = call(
         functools.partial(back_kernel, zs),
@@ -422,7 +424,7 @@
     (out,) = call(
         functools.partial(merge_kernel, zs, rows),
         [bf16(tokens, 2 * half)],
-        [me_arr, keep, got, middle, got_middle, keep_last, got_last],
+        [me_arr, keep, got, middle, keep_last, got_far],
         [pltpu.VMEM((2 * half, tokens), jnp.bfloat16)],
         smem=1,
     )

time: 123 us -> 128 us (1.041)
  waiting for transfers between devices: 67.8 us -> 77.1 us
  starting transfers between devices: 37.1 us -> 32.5 us
    ppermute x35, waiting for transfers between devices: 67.8 us -> 77.1 us  [swap(): return lax.ppermute(value, 'dp', [(i, i ^ m) for i in range(n)])]
    ppermute x35, starting transfers between devices: 32.3 us -> 29.6 us  [swap(): return lax.ppermute(value, 'dp', [(i, i ^ m) for i in range(n)])]
    ppermute x4 -> x3, starting transfers between devices: 4.82 us -> 2.93 us  [across_rep(): return lax.ppermute(value, 'rep', [(0, 1), (1, 0)])]
  transfers between devices with their start and end apart: 39 -> 38, of which waited for: 11 -> 15; matrix products, arithmetic and copies ran while one was open for 3% -> 3% of each run, Pallas kernels for 9% -> 8%
where the time goes in v5:
time: 128 us
  waiting for transfers between devices  77.1 us (60%)
  starting transfers between devices  32.5 us (25%)
  Pallas kernels  11.6 us (9%)
  other arithmetic  4.24 us (3%)
    ppermute x35, waiting for transfers between devices, swap(): return lax.ppermute(value, 'dp', [(i, i ^ m) for i in range(n)])  77.1 us
    ppermute x35, starting transfers between devices, swap(): return lax.ppermute(value, 'dp', [(i, i ^ m) for i in range(n)])  29.6 us
    pallas_call x14, Pallas kernels, call(): pl.pallas_call(kernel, out_shape=list(outs), in_specs=[SMEM] * smem + [VM...  11.6 us
    convert_element_type x2, other arithmetic, gated(): (gate * jax.nn.sigmoid(gate) * up_val.astype(jnp.float32)).astype(jnp.bfl...  3.09 us
    ppermute x3, starting transfers between devices, across_rep(): return lax.ppermute(value, 'rep', [(0, 1), (1, 0)])  2.93 us
  transfers between devices with their start and end apart: 38, of which 15 were waited for; matrix products, arithmetic and copies ran while one was open for 3% of the time, Pallas kernels for 8%

profile of v5, /device:TPU:0, one launch (start us, length us, event | category | flops | bytes accessed | tf_op | source)
XLA Modules:
  0.0 127.5 jit_solution(16297675283046533758)
XLA Ops:
  0.7 1.1 copy-done.5
  1.8 0.2 shard_map.109
  2.0 3.1 %collective-permute-start.18 = (bf16[256,256]{1,0:T(8,128)(2,1)S(1)}, bf16[256,256]{1,0:T(8,128)(2,1)S(1)}, u32[]{:S(2)}, u32[]{:S(2)}) collective-permute-start(bf16[256,256]{1,0:T(8,128)(2,1)S(1)} %get-tuple-element.60), channel_id=1, source_target_pairs={{0,4},{2,6},{4,0},{6,2},{8,12},{10,14},{12,8},{14,10},{16,20},{18,... | collective-permute-start | bytes 393224 | tf_op jit(solution)/shard_map/ppermute | solution.py:319
  5.1 1.1 convert_element_type.39.refs_4_
  6.3 0.1 collective-permute-start
  6.3 1.6 %collective-permute-start.1 = (bf16[64,2816]{1,0:T(8,128)(2,1)S(1)}, bf16[64,2816]{1,0:T(8,128)(2,1)S(1)}, u32[]{:S(2)}, u32[]{:S(2)}) collective-permute-start(bf16[64,2816]{1,0:T(8,128)(2,1)S(1)} %convert_element_type.39.refs_4_), channel_id=1, source_target_pairs={{0,8},{2,10},{4,12},{6,14},{8,0},{10,2},{12,4},{14,6},{16,24},{18,... | collective-permute-start | bytes 1081352 | tf_op jit(solution)/shard_map/ppermute | solution.py:319
  8.0 0.2 collective-permute-start.17
  8.1 0.5 collective-permute-done.18.refs_2_
  8.6 1.7 %collective-permute-start.19 = (bf16[256,256]{1,0:T(8,128)(2,1)S(1)}, bf16[256,256]{1,0:T(8,128)(2,1)S(1)}, u32[]{:S(2)}, u32[]{:S(2)}) collective-permute-start(bf16[256,256]{1,0:T(8,128)(2,1)S(1)} %collective-permute-done.18.refs_2_), channel_id=1, source_target_pairs={{0,1},{1,0},{2,3},{3,2},{4,5},{5,4},{6,7},{7,6},{8,9},{9,8},{10,11... | collective-permute-start | bytes 393224 | tf_op jit(solution)/shard_map/ppermute | solution.py:344
  10.3 1.3 fusion.14.refs_2_.refs_6_
  11.6 0.0 collective-permute-done.17.refs_1_
  11.6 2.7 %collective-permute-start.3 = (bf16[64,2816]{1,0:T(8,128)(2,1)S(1)}, bf16[64,2816]{1,0:T(8,128)(2,1)S(1)}, u32[]{:S(2)}, u32[]{:S(2)}) collective-permute-start(bf16[64,2816]{1,0:T(8,128)(2,1)S(1)} %convert_element_type.39.refs_4_), channel_id=1, source_target_pairs={{0,16},{2,18},{4,20},{6,22},{8,24},{10,26},{12,28},{14,30},{16,0},... | collective-permute-start | bytes 1081352 | tf_op jit(solution)/shard_map/ppermute | solution.py:319
  14.2 0.0 collective-permute-done.19.refs_3_
  14.2 1.5 %collective-permute-start.8 = (bf16[64,2816]{1,0:T(8,128)(2,1)S(1)}, bf16[64,2816]{1,0:T(8,128)(2,1)S(1)}, u32[]{:S(2)}, u32[]{:S(2)}) collective-permute-start(bf16[64,2816]{1,0:T(8,128)(2,1)S(1)} %convert_element_type.39.refs_4_), channel_id=1, source_target_pairs={{0,4},{2,6},{4,0},{6,2},{8,12},{10,14},{12,8},{14,10},{16,20},{18,... | collective-permute-start | bytes 1081352 | tf_op jit(solution)/shard_map/ppermute | solution.py:319
  15.8 0.0 collective-permute-done.20.refs_4_
  15.8 0.0 collective-permute-start.32
  15.8 0.5 collective-permute-start.21
  16.3 1.8 %fusion.8 = (bf16[256,1024]{1,0:T(8,128)(2,1)S(1)}, bf16[256,1024]{1,0:T(8,128)(2,1)S(1)}) fusion(bf16[256,2816]{1,0:T(8,128)(2,1)S(1)} %bitcast.9, bf16[256,2816]{1,0:T(8,128)(2,1)} %bitcast.12), kind=kLoop, calls=%fused_computation.12 | loop fusion | flops 4194304 | bytes 3145728 | tf_op jit(solution)/shard_map/convert_element_type | solution.py:29
  18.1 2.6 %collective-permute-done.1.refs_6_ = bf16[64,2816]{1,0:T(8,128)(2,1)S(1)} collective-permute-done((bf16[64,2816]{1,0:T(8,128)(2,1)S(1)}, bf16[64,2816]{1,0:T(8,128)(2,1)S(1)}, u32[]{:S(2)}, u32[]{:S(2)}) %collective-permute-start.1) | collective-permute-done | bytes 360480 | tf_op jit(solution)/shard_map/ppermute | solution.py:319
  20.7 10.4 %collective-permute-done.3.refs_8_ = bf16[64,2816]{1,0:T(8,128)(2,1)S(1)} collective-permute-done((bf16[64,2816]{1,0:T(8,128)(2,1)S(1)}, bf16[64,2816]{1,0:T(8,128)(2,1)S(1)}, u32[]{:S(2)}, u32[]{:S(2)}) %collective-permute-start.3) | collective-permute-done | bytes 360480 | tf_op jit(solution)/shard_map/ppermute | solution.py:319
  31.1 1.5 %collective-permute-start.33 = (bf16[256,768]{1,0:T(8,128)(2,1)S(1)}, bf16[256,768]{1,0:T(8,128)(2,1)S(1)}, u32[]{:S(2)}, u32[]{:S(2)}) collective-permute-start(bf16[256,768]{1,0:T(8,128)(2,1)S(1)} %fusion.14.refs_2_.refs_6_), channel_id=1, source_target_pairs={{0,4},{2,6},{4,0},{6,2},{8,12},{10,14},{12,8},{14,10},{16,20},{18,... | collective-permute-start | bytes 1179656 | tf_op jit(solution)/shard_map/ppermute | solution.py:319
  32.7 0.5 collective-permute-start.23
  33.2 1.6 %collective-permute-start.28 = (bf16[256,1024]{1,0:T(8,128)(2,1)S(1)}, bf16[256,1024]{1,0:T(8,128)(2,1)S(1)}, u32[]{:S(2)}, u32[]{:S(2)}) collective-permute-start(bf16[256,1024]{1,0:T(8,128)(2,1)S(1)} %get-tuple-element.74.refs_1_.refs_6_), channel_id=1, source_target_pairs={{0,4},{2,6},{4,0},{6,2},{8,12},{10,14},{12,8},{14,10},{16,20},{18,... | collective-permute-start | bytes 1572872 | tf_op jit(solution)/shard_map/ppermute | solution.py:319
  34.8 8.4 %collective-permute-done.33.refs_8_ = bf16[256,768]{1,0:T(8,128)(2,1)S(1)} collective-permute-done((bf16[256,768]{1,0:T(8,128)(2,1)S(1)}, bf16[256,768]{1,0:T(8,128)(2,1)S(1)}, u32[]{:S(2)}, u32[]{:S(2)}) %collective-permute-start.33) | collective-permute-done | bytes 393248 | tf_op jit(solution)/shard_map/ppermute | solution.py:319
  43.1 0.5 collective-permute-start.4
  43.6 10.7 %collective-permute-done.23.refs_8_ = bf16[256,1024]{1,0:T(8,128)(2,1)S(1)} collective-permute-done((bf16[256,1024]{1,0:T(8,128)(2,1)S(1)}, bf16[256,1024]{1,0:T(8,128)(2,1)S(1)}, u32[]{:S(2)}, u32[]{:S(2)}) %collective-permute-start.23) | collective-permute-done | bytes 524320 | tf_op jit(solution)/shard_map/ppermute | solution.py:319
  54.4 0.7 collective-permute-start.5
  55.1 9.2 %collective-permute-done.28.refs_8_ = bf16[256,1024]{1,0:T(8,128)(2,1)S(1)} collective-permute-done((bf16[256,1024]{1,0:T(8,128)(2,1)S(1)}, bf16[256,1024]{1,0:T(8,128)(2,1)S(1)}, u32[]{:S(2)}, u32[]{:S(2)}) %collective-permute-start.28) | collective-permute-done | bytes 524320 | tf_op jit(solution)/shard_map/ppermute | solution.py:319
  64.3 0.7 collective-permute-start.10
  65.0 0.5 collective-permute-start.24
  65.5 0.1 collective-permute-start.29
  65.6 1.7 %collective-permute-start.12 = (bf16[64,2816]{1,0:T(8,128)(2,1)S(1)}, bf16[64,2816]{1,0:T(8,128)(2,1)S(1)}, u32[]{:S(2)}, u32[]{:S(2)}) collective-permute-start(bf16[64,2816]{1,0:T(8,128)(2,1)S(1)} %collective-permute-done.3.refs_8_), channel_id=1, source_target_pairs={{0,4},{2,6},{4,0},{6,2},{8,12},{10,14},{12,8},{14,10},{16,20},{18,... | collective-permute-start | bytes 1081352 | tf_op jit(solution)/shard_map/ppermute | solution.py:319
  67.3 6.1 %collective-permute-done.10.refs_5_.refs_2_ = bf16[64,2816]{1,0:T(8,128)(2,1)S(1)} collective-permute-done((bf16[64,2816]{1,0:T(8,128)(2,1)S(1)}, bf16[64,2816]{1,0:T(8,128)(2,1)S(1)}, u32[]{:S(2)}, u32[]{:S(2)}) %collective-permute-start.10) | collective-permute-done | bytes 360480 | tf_op jit(solution)/shard_map/ppermute | solution.py:319
  73.4 1.5 %collective-permute-start.14 = (bf16[64,2816]{1,0:T(8,128)(2,1)S(1)}, bf16[64,2816]{1,0:T(8,128)(2,1)S(1)}, u32[]{:S(2)}, u32[]{:S(2)}) collective-permute-start(bf16[64,2816]{1,0:T(8,128)(2,1)S(1)} %collective-permute-done.5.refs_10_), channel_id=1, source_target_pairs={{0,4},{2,6},{4,0},{6,2},{8,12},{10,14},{12,8},{14,10},{16,20},{18,... | collective-permute-start | bytes 1081352 | tf_op jit(solution)/shard_map/ppermute | solution.py:319
  74.9 0.6 shard_map.121
  75.6 1.4 %collective-permute-done.12.refs_7_.refs_4_ = bf16[64,2816]{1,0:T(8,128)(2,1)S(1)} collective-permute-done((bf16[64,2816]{1,0:T(8,128)(2,1)S(1)}, bf16[64,2816]{1,0:T(8,128)(2,1)S(1)}, u32[]{:S(2)}, u32[]{:S(2)}) %collective-permute-start.12) | collective-permute-done | bytes 360480 | tf_op jit(solution)/shard_map/ppermute | solution.py:319
  76.9 1.3 %collective-permute-start.35 = (bf16[64,768]{1,0:T(8,128)(2,1)S(1)}, bf16[64,768]{1,0:T(8,128)(2,1)S(1)}, u32[]{:S(2)}, u32[]{:S(2)}) collective-permute-start(bf16[64,768]{1,0:T(8,128)(2,1)S(1)} %get-tuple-element.68), channel_id=1, source_target_pairs={{0,8},{2,10},{4,12},{6,14},{8,0},{10,2},{12,4},{14,6},{16,24},{18,... | collective-permute-start | bytes 294920 | tf_op jit(solution)/shard_map/ppermute | solution.py:319
  78.2 3.3 %collective-permute-done.35.refs_7_ = bf16[64,768]{1,0:T(8,128)(2,1)S(1)} collective-permute-done((bf16[64,768]{1,0:T(8,128)(2,1)S(1)}, bf16[64,768]{1,0:T(8,128)(2,1)S(1)}, u32[]{:S(2)}, u32[]{:S(2)}) %collective-permute-start.35) | collective-permute-done | bytes 98336 | tf_op jit(solution)/shard_map/ppermute | solution.py:319
  81.5 0.5 collective-permute-start.13
  82.0 2.1 %collective-permute-done.14.refs_5_.refs_6_ = bf16[64,2816]{1,0:T(8,128)(2,1)S(1)} collective-permute-done((bf16[64,2816]{1,0:T(8,128)(2,1)S(1)}, bf16[64,2816]{1,0:T(8,128)(2,1)S(1)}, u32[]{:S(2)}, u32[]{:S(2)}) %collective-permute-start.14) | collective-permute-done | bytes 360480 | tf_op jit(solution)/shard_map/ppermute | solution.py:319
  84.1 0.7 shard_map.117
  84.9 1.3 %collective-permute-start.25 = (bf16[128,1024]{1,0:T(8,128)(2,1)S(1)}, bf16[128,1024]{1,0:T(8,128)(2,1)S(1)}, u32[]{:S(2)}, u32[]{:S(2)}) collective-permute-start(bf16[128,1024]{1,0:T(8,128)(2,1)S(1)} %get-tuple-element.62), channel_id=1, source_target_pairs={{0,8},{2,10},{4,12},{6,14},{8,0},{10,2},{12,4},{14,6},{16,24},{18,... | collective-permute-start | bytes 786440 | tf_op jit(solution)/shard_map/ppermute | solution.py:319
  86.2 0.7 shard_map.119
  87.0 0.8 collective-permute-start.30
  87.8 0.6 shard_map.110
  88.4 1.8 %shard_map.111 = (f32[256,256]{1,0:T(8,128)S(1)}, f32[256,256]{1,0:T(8,128)S(1)}, f32[256,2816]{1,0:T(8,128)S(1)}) custom-call(s32[1]{0:T(128)} %bitcast.me_ref, s32[1]{0:T(128)} %bitcast.1.rep_ref, bf16[1024,256]{1,0:T(8,128)(2,1)S(1)} %get-tuple-element.43.refs_0_, bf16[1024,256]{1,0:T(8,128)(2,1)S(1)} %get-tuple-element.44.refs_1_, ...), custom_call_target="tpu_custom_call" | custom-call | flops 1476395008 | bytes 7995400 | tf_op jit(solution)/shard_map/pallas_call | solution.py:293
  90.1 4.0 %collective-permute-done.25.side.refs_1_ = bf16[128,1024]{1,0:T(8,128)(2,1)S(1)} collective-permute-done((bf16[128,1024]{1,0:T(8,128)(2,1)S(1)}, bf16[128,1024]{1,0:T(8,128)(2,1)S(1)}, u32[]{:S(2)}, u32[]{:S(2)}) %collective-permute-start.25) | collective-permute-done | bytes 262176 | tf_op jit(solution)/shard_map/ppermute | solution.py:319
  94.1 0.6 collective-permute-start.7
  94.7 4.6 %collective-permute-done.30.side.refs_4_ = bf16[128,1024]{1,0:T(8,128)(2,1)S(1)} collective-permute-done((bf16[128,1024]{1,0:T(8,128)(2,1)S(1)}, bf16[128,1024]{1,0:T(8,128)(2,1)S(1)}, u32[]{:S(2)}, u32[]{:S(2)}) %collective-permute-start.30) | collective-permute-done | bytes 262176 | tf_op jit(solution)/shard_map/ppermute | solution.py:319
  99.3 3.4 %collective-permute-start.36 = (bf16[64,768]{1,0:T(8,128)(2,1)S(1)}, bf16[64,768]{1,0:T(8,128)(2,1)S(1)}, u32[]{:S(2)}, u32[]{:S(2)}) collective-permute-start(bf16[64,768]{1,0:T(8,128)(2,1)S(1)} %get-tuple-element.69), channel_id=1, source_target_pairs={{0,16},{2,18},{4,20},{6,22},{8,24},{10,26},{12,28},{14,30},{16,0},... | collective-permute-start | bytes 294920 | tf_op jit(solution)/shard_map/ppermute | solution.py:319
  102.7 0.3 collective-permute-start.37
  103.1 1.5 %collective-permute-start.26 = (bf16[64,1024]{1,0:T(8,128)(2,1)S(1)}, bf16[64,1024]{1,0:T(8,128)(2,1)S(1)}, u32[]{:S(2)}, u32[]{:S(2)}) collective-permute-start(bf16[64,1024]{1,0:T(8,128)(2,1)S(1)} %shard_map.118), channel_id=1, source_target_pairs={{0,16},{2,18},{4,20},{6,22},{8,24},{10,26},{12,28},{14,30},{16,0},... | collective-permute-start | bytes 393224 | tf_op jit(solution)/shard_map/ppermute | solution.py:319
  104.5 1.4 %collective-permute-start.31 = (bf16[64,1024]{1,0:T(8,128)(2,1)S(1)}, bf16[64,1024]{1,0:T(8,128)(2,1)S(1)}, u32[]{:S(2)}, u32[]{:S(2)}) collective-permute-start(bf16[64,1024]{1,0:T(8,128)(2,1)S(1)} %shard_map.120), channel_id=1, source_target_pairs={{0,16},{2,18},{4,20},{6,22},{8,24},{10,26},{12,28},{14,30},{16,0},... | collective-permute-start | bytes 393224 | tf_op jit(solution)/shard_map/ppermute | solution.py:319
  106.0 0.7 shard_map.112
  106.7 0.0 copy-start.1
  106.7 0.4 shard_map.113
  107.1 8.1 %collective-permute-done.36.refs_8_ = bf16[64,768]{1,0:T(8,128)(2,1)S(1)} collective-permute-done((bf16[64,768]{1,0:T(8,128)(2,1)S(1)}, bf16[64,768]{1,0:T(8,128)(2,1)S(1)}, u32[]{:S(2)}, u32[]{:S(2)}) %collective-permute-start.36) | collective-permute-done | bytes 98336 | tf_op jit(solution)/shard_map/ppermute | solution.py:319
  115.2 0.6 collective-permute-start.16
  115.8 1.1 shard_map.115
  117.0 3.1 %collective-permute-done.26.refs_2_ = bf16[64,1024]{1,0:T(8,128)(2,1)S(1)} collective-permute-done((bf16[64,1024]{1,0:T(8,128)(2,1)S(1)}, bf16[64,1024]{1,0:T(8,128)(2,1)S(1)}, u32[]{:S(2)}, u32[]{:S(2)}) %collective-permute-start.26) | collective-permute-done | bytes 131104 | tf_op jit(solution)/shard_map/ppermute | solution.py:319
  120.1 2.7 %collective-permute-done.31.refs_5_ = bf16[64,1024]{1,0:T(8,128)(2,1)S(1)} collective-permute-done((bf16[64,1024]{1,0:T(8,128)(2,1)S(1)}, bf16[64,1024]{1,0:T(8,128)(2,1)S(1)}, u32[]{:S(2)}, u32[]{:S(2)}) %collective-permute-start.31) | collective-permute-done | bytes 131104 | tf_op jit(solution)/shard_map/ppermute | solution.py:319
  122.8 1.7 %shard_map.122 = (f32[64,2816]{1,0:T(8,128)}, f32[64,2816]{1,0:T(8,128)}, f32[64,2816]{1,0:T(8,128)}) custom-call(f32[64,1024]{1,0:T(8,128)S(1)} %get-tuple-element.61.refs_0_, bf16[128,1024]{1,0:T(8,128)(2,1)S(1)} %collective-permute-done.25.side.refs_1_, bf16[64,1024]{1,0:T(8,128)(2,1)S(1)} %collective-permute-done.26.refs_2_, ...), custom_call_target="tpu_custom_call" | custom-call | bytes 6127616 | tf_op jit(solution)/shard_map/pallas_call | solution.py:293
  124.5 2.1 %shard_map.116 = (bf16[256,2816]{1,0:T(8,128)(2,1)}, bf16[256,2816]{1,0:T(8,128)(2,1)}) custom-call(bf16[256,512]{1,0:T(8,128)(2,1)S(1)} %get-tuple-element.54.left, f32[256,2816]{1,0:T(8,128)S(1)} %get-tuple-element.55.gate_slope, f32[256,2816]{1,0:T(8,128)S(1)} %get-tuple-element.56.up_slope, f32[256,2816]{1,0:T(8,128)S(1)} %get-tuple-element.57.early, ...), custom_call_target="tpu_custom_call" | custom-call | flops 738197504 | bytes 14680064 | tf_op jit(solution)/shard_map/pallas_call | solution.py:293
  126.6 0.9 shard_map.114
  (41 shorter events, 0.2 us)
Async XLA Ops:
  0.6 9.7 %copy-start = (bf16[2,128,2816]{2,1,0:T(8,128)(2,1)S(1)}, bf16[2,128,2816]{2,1,0:T(8,128)(2,1)}, u32[]{:S(2)}) copy-start(bf16[2,128,2816]{2,1,0:T(8,128)(2,1)} %param.7) | copy-start | bytes 4325380
  0.6 1.2 copy-start.5
  2.0 6.6 %collective-permute-start.18 = (bf16[256,256]{1,0:T(8,128)(2,1)S(1)}, bf16[256,256]{1,0:T(8,128)(2,1)S(1)}, u32[]{:S(2)}, u32[]{:S(2)}) collective-permute-start(bf16[256,256]{1,0:T(8,128)(2,1)S(1)} %get-tuple-element.60), channel_id=1, source_target_pairs={{0,4},{2,6},{4,0},{6,2},{8,12},{10,14},{12,8},{14,10},{16,20},{18,... | collective-permute-start | bytes 393224 | tf_op jit(solution)/shard_map/ppermute | solution.py:319
  6.3 9.5 %collective-permute-start = (bf16[64,2816]{1,0:T(8,128)(2,1)S(1)}, bf16[64,2816]{1,0:T(8,128)(2,1)S(1)}, u32[]{:S(2)}, u32[]{:S(2)}) collective-permute-start(bf16[64,2816]{1,0:T(8,128)(2,1)S(1)} %convert_element_type.39.refs_4_), channel_id=1, source_target_pairs={{0,2},{2,0},{4,6},{6,4},{8,10},{10,8},{12,14},{14,12},{16,18},{18,... | collective-permute-start | bytes 1081352 | tf_op jit(solution)/shard_map/ppermute | solution.py:319
  6.3 14.4 %collective-permute-start.1 = (bf16[64,2816]{1,0:T(8,128)(2,1)S(1)}, bf16[64,2816]{1,0:T(8,128)(2,1)S(1)}, u32[]{:S(2)}, u32[]{:S(2)}) collective-permute-start(bf16[64,2816]{1,0:T(8,128)(2,1)S(1)} %convert_element_type.39.refs_4_), channel_id=1, source_target_pairs={{0,8},{2,10},{4,12},{6,14},{8,0},{10,2},{12,4},{14,6},{16,24},{18,... | collective-permute-start | bytes 1081352 | tf_op jit(solution)/shard_map/ppermute | solution.py:319
  8.0 3.6 %collective-permute-start.17 = (bf16[256,256]{1,0:T(8,128)(2,1)S(1)}, bf16[256,256]{1,0:T(8,128)(2,1)S(1)}, u32[]{:S(2)}, u32[]{:S(2)}) collective-permute-start(bf16[256,256]{1,0:T(8,128)(2,1)S(1)} %get-tuple-element.41.refs_4_), channel_id=1, source_target_pairs={{0,2},{2,0},{4,6},{6,4},{8,10},{10,8},{12,14},{14,12},{16,18},{18,... | collective-permute-start | bytes 393224 | tf_op jit(solution)/shard_map/ppermute | solution.py:319
  8.6 5.6 %collective-permute-start.19 = (bf16[256,256]{1,0:T(8,128)(2,1)S(1)}, bf16[256,256]{1,0:T(8,128)(2,1)S(1)}, u32[]{:S(2)}, u32[]{:S(2)}) collective-permute-start(bf16[256,256]{1,0:T(8,128)(2,1)S(1)} %collective-permute-done.18.refs_2_), channel_id=1, source_target_pairs={{0,1},{1,0},{2,3},{3,2},{4,5},{5,4},{6,7},{7,6},{8,9},{9,8},{10,11... | collective-permute-start | bytes 393224 | tf_op jit(solution)/shard_map/ppermute | solution.py:344
  10.3 5.5 %collective-permute-start.20 = (bf16[256,256]{1,0:T(8,128)(2,1)S(1)}, bf16[256,256]{1,0:T(8,128)(2,1)S(1)}, u32[]{:S(2)}, u32[]{:S(2)}) collective-permute-start(bf16[256,256]{1,0:T(8,128)(2,1)S(1)} %collective-permute-done.18.refs_2_), channel_id=1, source_target_pairs={{0,2},{2,0},{4,6},{6,4},{8,10},{10,8},{12,14},{14,12},{16,18},{18,... | collective-permute-start | bytes 393224 | tf_op jit(solution)/shard_map/ppermute | solution.py:319
  11.6 19.6 %collective-permute-start.3 = (bf16[64,2816]{1,0:T(8,128)(2,1)S(1)}, bf16[64,2816]{1,0:T(8,128)(2,1)S(1)}, u32[]{:S(2)}, u32[]{:S(2)}) collective-permute-start(bf16[64,2816]{1,0:T(8,128)(2,1)S(1)} %convert_element_type.39.refs_4_), channel_id=1, source_target_pairs={{0,16},{2,18},{4,20},{6,22},{8,24},{10,26},{12,28},{14,30},{16,0},... | collective-permute-start | bytes 1081352 | tf_op jit(solution)/shard_map/ppermute | solution.py:319
  14.2 18.4 %collective-permute-start.8 = (bf16[64,2816]{1,0:T(8,128)(2,1)S(1)}, bf16[64,2816]{1,0:T(8,128)(2,1)S(1)}, u32[]{:S(2)}, u32[]{:S(2)}) collective-permute-start(bf16[64,2816]{1,0:T(8,128)(2,1)S(1)} %convert_element_type.39.refs_4_), channel_id=1, source_target_pairs={{0,4},{2,6},{4,0},{6,2},{8,12},{10,14},{12,8},{14,10},{16,20},{18,... | collective-permute-start | bytes 1081352 | tf_op jit(solution)/shard_map/ppermute | solution.py:319
  15.8 17.4 %collective-permute-start.32 = (bf16[256,768]{1,0:T(8,128)(2,1)S(1)}, bf16[256,768]{1,0:T(8,128)(2,1)S(1)}, u32[]{:S(2)}, u32[]{:S(2)}) collective-permute-start(bf16[256,768]{1,0:T(8,128)(2,1)S(1)} %fusion.14.refs_2_.refs_6_), channel_id=1, source_target_pairs={{0,2},{2,0},{4,6},{6,4},{8,10},{10,8},{12,14},{14,12},{16,18},{18,... | collective-permute-start | bytes 1179656 | tf_op jit(solution)/shard_map/ppermute | solution.py:319
  15.8 17.4 %collective-permute-start.21 = (bf16[256,256]{1,0:T(8,128)(2,1)S(1)}, bf16[256,256]{1,0:T(8,128)(2,1)S(1)}, u32[]{:S(2)}, u32[]{:S(2)}) collective-permute-start(bf16[256,256]{1,0:T(8,128)(2,1)S(1)} %collective-permute-done.19.refs_3_), channel_id=1, source_target_pairs={{0,2},{2,0},{4,6},{6,4},{8,10},{10,8},{12,14},{14,12},{16,18},{18,... | collective-permute-start | bytes 393224 | tf_op jit(solution)/shard_map/ppermute | solution.py:319
  20.7 22.4 %collective-permute-start.22 = (bf16[256,1024]{1,0:T(8,128)(2,1)S(1)}, bf16[256,1024]{1,0:T(8,128)(2,1)S(1)}, u32[]{:S(2)}, u32[]{:S(2)}) collective-permute-start(bf16[256,1024]{1,0:T(8,128)(2,1)S(1)} %get-tuple-element.75.refs_0_.refs_6_), channel_id=1, source_target_pairs={{0,2},{2,0},{4,6},{6,4},{8,10},{10,8},{12,14},{14,12},{16,18},{18,... | collective-permute-start | bytes 1572872 | tf_op jit(solution)/shard_map/ppermute | solution.py:319
  31.1 12.0 %collective-permute-start.33 = (bf16[256,768]{1,0:T(8,128)(2,1)S(1)}, bf16[256,768]{1,0:T(8,128)(2,1)S(1)}, u32[]{:S(2)}, u32[]{:S(2)}) collective-permute-start(bf16[256,768]{1,0:T(8,128)(2,1)S(1)} %fusion.14.refs_2_.refs_6_), channel_id=1, source_target_pairs={{0,4},{2,6},{4,0},{6,2},{8,12},{10,14},{12,8},{14,10},{16,20},{18,... | collective-permute-start | bytes 1179656 | tf_op jit(solution)/shard_map/ppermute | solution.py:319
  32.7 21.7 %collective-permute-start.23 = (bf16[256,1024]{1,0:T(8,128)(2,1)S(1)}, bf16[256,1024]{1,0:T(8,128)(2,1)S(1)}, u32[]{:S(2)}, u32[]{:S(2)}) collective-permute-start(bf16[256,1024]{1,0:T(8,128)(2,1)S(1)} %get-tuple-element.75.refs_0_.refs_6_), channel_id=1, source_target_pairs={{0,4},{2,6},{4,0},{6,2},{8,12},{10,14},{12,8},{14,10},{16,20},{18,... | collective-permute-start | bytes 1572872 | tf_op jit(solution)/shard_map/ppermute | solution.py:319
  33.2 21.9 %collective-permute-start.27 = (bf16[256,1024]{1,0:T(8,128)(2,1)S(1)}, bf16[256,1024]{1,0:T(8,128)(2,1)S(1)}, u32[]{:S(2)}, u32[]{:S(2)}) collective-permute-start(bf16[256,1024]{1,0:T(8,128)(2,1)S(1)} %get-tuple-element.74.refs_1_.refs_6_), channel_id=1, source_target_pairs={{0,2},{2,0},{4,6},{6,4},{8,10},{10,8},{12,14},{14,12},{16,18},{18,... | collective-permute-start | bytes 1572872 | tf_op jit(solution)/shard_map/ppermute | solution.py:319
  33.2 31.1 %collective-permute-start.28 = (bf16[256,1024]{1,0:T(8,128)(2,1)S(1)}, bf16[256,1024]{1,0:T(8,128)(2,1)S(1)}, u32[]{:S(2)}, u32[]{:S(2)}) collective-permute-start(bf16[256,1024]{1,0:T(8,128)(2,1)S(1)} %get-tuple-element.74.refs_1_.refs_6_), channel_id=1, source_target_pairs={{0,4},{2,6},{4,0},{6,2},{8,12},{10,14},{12,8},{14,10},{16,20},{18,... | collective-permute-start | bytes 1572872 | tf_op jit(solution)/shard_map/ppermute | solution.py:319
  43.1 21.9 %collective-permute-start.2 = (bf16[64,2816]{1,0:T(8,128)(2,1)S(1)}, bf16[64,2816]{1,0:T(8,128)(2,1)S(1)}, u32[]{:S(2)}, u32[]{:S(2)}) collective-permute-start(bf16[64,2816]{1,0:T(8,128)(2,1)S(1)} %collective-permute-done.1.refs_6_), channel_id=1, source_target_pairs={{0,2},{2,0},{4,6},{6,4},{8,10},{10,8},{12,14},{14,12},{16,18},{18,... | collective-permute-start | bytes 1081352 | tf_op jit(solution)/shard_map/ppermute | solution.py:319
  43.1 21.9 %collective-permute-start.4 = (bf16[64,2816]{1,0:T(8,128)(2,1)S(1)}, bf16[64,2816]{1,0:T(8,128)(2,1)S(1)}, u32[]{:S(2)}, u32[]{:S(2)}) collective-permute-start(bf16[64,2816]{1,0:T(8,128)(2,1)S(1)} %collective-permute-done.3.refs_8_), channel_id=1, source_target_pairs={{0,2},{2,0},{4,6},{6,4},{8,10},{10,8},{12,14},{14,12},{16,18},{18,... | collective-permute-start | bytes 1081352 | tf_op jit(solution)/shard_map/ppermute | solution.py:319
  54.4 11.2 %collective-permute-start.5 = (bf16[64,2816]{1,0:T(8,128)(2,1)S(1)}, bf16[64,2816]{1,0:T(8,128)(2,1)S(1)}, u32[]{:S(2)}, u32[]{:S(2)}) collective-permute-start(bf16[64,2816]{1,0:T(8,128)(2,1)S(1)} %collective-permute-done.3.refs_8_), channel_id=1, source_target_pairs={{0,8},{2,10},{4,12},{6,14},{8,0},{10,2},{12,4},{14,6},{16,24},{18,... | collective-permute-start | bytes 1081352 | tf_op jit(solution)/shard_map/ppermute | solution.py:319
  55.1 10.5 %collective-permute-start.9 = (bf16[64,2816]{1,0:T(8,128)(2,1)S(1)}, bf16[64,2816]{1,0:T(8,128)(2,1)S(1)}, u32[]{:S(2)}, u32[]{:S(2)}) collective-permute-start(bf16[64,2816]{1,0:T(8,128)(2,1)S(1)} %collective-permute-done.8.refs_3_.refs_0_), channel_id=1, source_target_pairs={{0,2},{2,0},{4,6},{6,4},{8,10},{10,8},{12,14},{14,12},{16,18},{18,... | collective-permute-start | bytes 1081352 | tf_op jit(solution)/shard_map/ppermute | solution.py:319
  64.3 9.1 %collective-permute-start.10 = (bf16[64,2816]{1,0:T(8,128)(2,1)S(1)}, bf16[64,2816]{1,0:T(8,128)(2,1)S(1)}, u32[]{:S(2)}, u32[]{:S(2)}) collective-permute-start(bf16[64,2816]{1,0:T(8,128)(2,1)S(1)} %collective-permute-done.8.refs_3_.refs_0_), channel_id=1, source_target_pairs={{0,8},{2,10},{4,12},{6,14},{8,0},{10,2},{12,4},{14,6},{16,24},{18,... | collective-permute-start | bytes 1081352 | tf_op jit(solution)/shard_map/ppermute | solution.py:319
  65.0 9.9 %collective-permute-start.34 = (bf16[256,768]{1,0:T(8,128)(2,1)S(1)}, bf16[256,768]{1,0:T(8,128)(2,1)S(1)}, u32[]{:S(2)}, u32[]{:S(2)}) collective-permute-start(bf16[256,768]{1,0:T(8,128)(2,1)S(1)} %collective-permute-done.33.refs_8_), channel_id=1, source_target_pairs={{0,2},{2,0},{4,6},{6,4},{8,10},{10,8},{12,14},{14,12},{16,18},{18,... | collective-permute-start | bytes 1179656 | tf_op jit(solution)/shard_map/ppermute | solution.py:319
  65.0 16.5 %collective-permute-start.24 = (bf16[256,1024]{1,0:T(8,128)(2,1)S(1)}, bf16[256,1024]{1,0:T(8,128)(2,1)S(1)}, u32[]{:S(2)}, u32[]{:S(2)}) collective-permute-start(bf16[256,1024]{1,0:T(8,128)(2,1)S(1)} %collective-permute-done.23.refs_8_), channel_id=1, source_target_pairs={{0,2},{2,0},{4,6},{6,4},{8,10},{10,8},{12,14},{14,12},{16,18},{18,... | collective-permute-start | bytes 1572872 | tf_op jit(solution)/shard_map/ppermute | solution.py:319
  65.5 19.3 %collective-permute-start.29 = (bf16[256,1024]{1,0:T(8,128)(2,1)S(1)}, bf16[256,1024]{1,0:T(8,128)(2,1)S(1)}, u32[]{:S(2)}, u32[]{:S(2)}) collective-permute-start(bf16[256,1024]{1,0:T(8,128)(2,1)S(1)} %collective-permute-done.28.refs_8_), channel_id=1, source_target_pairs={{0,2},{2,0},{4,6},{6,4},{8,10},{10,8},{12,14},{14,12},{16,18},{18,... | collective-permute-start | bytes 1572872 | tf_op jit(solution)/shard_map/ppermute | solution.py:319
  65.6 11.3 %collective-permute-start.12 = (bf16[64,2816]{1,0:T(8,128)(2,1)S(1)}, bf16[64,2816]{1,0:T(8,128)(2,1)S(1)}, u32[]{:S(2)}, u32[]{:S(2)}) collective-permute-start(bf16[64,2816]{1,0:T(8,128)(2,1)S(1)} %collective-permute-done.3.refs_8_), channel_id=1, source_target_pairs={{0,4},{2,6},{4,0},{6,2},{8,12},{10,14},{12,8},{14,10},{16,20},{18,... | collective-permute-start | bytes 1081352 | tf_op jit(solution)/shard_map/ppermute | solution.py:319
  73.4 10.7 %collective-permute-start.14 = (bf16[64,2816]{1,0:T(8,128)(2,1)S(1)}, bf16[64,2816]{1,0:T(8,128)(2,1)S(1)}, u32[]{:S(2)}, u32[]{:S(2)}) collective-permute-start(bf16[64,2816]{1,0:T(8,128)(2,1)S(1)} %collective-permute-done.5.refs_10_), channel_id=1, source_target_pairs={{0,4},{2,6},{4,0},{6,2},{8,12},{10,14},{12,8},{14,10},{16,20},{18,... | collective-permute-start | bytes 1081352 | tf_op jit(solution)/shard_map/ppermute | solution.py:319
  74.9 12.1 %collective-permute-start.6 = (bf16[64,2816]{1,0:T(8,128)(2,1)S(1)}, bf16[64,2816]{1,0:T(8,128)(2,1)S(1)}, u32[]{:S(2)}, u32[]{:S(2)}) collective-permute-start(bf16[64,2816]{1,0:T(8,128)(2,1)S(1)} %collective-permute-done.5.refs_10_), channel_id=1, source_target_pairs={{0,2},{2,0},{4,6},{6,4},{8,10},{10,8},{12,14},{14,12},{16,18},{18,... | collective-permute-start | bytes 1081352 | tf_op jit(solution)/shard_map/ppermute | solution.py:319
  76.9 4.6 %collective-permute-start.35 = (bf16[64,768]{1,0:T(8,128)(2,1)S(1)}, bf16[64,768]{1,0:T(8,128)(2,1)S(1)}, u32[]{:S(2)}, u32[]{:S(2)}) collective-permute-start(bf16[64,768]{1,0:T(8,128)(2,1)S(1)} %get-tuple-element.68), channel_id=1, source_target_pairs={{0,8},{2,10},{4,12},{6,14},{8,0},{10,2},{12,4},{14,6},{16,24},{18,... | collective-permute-start | bytes 294920 | tf_op jit(solution)/shard_map/ppermute | solution.py:319
  81.5 21.2 %collective-permute-start.11 = (bf16[64,2816]{1,0:T(8,128)(2,1)S(1)}, bf16[64,2816]{1,0:T(8,128)(2,1)S(1)}, u32[]{:S(2)}, u32[]{:S(2)}) collective-permute-start(bf16[64,2816]{1,0:T(8,128)(2,1)S(1)} %collective-permute-done.10.refs_5_.refs_2_), channel_id=1, source_target_pairs={{0,2},{2,0},{4,6},{6,4},{8,10},{10,8},{12,14},{14,12},{16,18},{18,... | collective-permute-start | bytes 1081352 | tf_op jit(solution)/shard_map/ppermute | solution.py:319
  81.5 21.5 %collective-permute-start.13 = (bf16[64,2816]{1,0:T(8,128)(2,1)S(1)}, bf16[64,2816]{1,0:T(8,128)(2,1)S(1)}, u32[]{:S(2)}, u32[]{:S(2)}) collective-permute-start(bf16[64,2816]{1,0:T(8,128)(2,1)S(1)} %collective-permute-done.12.refs_7_.refs_4_), channel_id=1, source_target_pairs={{0,2},{2,0},{4,6},{6,4},{8,10},{10,8},{12,14},{14,12},{16,18},{18,... | collective-permute-start | bytes 1081352 | tf_op jit(solution)/shard_map/ppermute | solution.py:319
  84.1 20.4 %collective-permute-start.15 = (bf16[64,2816]{1,0:T(8,128)(2,1)S(1)}, bf16[64,2816]{1,0:T(8,128)(2,1)S(1)}, u32[]{:S(2)}, u32[]{:S(2)}) collective-permute-start(bf16[64,2816]{1,0:T(8,128)(2,1)S(1)} %collective-permute-done.14.refs_5_.refs_6_), channel_id=1, source_target_pairs={{0,2},{2,0},{4,6},{6,4},{8,10},{10,8},{12,14},{14,12},{16,18},{18,... | collective-permute-start | bytes 1081352 | tf_op jit(solution)/shard_map/ppermute | solution.py:319
  84.9 9.2 %collective-permute-start.25 = (bf16[128,1024]{1,0:T(8,128)(2,1)S(1)}, bf16[128,1024]{1,0:T(8,128)(2,1)S(1)}, u32[]{:S(2)}, u32[]{:S(2)}) collective-permute-start(bf16[128,1024]{1,0:T(8,128)(2,1)S(1)} %get-tuple-element.62), channel_id=1, source_target_pairs={{0,8},{2,10},{4,12},{6,14},{8,0},{10,2},{12,4},{14,6},{16,24},{18,... | collective-permute-start | bytes 786440 | tf_op jit(solution)/shard_map/ppermute | solution.py:319
  87.0 12.3 %collective-permute-start.30 = (bf16[128,1024]{1,0:T(8,128)(2,1)S(1)}, bf16[128,1024]{1,0:T(8,128)(2,1)S(1)}, u32[]{:S(2)}, u32[]{:S(2)}) collective-permute-start(bf16[128,1024]{1,0:T(8,128)(2,1)S(1)} %get-tuple-element.65), channel_id=1, source_target_pairs={{0,8},{2,10},{4,12},{6,14},{8,0},{10,2},{12,4},{14,6},{16,24},{18,... | collective-permute-start | bytes 786440 | tf_op jit(solution)/shard_map/ppermute | solution.py:319
  94.1 32.5 %collective-permute-start.7 = (f32[256,256]{1,0:T(8,128)S(1)}, f32[256,256]{1,0:T(8,128)S(1)}, u32[]{:S(2)}, u32[]{:S(2)}) collective-permute-start(f32[256,256]{1,0:T(8,128)S(1)} %get-tuple-element.48), channel_id=1, source_target_pairs={{0,1},{1,0},{2,3},{3,2},{4,5},{5,4},{6,7},{7,6},{8,9},{9,8},{10,11... | collective-permute-start | bytes 786440 | tf_op jit(solution)/shard_map/ppermute | solution.py:344
  99.3 15.9 %collective-permute-start.36 = (bf16[64,768]{1,0:T(8,128)(2,1)S(1)}, bf16[64,768]{1,0:T(8,128)(2,1)S(1)}, u32[]{:S(2)}, u32[]{:S(2)}) collective-permute-start(bf16[64,768]{1,0:T(8,128)(2,1)S(1)} %get-tuple-element.69), channel_id=1, source_target_pairs={{0,16},{2,18},{4,20},{6,22},{8,24},{10,26},{12,28},{14,30},{16,0},... | collective-permute-start | bytes 294920 | tf_op jit(solution)/shard_map/ppermute | solution.py:319
  102.7 14.2 %collective-permute-start.37 = (bf16[64,768]{1,0:T(8,128)(2,1)S(1)}, bf16[64,768]{1,0:T(8,128)(2,1)S(1)}, u32[]{:S(2)}, u32[]{:S(2)}) collective-permute-start(bf16[64,768]{1,0:T(8,128)(2,1)S(1)} %get-tuple-element.70), channel_id=1, source_target_pairs={{0,24},{2,26},{4,28},{6,30},{8,16},{10,18},{12,20},{14,22},{16,8},... | collective-permute-start | bytes 294920 | tf_op jit(solution)/shard_map/ppermute | solution.py:319
  103.1 17.0 %collective-permute-start.26 = (bf16[64,1024]{1,0:T(8,128)(2,1)S(1)}, bf16[64,1024]{1,0:T(8,128)(2,1)S(1)}, u32[]{:S(2)}, u32[]{:S(2)}) collective-permute-start(bf16[64,1024]{1,0:T(8,128)(2,1)S(1)} %shard_map.118), channel_id=1, source_target_pairs={{0,16},{2,18},{4,20},{6,22},{8,24},{10,26},{12,28},{14,30},{16,0},... | collective-permute-start | bytes 393224 | tf_op jit(solution)/shard_map/ppermute | solution.py:319
  104.5 18.3 %collective-permute-start.31 = (bf16[64,1024]{1,0:T(8,128)(2,1)S(1)}, bf16[64,1024]{1,0:T(8,128)(2,1)S(1)}, u32[]{:S(2)}, u32[]{:S(2)}) collective-permute-start(bf16[64,1024]{1,0:T(8,128)(2,1)S(1)} %shard_map.120), channel_id=1, source_target_pairs={{0,16},{2,18},{4,20},{6,22},{8,24},{10,26},{12,28},{14,30},{16,0},... | collective-permute-start | bytes 393224 | tf_op jit(solution)/shard_map/ppermute | solution.py:319
  106.7 9.1 %copy-start.1 = (bf16[2,128,2816]{2,1,0:T(8,128)(2,1)S(1)}, bf16[2,128,2816]{2,1,0:T(8,128)(2,1)}, u32[]{:S(2)}) copy-start(bf16[2,128,2816]{2,1,0:T(8,128)(2,1)} %param.6) | copy-start | bytes 4325380
  115.2 7.6 %copy-start.2 = (f32[64,2816]{1,0:T(8,128)S(1)}, f32[64,2816]{1,0:T(8,128)}, u32[]{:S(2)}) copy-start(f32[64,2816]{1,0:T(8,128)} %refs_10_.1) | copy-start | bytes 2162692
  115.2 7.6 %copy-start.3 = (f32[64,2816]{1,0:T(8,128)S(1)}, f32[64,2816]{1,0:T(8,128)}, u32[]{:S(2)}) copy-start(f32[64,2816]{1,0:T(8,128)} %refs_11_.1) | copy-start | bytes 2162692
  115.2 7.6 %copy-start.4 = (f32[64,2816]{1,0:T(8,128)S(1)}, f32[64,2816]{1,0:T(8,128)}, u32[]{:S(2)}) copy-start(f32[64,2816]{1,0:T(8,128)} %refs_12_.1) | copy-start | bytes 2162692
  115.2 11.4 %collective-permute-start.16 = (bf16[256,256]{1,0:T(8,128)(2,1)S(1)}, bf16[256,256]{1,0:T(8,128)(2,1)S(1)}, u32[]{:S(2)}, u32[]{:S(2)}) collective-permute-start(bf16[256,256]{1,0:T(8,128)(2,1)S(1)} %get-tuple-element.53), channel_id=1, source_target_pairs={{0,1},{1,0},{2,3},{3,2},{4,5},{5,4},{6,7},{7,6},{8,9},{9,8},{10,11... | collective-permute-start | bytes 393224 | tf_op jit(solution)/shard_map/ppermute | solution.py:344
